TPU v7x, 32 devices: a whole 2x2x4 slice. The times are simulated.
32 devices in a mesh: dp: 4 (over y, x), row: 2 (over core), col: 4 (over z).
Axes of the slice: x: 2, y: 2, z: 4, core: 2. Of those that a mesh axis runs over, the one named last changes fastest.
Arguments:
- layer_input: bfloat16 [16384, 768], P(('dp', 'col'), 'row'), may hold values from -6 to 6
- lengths: int32 [8, 16], P('dp'), may hold values from 1 to 1024, 2048 in all within a row
- w_qkv: bfloat16 [768, 3, 768], P('col', None, 'row'), may hold values from -0.21875 to 0.21875
- bias_qv: bfloat16 [2, 768], P(None, ('row', 'col')), may hold values from -3 to 3
- w_out: bfloat16 [768, 768], P(('row', 'col')), may hold values from -0.875 to 0.875
- bias_out: bfloat16 [768], P(('row', 'col')), may hold values from -3 to 3
- gain_attn: bfloat16 [768], P(('row', 'col')), may hold values from 0.25 to 1.75
- shift_attn: bfloat16 [768], P(('row', 'col')), may hold values from -3 to 3
- w_in: bfloat16 [768, 3072], P('col', 'row'), may hold values from -0.21875 to 0.21875
- bias_in: bfloat16 [3072], P(('row', 'col')), may hold values from -3 to 3
- w_down: bfloat16 [3072, 768], P(('row', 'col')), may hold values from -0.109375 to 0.109375
- bias_down: bfloat16 [768], P(('row', 'col')), may hold values from -3 to 3
- gain_ffn: bfloat16 [768], P(('row', 'col')), may hold values from 0.25 to 1.75
- shift_ffn: bfloat16 [768], P(('row', 'col')), may hold values from -3 to 3
- cotangent: bfloat16 [16384, 768], P(('dp', 'col'), 'row'), may hold values from -6 to 6
Outputs:
- output: bfloat16 [16384, 768], P(('dp', 'col'), 'row')
- grad_input: float32 [16384, 768], P(('dp', 'col'), 'row')
- grad_w_qkv: float32 [768, 3, 768], P('col', None, 'row')
- grad_bias_qv: float32 [2, 768], P(None, ('row', 'col'))
- grad_w_out: float32 [768, 768], P(('row', 'col'))
- grad_bias_out: float32 [768], P(('row', 'col'))
- grad_gain_attn: float32 [768], P(('row', 'col'))
- grad_shift_attn: float32 [768], P(('row', 'col'))
- grad_w_in: float32 [768, 3072], P('col', 'row')
- grad_bias_in: float32 [3072], P(('row', 'col'))
- grad_w_down: float32 [3072, 768], P(('row', 'col'))
- grad_bias_down: float32 [768], P(('row', 'col'))
- grad_gain_ffn: float32 [768], P(('row', 'col'))
- grad_shift_ffn: float32 [768], P(('row', 'col'))
Inputs may be any that keep to these rules, and one draw needn't show every extreme that they name: Row s gives, in order, the lengths of the 16 documents packed into sequence s; they sum to 2048, and in every row the longest is exactly half of 2048.
All inputs are finite; a program needn't handle non-finite values.
Results may differ from a plain program's by a relative error of at most 0.04.
Values may be sent and summed in bfloat16 or wider, within the bound.
A program may use at most 256 MiB of HBM per device.

v0:
```python
import functools

import jax
import jax.numpy as jnp
from jax import lax
from jax.experimental import pallas as pl
from jax.experimental.pallas import tpu as pltpu
from jax.sharding import PartitionSpec as P


D = 768
HD = 64
LEN = 2048
WIDE = 384
LANES = 128
PAIRS = WIDE // LANES

EPSILON = 1e-12
MASKED = -1e30
HALF_ROOT = 0.7071067811865476
DENSITY = 0.3989422804014327
BF = jnp.bfloat16
F32 = jnp.float32


def matmul(left_mat, right_mat):
    return jnp.dot(left_mat, right_mat, preferred_element_type=F32)


def left_inner(left_mat, right_mat):
    return lax.dot_general(
        left_mat, right_mat, (((0,), (0,)), ((), ())), preferred_element_type=F32
    )


def right_inner(left_mat, right_mat):
    return lax.dot_general(
        left_mat, right_mat, (((1,), (1,)), ((), ())), preferred_element_type=F32
    )


def swap(value):
    return lax.ppermute(value, "row", [(0, 1), (1, 0)])


def ordered(row, mine, other, axis):
    return jnp.where(
        row == 0,
        jnp.concatenate([mine, other], axis=axis),
        jnp.concatenate([other, mine], axis=axis),
    )


def half_of(value, which, axis):
    size = value.shape[axis] // 2
    return lax.dynamic_slice_in_dim(value, which * size, size, axis)


def to_tokens(value, row):
    return half_of(value, row, 0), swap(half_of(value, 1 - row, 0))


def to_features(value, row):
    other = swap(half_of(value, 1 - row, 1))
    return ordered(row, half_of(value, row, 1), other, 0)


def xor_swap(value, axis, mask):
    count = lax.axis_size(axis)
    return lax.ppermute(value, axis, [(i, i ^ mask) for i in range(count)])


def picked(parts, axis):
    stacked = jnp.stack(parts)
    own = lax.axis_index(axis)
    return [
        lax.dynamic_index_in_dim(stacked, own ^ i, 0, keepdims=False) for i in range(len(parts))
    ]


def gathered(value, axis):
    count = lax.axis_size(axis)
    if count > 4:
        return lax.all_gather(value, axis, axis=0)
    parts = [value] + [xor_swap(value, axis, k) for k in range(1, count)]
    return jnp.stack(picked(parts, axis))


def scattered(value, axis, dim):
    count = lax.axis_size(axis)
    if count > 4:
        return lax.psum_scatter(value, axis, scatter_dimension=dim, tiled=False).astype(F32)
    own = lax.axis_index(axis)

    def part(k):
        return lax.dynamic_index_in_dim(value, own ^ k, dim, keepdims=False)

    arrived = [xor_swap(part(k), axis, k) for k in range(1, count)]
    total = part(0).astype(F32)
    for one in arrived:
        total = total + one.astype(F32)
    return total


def two_level(piece, used):
    arrived = [xor_swap(piece, "col", k) for k in range(1, lax.axis_size("col"))]
    ours = jnp.stack([one[:used] for one in arrived])
    return arrived, [ours] + [xor_swap(ours, "dp", j) for j in range(1, 4)]


def reduce_all(quarters):
    own = lax.axis_index("dp")

    def part(k):
        return lax.dynamic_index_in_dim(quarters, own ^ k, 1, keepdims=False)

    arrived = []
    for k in range(1, 4):
        arrived.append(xor_swap(part(k), "dp", k))
    total = part(0).astype(F32)
    for one in arrived:
        total = total + one.astype(F32)
    piece = scattered(total.astype(BF), "col", 0).astype(BF)
    return [piece] + [xor_swap(piece, "dp", k) for k in range(1, 4)]


def places_of():
    return jnp.stack([lax.axis_index("col"), lax.axis_index("dp")]).astype(jnp.int32)


def at_rows(start, count):
    return pl.ds(pl.multiple_of(start, 16), count)


def local_call(kernel, places, inputs, outs):
    spec = pl.BlockSpec(memory_space=pltpu.VMEM)
    return pl.pallas_call(
        kernel,
        out_shape=outs,
        in_specs=[pl.BlockSpec(memory_space=pltpu.SMEM)] + [spec] * len(inputs),
        out_specs=jax.tree.map(lambda _: spec, outs),
        cost_estimate=pl.CostEstimate(flops=0, bytes_accessed=4 << 20, transcendentals=0),
    )(places, *inputs)


def qkv_kernel(places, own, *refs):
    parts, out = refs[:-1], refs[-1]
    col, dp = places[0], places[1]
    share = own.shape[1]
    depth = share // 4
    for kind in range(3):
        for pair in range(PAIRS):
            lanes = slice((3 * pair + kind) * LANES, (3 * pair + kind + 1) * LANES)
            source = slice(pair * LANES, (pair + 1) * LANES)
            out[at_rows(col * share, share), lanes] = own[kind, :, source]
            for j in range(4):
                for k in range(1, 4):
                    rows = at_rows((col ^ k) * share + (dp ^ j) * depth, depth)
                    out[rows, lanes] = parts[j][
                        k - 1, kind * depth : (kind + 1) * depth, source
                    ]


def later_kernel(places, own_down, own_in, own_out, *refs):
    parts, (down, inner, out) = refs[:-3], refs[-3:]
    col, dp = places[0], places[1]
    wide_rows, deep_rows, out_rows = own_down.shape[0], own_in.shape[0], own_out.shape[0]
    down[at_rows(col * wide_rows, wide_rows), :] = own_down[...]
    inner[at_rows(col * deep_rows, deep_rows), :] = own_in[...]
    out[at_rows(col * out_rows, out_rows), :] = own_out[...]
    for j in range(4):
        there = dp ^ j
        for k in range(1, 4):
            part = parts[j].at[k - 1]
            count, at = wide_rows // 4, 0
            rows = at_rows((col ^ k) * wide_rows + there * count, count)
            for i in range(2):
                down[rows, i * WIDE : (i + 1) * WIDE] = part[at : at + count, :]
                at += count
            count = deep_rows // 4
            rows = at_rows((col ^ k) * deep_rows + there * count, count)
            for i in range(4):
                inner[rows, i * WIDE : (i + 1) * WIDE] = part[at : at + count, :]
                at += count
            count = out_rows // 2
            rows = at_rows((col ^ k) * out_rows + lax.rem(there, 2) * count, count)
            lanes = pl.ds(pl.multiple_of(there // 2 * WIDE, LANES), WIDE)
            out[rows, lanes] = part[at : at + count, :]


def early_out_kernel(places, *refs):
    parts, (down, inner, out) = refs[:-3], refs[-3:]
    dp = places[1]
    for j in range(4):
        there = dp ^ j
        count, at = down.shape[0] // 4, 0
        for i in range(2):
            down[at_rows(there * count, count), i * WIDE : (i + 1) * WIDE] = parts[j][
                at : at + count, :
            ].astype(F32)
            at += count
        count = inner.shape[0] // 4
        for i in range(4):
            inner[at_rows(there * count, count), i * WIDE : (i + 1) * WIDE] = parts[j][
                at : at + count, :
            ].astype(F32)
            at += count
        count = out.shape[0] // 2
        lanes = pl.ds(pl.multiple_of(there // 2 * WIDE, LANES), WIDE)
        out[at_rows(lax.rem(there, 2) * count, count), lanes] = parts[j][
            at : at + count, :
        ].astype(F32)


def late_out_kernel(places, *refs):
    parts, out = refs[:-1], refs[-1]
    dp = places[1]
    count = out.shape[1] // 4
    for j in range(4):
        rows = at_rows((dp ^ j) * count, count)
        for pair in range(PAIRS):
            for kind in range(3):
                out[kind, rows, pair * LANES : (pair + 1) * LANES] = parts[j][
                    pair * count : (pair + 1) * count, kind * LANES : (kind + 1) * LANES
                ].astype(F32)


def quartered_rows(value, count):
    pieces = value.shape[1] // WIDE
    cut = value.reshape(count, 4, -1, value.shape[1])
    return jnp.concatenate(
        [cut[..., i * WIDE : (i + 1) * WIDE] for i in range(pieces)], axis=2
    )


def quartered_halves(value, count):
    cut = value.reshape(count, 2, -1, 2 * WIDE)
    return jnp.concatenate([cut[..., :WIDE], cut[..., WIDE:]], axis=1)


def quartered_vector(flat, rows):
    count, size = flat.shape
    return jnp.pad(flat, ((0, 0), (0, 4 * rows * WIDE - size))).reshape(count, 4, rows, WIDE)


def first_quarter(parts, rows):
    stacked = jnp.stack([one[-rows:] for one in parts])
    return lax.dynamic_index_in_dim(
        stacked, lax.axis_index("dp"), 0, keepdims=False
    ).astype(F32).reshape(-1)


def stack_heads(value):
    lane = lax.broadcasted_iota(jnp.int32, value.shape, 1)
    zero = jnp.zeros_like(value)
    return jnp.concatenate(
        [jnp.where(lane < HD, value, zero), jnp.where(lane >= HD, value, zero)], axis=0
    )


def join_heads(value, block):
    lane = lax.broadcasted_iota(jnp.int32, (LANES, block), 0)
    return jnp.where(lane < HD, value[:, :block], value[:, block:]).T


def doubled(value):
    return jnp.concatenate([value, value], axis=1)


def mask_bias(key_place, first_key, past_key):
    places = key_place + lax.broadcasted_iota(jnp.int32, (key_place_rows(), first_key.shape[1]), 0)
    inside = (places >= first_key) & (places < past_key)
    return doubled(jnp.where(inside, 0.0, MASKED))


KEY_BLOCK = 256


def key_place_rows():
    return KEY_BLOCK


def copy_blocks(dest, own, others, rows):
    dest[:rows, :] = own[...]
    dest[rows:, :] = others[...]


def forward_kernel(
    blocks, table, q_ref, k_ref, v_ref, ko_ref, vo_ref, span_ref, out_ref, log_ref, keys, values
):
    rows = q_ref.shape[0]
    block = rows // blocks
    copy_blocks(keys, k_ref, ko_ref, rows)
    copy_blocks(values, v_ref, vo_ref, rows)
    slots = keys.shape[0] // KEY_BLOCK
    base = table[2 * blocks]

    @pl.loop(0, blocks)
    def _(at):
        here = pl.ds(pl.multiple_of(at * block, block), block)
        wide = pl.ds(pl.multiple_of(at * 2 * block, 2 * block), 2 * block)
        query = stack_heads((q_ref[here, :].astype(F32) * 0.125).astype(BF))
        first_key = span_ref[0:1, here]
        past_key = span_ref[1:2, here]

        def step(place, running):
            peak, total, summed = running
            slot = lax.rem(place - base + slots, slots)
            rows_at = pl.ds(pl.multiple_of(slot * KEY_BLOCK, KEY_BLOCK), KEY_BLOCK)
            scores = right_inner(keys[rows_at, :], query)
            scores = scores + mask_bias(place * KEY_BLOCK, first_key, past_key)
            higher = jnp.maximum(peak, jnp.max(scores, axis=0, keepdims=True))
            raised = jnp.exp(scores - higher)
            fade = jnp.exp(peak - higher)
            total = total * fade + jnp.sum(raised, axis=0, keepdims=True)
            summed = summed * fade + left_inner(values[rows_at, :], raised.astype(BF))
            return (higher, total, summed)

        init = (
            jnp.full((1, 2 * block), MASKED, F32),
            jnp.zeros((1, 2 * block), F32),
            jnp.zeros((LANES, 2 * block), F32),
        )
        peak, total, summed = lax.fori_loop(table[at], table[blocks + at], step, init)
        out_ref[here, :] = join_heads(summed / total, block).astype(BF)
        log_ref[:, wide] = jnp.broadcast_to(
            peak + jnp.log(total), (8, 2 * block)
        )


def backward_kernel(
    blocks,
    table,
    q_ref,
    k_ref,
    v_ref,
    ko_ref,
    vo_ref,
    span_ref,
    out_ref,
    log_ref,
    grad_ref,
    dq_ref,
    dk_ref,
    dv_ref,
    others_ref,
    keys,
    values,
    key_sum,
    value_sum,
):
    rows = q_ref.shape[0]
    block = rows // blocks
    copy_blocks(keys, k_ref, ko_ref, rows)
    copy_blocks(values, v_ref, vo_ref, rows)
    slots = keys.shape[0] // KEY_BLOCK
    base = table[2 * blocks]
    key_sum[...] = jnp.zeros_like(key_sum)
    value_sum[...] = jnp.zeros_like(value_sum)

    @pl.loop(0, blocks)
    def _(at):
        here = pl.ds(pl.multiple_of(at * block, block), block)
        wide = pl.ds(pl.multiple_of(at * 2 * block, 2 * block), 2 * block)
        query = stack_heads((q_ref[here, :].astype(F32) * 0.125).astype(BF))
        grad = stack_heads(grad_ref[here, :])
        along = (grad_ref[here, :].astype(F32) * out_ref[here, :].astype(F32)).T
        dots = jnp.concatenate(
            [
                jnp.sum(along[:HD], axis=0, keepdims=True),
                jnp.sum(along[HD:], axis=0, keepdims=True),
            ],
            axis=1,
        )
        logs = log_ref[0:1, wide]
        first_key = span_ref[0:1, here]
        past_key = span_ref[1:2, here]

        def step(place, summed):
            slot = lax.rem(place - base + slots, slots)
            rows_at = pl.ds(pl.multiple_of(slot * KEY_BLOCK, KEY_BLOCK), KEY_BLOCK)
            key = keys[rows_at, :]
            scores = right_inner(key, query)
            scores = scores + mask_bias(place * KEY_BLOCK, first_key, past_key)
            weights = jnp.exp(scores - logs)
            grad_weights = right_inner(values[rows_at, :], grad)
            value_sum[rows_at, :] += matmul(weights.astype(BF), grad)
            grad_scores = (weights * (grad_weights - dots)).astype(BF)
            key_sum[rows_at, :] += matmul(grad_scores, query)
            return summed + left_inner(key, grad_scores)

        summed = lax.fori_loop(
            table[at], table[blocks + at], step, jnp.zeros((LANES, 2 * block), F32)
        )
        dq_ref[here, :] = (join_heads(summed, block) * 0.125).astype(BF)

    dk_ref[...] = key_sum[:rows, :]
    dv_ref[...] = value_sum[:rows, :]
    others_ref[:, :LANES] = key_sum[rows:, :].astype(BF)
    others_ref[:, LANES:] = value_sum[rows:, :].astype(BF)


def attention_specs(rows, others, pair):
    return [
        pl.BlockSpec((rows, LANES), lambda g, t: (0, 3 * pair)),
        pl.BlockSpec((rows, LANES), lambda g, t: (0, 3 * pair + 1)),
        pl.BlockSpec((rows, LANES), lambda g, t: (0, 3 * pair + 2)),
        pl.BlockSpec((others, LANES), lambda g, t: (0, 0)),
        pl.BlockSpec((others, LANES), lambda g, t: (0, 1)),
        pl.BlockSpec((8, rows), lambda g, t: (0, 0)),
    ]


def attend_forward(table, qkv, kv_others, spans, blocks, pair):
    rows, others = qkv.shape[0], kv_others.shape[0]
    return pl.pallas_call(
        functools.partial(forward_kernel, blocks),
        out_shape=(
            jax.ShapeDtypeStruct((rows, LANES), BF),
            jax.ShapeDtypeStruct((8, 2 * rows), F32),
        ),
        grid_spec=pltpu.PrefetchScalarGridSpec(
            num_scalar_prefetch=1,
            grid=(1,),
            in_specs=attention_specs(rows, others, pair),
            out_specs=(
                pl.BlockSpec((rows, LANES), lambda g, t: (0, 0)),
                pl.BlockSpec((8, 2 * rows), lambda g, t: (0, 0)),
            ),
            scratch_shapes=[pltpu.VMEM((rows + others, LANES), BF)] * 2,
        ),
        cost_estimate=pl.CostEstimate(
            flops=8 * rows * LEN * LANES, bytes_accessed=8 * rows * LANES, transcendentals=0
        ),
        name="attend_forward",
    )(table, qkv, qkv, qkv, kv_others, kv_others, spans)


def attend_backward(table, qkv, kv_others, spans, out, logs, grad, blocks, pair):
    rows, others = qkv.shape[0], kv_others.shape[0]
    whole = pl.BlockSpec((rows, LANES), lambda g, t: (0, 0))
    mine = pl.BlockSpec((rows, LANES), lambda g, t: (0, pair))
    return pl.pallas_call(
        functools.partial(backward_kernel, blocks),
        out_shape=(
            jax.ShapeDtypeStruct((rows, LANES), BF),
            jax.ShapeDtypeStruct((rows, LANES), F32),
            jax.ShapeDtypeStruct((rows, LANES), F32),
            jax.ShapeDtypeStruct((others, 2 * LANES), BF),
        ),
        grid_spec=pltpu.PrefetchScalarGridSpec(
            num_scalar_prefetch=1,
            grid=(1,),
            in_specs=attention_specs(rows, others, pair)
            + [whole, pl.BlockSpec((8, 2 * rows), lambda g, t: (0, 0)), mine],
            out_specs=(
                whole,
                whole,
                whole,
                pl.BlockSpec((others, 2 * LANES), lambda g, t: (0, 0)),
            ),
            scratch_shapes=[pltpu.VMEM((rows + others, LANES), BF)] * 2
            + [pltpu.VMEM((rows + others, LANES), F32)] * 2,
        ),
        cost_estimate=pl.CostEstimate(
            flops=20 * rows * LEN * LANES, bytes_accessed=16 * rows * LANES, transcendentals=0
        ),
        name="attend_backward",
    )(table, qkv, qkv, qkv, kv_others, kv_others, spans, out, logs, grad)


def norm_forward(summed, gain_vec, shift_vec):
    center = jnp.mean(summed, axis=1, keepdims=True)
    centered = summed - center
    spread = jnp.mean(centered * centered, axis=1, keepdims=True)
    inv_scale = lax.rsqrt(spread + EPSILON)
    normed_hat = centered * inv_scale
    return (normed_hat * gain_vec + shift_vec, normed_hat, inv_scale)


def norm_backward(grad_vals, normed_hat, inv_scale, gain_vec):
    grad_hat = grad_vals * gain_vec
    return inv_scale * (
        grad_hat
        - jnp.mean(grad_hat, axis=1, keepdims=True)
        - normed_hat * jnp.mean(grad_hat * normed_hat, axis=1, keepdims=True)
    )


def gelu_value(hidden):
    return 0.5 * hidden * (1.0 + lax.erf(hidden * HALF_ROOT))


def gelu_slope(hidden):
    return (
        0.5 * (1.0 + lax.erf(hidden * HALF_ROOT))
        + hidden * jnp.exp(-0.5 * hidden * hidden) * DENSITY
    )


def lanes_to_rows(value):
    pieces = value.shape[2] // WIDE
    return jnp.concatenate(
        [value[:, :, i * WIDE : (i + 1) * WIDE] for i in range(pieces)], axis=1
    )


def rows_to_lanes(value, pieces):
    rows = value.shape[-2] // pieces
    return jnp.concatenate(
        [value[..., i * rows : (i + 1) * rows, :] for i in range(pieces)], axis=-1
    )


def dp_part(value, own, axis=0):
    size = value.shape[axis] // 4
    return lax.dynamic_slice_in_dim(value, own * size, size, axis)


def padded_rows(flat, rows):
    count, size = flat.shape
    return jnp.pad(flat, ((0, 0), (0, rows * WIDE - size))).reshape(count, rows, WIDE)


def body(
    layer_input,
    lengths,
    w_qkv,
    bias_qv,
    w_out,
    bias_out,
    gain_attn,
    shift_attn,
    w_in,
    bias_in,
    w_down,
    bias_down,
    gain_ffn,
    shift_ffn,
    cotangent,
):
    col_grid = lax.axis_size("col")
    rows = layer_input.shape[0]
    row = lax.axis_index("row")
    own_dp = lax.axis_index("dp")
    own_col = lax.axis_index("col")
    group = LEN // rows
    start_row = own_col * rows
    block = min(256, rows)
    blocks = rows // block

    qkv_piece = jnp.swapaxes(dp_part(w_qkv, own_dp), 0, 1)
    depth = qkv_piece.shape[1]
    vectors = jnp.concatenate(
        [
            bias_qv.reshape(-1),
            bias_out,
            gain_attn,
            shift_attn,
            bias_down,
            gain_ffn,
            shift_ffn,
            bias_in,
        ]
    )
    share = bias_out.shape[0]
    vector_rows = 16
    first_piece = jnp.concatenate(
        [qkv_piece.reshape(3 * depth, WIDE), padded_rows(vectors[None], vector_rows)[0]], axis=0
    )
    places = places_of()
    if col_grid > 4:
        first_cols = gathered(first_piece, "col")
        vectors_col = first_cols[:, 3 * depth :]
        qkv_parts = gathered(first_cols[:, : 3 * depth], "dp")
        w_qkv_half = jnp.transpose(
            qkv_parts.reshape(4, col_grid, 3, depth, PAIRS, LANES), (1, 0, 3, 4, 2, 5)
        ).reshape(D, 3 * WIDE)
    else:
        first_arrived, first_parts = two_level(first_piece, 3 * depth)
        vectors_col = jnp.stack(
            picked([one[3 * depth :] for one in [first_piece] + first_arrived], "col")
        )
        w_qkv_half = local_call(
            qkv_kernel,
            places,
            [jnp.swapaxes(w_qkv, 0, 1)] + first_parts,
            jax.ShapeDtypeStruct((D, 3 * WIDE), BF),
        )
    vectors_col = vectors_col.reshape(col_grid, vector_rows * WIDE)[:, : vectors.shape[0]]
    vectors_both = swap(vectors_col)

    def vector(at, count=1):
        mine = vectors_col[:, at * share : (at + count) * share].reshape(-1)
        other = vectors_both[:, at * share : (at + count) * share].reshape(-1)
        return mine.astype(F32), other.astype(F32)

    def whole_vector(at):
        mine, other = vector(at)
        return ordered(row, mine, other, 0)[None]

    bias_q = vectors_col[:, :share].reshape(-1).astype(F32)
    bias_v = vectors_col[:, share : 2 * share].reshape(-1).astype(F32)
    bias_out_f = whole_vector(2)
    gain_attn_f = whole_vector(3)
    shift_attn_f = whole_vector(4)
    bias_down_f = whole_vector(5)
    gain_ffn_f = whole_vector(6)
    shift_ffn_f = whole_vector(7)
    bias_in_mine, bias_in_other = vector(8, 4)

    input_full = ordered(row, layer_input, swap(layer_input), 1)
    input_tokens = half_of(input_full, row, 0).astype(F32)
    cot_mine, cot_other = to_tokens(cotangent, row)
    grad_out = ordered(row, cot_mine, cot_other, 1).astype(F32)

    bias_rows = jnp.stack(
        [
            bias_q.reshape(PAIRS, LANES),
            jnp.zeros((PAIRS, LANES), F32),
            bias_v.reshape(PAIRS, LANES),
        ],
        axis=1,
    ).reshape(-1)
    qkv_low = (matmul(input_full, w_qkv_half) + bias_rows[None]).astype(BF)

    def group_perm(offset, back):
        pairs = []
        for i in range(col_grid):
            source = i // group * group + (i + offset) % group
            pairs.append((i, source) if back else (source, i))
        return pairs

    kv_others = []
    for pair in range(PAIRS):
        kv_local = qkv_low[:, (3 * pair + 1) * LANES : (3 * pair + 3) * LANES]
        kv_others.append(
            jnp.concatenate(
                [lax.ppermute(kv_local, "col", group_perm(j, False)) for j in range(1, group)],
                axis=0,
            )
        )

    down_piece = lanes_to_rows(dp_part(w_down, own_dp)[None])[0]
    in_piece = lanes_to_rows(dp_part(w_in, own_dp)[None])[0]
    if col_grid > 4:
        out_piece = lanes_to_rows(dp_part(w_out, own_dp)[None])[0]
        later_piece = jnp.concatenate([down_piece, in_piece, out_piece], axis=0)
        later_parts = gathered(gathered(later_piece, "col"), "dp")
        cut_down = down_piece.shape[0]
        cut_in = cut_down + in_piece.shape[0]

        def whole_half(parts, pieces):
            joined = jnp.swapaxes(rows_to_lanes(parts, pieces), 0, 1)
            return joined.reshape(-1, joined.shape[-1])

        w_down_mine = whole_half(later_parts[:, :, :cut_down], 2)
        w_in_mine = whole_half(later_parts[:, :, cut_down:cut_in], 4)
        w_out_mine = whole_half(later_parts[:, :, cut_in:], 2)
    else:
        out_half = w_out.shape[0] // 2
        out_piece = lax.dynamic_slice(
            w_out, (own_dp % 2 * out_half, own_dp // 2 * WIDE), (out_half, WIDE)
        )
        later_piece = jnp.concatenate([down_piece, in_piece, out_piece], axis=0)
        _, later_parts = two_level(later_piece, later_piece.shape[0])
        w_down_mine, w_in_mine, w_out_mine = local_call(
            later_kernel,
            places,
            [w_down, w_in, w_out] + later_parts,
            (
                jax.ShapeDtypeStruct((4 * w_down.shape[0], D), BF),
                jax.ShapeDtypeStruct((4 * w_in.shape[0], w_in.shape[1]), BF),
                jax.ShapeDtypeStruct((4 * w_out.shape[0], D), BF),
            ),
        )
    w_out_other, w_in_other, w_down_other = swap(w_out_mine), swap(w_in_mine), swap(w_down_mine)

    own_lengths = lax.dynamic_index_in_dim(lengths, start_row // LEN, 0, keepdims=False)
    ends = jnp.cumsum(own_lengths)
    first_place = start_row % LEN
    spots = first_place + jnp.arange(rows, dtype=jnp.int32)
    past = spots[:, None] >= ends[None, :]
    first_key = jnp.max(jnp.where(past, ends[None, :], 0), axis=1)
    past_key = jnp.min(jnp.where(past, LEN, ends[None, :]), axis=1)
    spans = jnp.pad(jnp.stack([first_key, past_key]), ((0, 6), (0, 0)))
    table = jnp.concatenate(
        [
            first_key[::block] // KEY_BLOCK,
            (past_key[block - 1 :: block] + (KEY_BLOCK - 1)) // KEY_BLOCK,
            (first_place // KEY_BLOCK)[None],
        ]
    ).astype(jnp.int32)

    attended = [
        attend_forward(table, qkv_low, kv_others[pair], spans, blocks, pair)
        for pair in range(PAIRS)
    ]
    att_mine, att_other = to_tokens(jnp.concatenate([out for out, _ in attended], axis=1), row)

    projected = matmul(att_mine, w_out_mine) + matmul(att_other, w_out_other)
    first_sum = input_tokens + projected + bias_out_f
    normed, first_hat, first_scale = norm_forward(first_sum, gain_attn_f, shift_attn_f)
    normed_low = normed.astype(BF)
    hidden_mine = matmul(normed_low, w_in_mine) + bias_in_mine[None]
    hidden_other = matmul(normed_low, w_in_other) + bias_in_other[None]
    act_mine = gelu_value(hidden_mine).astype(BF)
    act_other = gelu_value(hidden_other).astype(BF)
    second_sum = (
        normed
        + matmul(act_mine, w_down_mine)
        + matmul(act_other, w_down_other)
        + bias_down_f
    )
    result, second_hat, second_scale = norm_forward(second_sum, gain_ffn_f, shift_ffn_f)
    result = to_features(result.astype(BF), row)

    grad_gain_ffn = jnp.sum(grad_out * second_hat, axis=0)
    grad_shift_ffn = jnp.sum(grad_out, axis=0)
    grad_second = norm_backward(grad_out, second_hat, second_scale, gain_ffn_f)
    grad_bias_down = jnp.sum(grad_second, axis=0)
    grad_ffn = grad_second.astype(BF)
    grad_hidden_mine = (right_inner(grad_ffn, w_down_mine) * gelu_slope(hidden_mine)).astype(BF)
    grad_hidden_other = (right_inner(grad_ffn, w_down_other) * gelu_slope(hidden_other)).astype(BF)
    grad_normed = (
        grad_second
        + right_inner(grad_hidden_mine, w_in_mine)
        + right_inner(grad_hidden_other, w_in_other)
    )
    grad_gain_attn = jnp.sum(grad_normed * first_hat, axis=0)
    grad_shift_attn = jnp.sum(grad_normed, axis=0)
    grad_first = norm_backward(grad_normed, first_hat, first_scale, gain_attn_f)
    grad_bias_out = jnp.sum(grad_first, axis=0)
    grad_proj = grad_first.astype(BF)
    grad_att_mine = right_inner(grad_proj, w_out_mine).astype(BF)
    grad_att_other = right_inner(grad_proj, w_out_other).astype(BF)
    grad_attended = ordered(row, grad_att_mine, swap(grad_att_other), 0)
    grad_first_features = to_features(grad_first, row)

    def both_tokens(mine, other):
        return (mine + swap(other.astype(BF)).astype(F32)).astype(BF)

    grad_down = both_tokens(left_inner(act_mine, grad_ffn), left_inner(act_other, grad_ffn))
    grad_in = both_tokens(
        left_inner(normed_low, grad_hidden_mine), left_inner(normed_low, grad_hidden_other)
    )
    grad_out_w = both_tokens(left_inner(att_mine, grad_proj), left_inner(att_other, grad_proj))
    by_row = jnp.stack(
        [
            grad_bias_out,
            grad_gain_attn,
            grad_shift_attn,
            grad_bias_down,
            grad_gain_ffn,
            grad_shift_ffn,
        ]
    )
    in_mine = jnp.sum(grad_hidden_mine, axis=0, dtype=F32)
    in_other = jnp.sum(grad_hidden_other, axis=0, dtype=F32)

    def vector_block(six, inner):
        split = jnp.swapaxes(six.reshape(6, col_grid, share), 0, 1).reshape(col_grid, -1)
        return jnp.concatenate([split, inner.reshape(col_grid, -1)], axis=1)

    vec_mine = vector_block(half_of(by_row, row, 1), in_mine)
    vec_other = vector_block(half_of(by_row, 1 - row, 1), in_other)
    vec_sum = (vec_mine + swap(vec_other)).astype(BF)

    vec_pad = 16
    early = jnp.concatenate(
        [
            quartered_rows(grad_down, col_grid),
            quartered_rows(grad_in, col_grid),
            quartered_halves(grad_out_w, col_grid)
            if col_grid <= 4
            else quartered_rows(grad_out_w, col_grid),
            quartered_vector(vec_sum, vec_pad),
        ],
        axis=2,
    )
    early, grad_attended = lax.optimization_barrier((early, grad_attended))
    early_parts = reduce_all(early)

    grad_pairs = []
    for pair in range(PAIRS):
        out, logs = attended[pair]
        grad_query, key_own, value_own, others = attend_backward(
            table, qkv_low, kv_others[pair], spans, out, logs, grad_attended, blocks, pair
        )
        for j in range(1, group):
            arrived = lax.ppermute(
                others[(j - 1) * rows : j * rows], "col", group_perm(j, True)
            ).astype(F32)
            key_own = key_own + arrived[:, :LANES]
            value_own = value_own + arrived[:, LANES:]
        grad_pairs += [grad_query, key_own.astype(BF), value_own.astype(BF)]
    grad_qkv = jnp.concatenate(grad_pairs, axis=1)

    grad_w_qkv = left_inner(input_full, grad_qkv).astype(BF)
    bias_sums = jnp.sum(grad_qkv, axis=0, dtype=F32).reshape(PAIRS, 3, LANES)
    bias_pair = jnp.stack([bias_sums[:, 0].reshape(-1), bias_sums[:, 2].reshape(-1)])
    bias_pair = jnp.swapaxes(bias_pair.reshape(2, col_grid, share), 0, 1).reshape(col_grid, -1)
    late = jnp.concatenate(
        [
            quartered_rows(grad_w_qkv, col_grid),
            quartered_vector(bias_pair.astype(BF), vec_pad),
        ],
        axis=2,
    )
    late_parts = reduce_all(late)

    partial = right_inner(grad_qkv, w_qkv_half)
    arrived = swap(half_of(partial, 1 - row, 1).astype(BF)).astype(F32)
    grad_input = grad_first_features + half_of(partial, row, 1) + arrived

    if col_grid > 4:
        early_all = jnp.stack(picked(early_parts, "dp")).astype(F32)
        late_all = jnp.stack(picked(late_parts, "dp")).astype(F32)
        cut_down = 2 * w_down.shape[0] // 4
        cut_in = cut_down + w_in.shape[0]
        grad_down_own = rows_to_lanes(early_all[:, :cut_down], 2).reshape(w_down.shape)
        grad_in_own = rows_to_lanes(early_all[:, cut_down:cut_in], 4).reshape(w_in.shape)
        grad_out_own = rows_to_lanes(early_all[:, cut_in:-vec_pad], 2).reshape(w_out.shape)
        qkv_own = late_all[:, :-vec_pad].reshape(4, PAIRS, depth, 3, LANES)
        qkv_own = jnp.transpose(qkv_own, (0, 2, 3, 1, 4)).reshape(w_qkv.shape)
    else:
        grad_down_own, grad_in_own, grad_out_own = local_call(
            early_out_kernel,
            places,
            early_parts,
            tuple(jax.ShapeDtypeStruct(one.shape, F32) for one in (w_down, w_in, w_out)),
        )
        qkv_own = local_call(
            late_out_kernel,
            places,
            late_parts,
            jax.ShapeDtypeStruct((3, w_qkv.shape[0], WIDE), F32),
        )
        qkv_own = jnp.swapaxes(qkv_own, 0, 1)
    vec_own = first_quarter(early_parts, vec_pad)
    vecs = [vec_own[i * share : (i + 1) * share] for i in range(6)]
    bias_in_own = vec_own[6 * share : 10 * share]
    bias_own = first_quarter(late_parts, vec_pad)[: 2 * share].reshape(2, share)
    return (
        result,
        grad_input,
        qkv_own,
        bias_own,
        grad_out_own,
        vecs[0],
        vecs[1],
        vecs[2],
        grad_in_own,
        bias_in_own,
        grad_down_own,
        vecs[3],
        vecs[4],
        vecs[5],
    )


def solution(mesh):
    both = P(("row", "col"))
    specs = (
        P("col", None, "row"),
        P(None, ("row", "col")),
        P(("row", "col"), None),
        both,
        both,
        both,
        P("col", "row"),
        both,
        P(("row", "col"), None),
        both,
        both,
        both,
    )
    tokens = P(("dp", "col"), "row")
    return jax.shard_map(
        body,
        mesh=mesh,
        in_specs=(tokens, P("dp", None)) + specs + (tokens,),
        out_specs=(tokens, tokens) + specs,
        check_vma=False,
    )
```

profile of v0, /device:TPU:0, one launch (start us, length us, event | category | flops | bytes accessed | tf_op | source)
XLA Modules:
  0.0 407.5 jit_solution(12090916269184937263)
XLA Ops:
  1.5 4.8 %concatenate.158 = bf16[1152]{0:T(1024)(128)(2,1)S(1)} concatenate(bf16[192]{0:T(256)(128)(2,1)S(1)} %reshape.416, bf16[96]{0:T(256)(128)(2,1)} %param.20, bf16[96]{0:T(256)(128)(2,1)} %param.21, bf16[96]{0:T(256)(128)(2,1)} %param.22, bf16[96]{0:T(256)(128)(2,1)} %param.26, bf16[96]{0:T(256)(128)(2,1)} %param.27, bf16[96]{0:T(256)(128)(2,1)} %param.28, bf16[384]{0:T(512)(128)(2,1)} %param.24), dimensions={0} | concatenate | bytes 4608 | tf_op jit(solution)/shard_map/concatenate | solution.py:554
  7.3 5.1 %collective-permute-start.3 = (bf16[160,384]{1,0:T(8,128)(2,1)S(1)}, bf16[160,384]{1,0:T(8,128)(2,1)S(1)}, u32[]{:S(2)}, u32[]{:S(2)}) collective-permute-start(bf16[160,384]{1,0:T(8,128)(2,1)S(1)} %pad_maximum_fusion.4), channel_id=1, source_target_pairs={{0,3},{1,2},{2,1},{3,0},{4,7},{5,6},{6,5},{7,4},{8,11},{9,10},{10,... | collective-permute-start | bytes 368648 | tf_op jit(solution)/shard_map/ppermute | solution.py:70
  24.0 6.9 %collective-permute-done.2 = bf16[160,384]{1,0:T(8,128)(2,1)S(1)} collective-permute-done((bf16[160,384]{1,0:T(8,128)(2,1)S(1)}, bf16[160,384]{1,0:T(8,128)(2,1)S(1)}, u32[]{:S(2)}, u32[]{:S(2)}) %collective-permute-start.2) | collective-permute-done | bytes 122912 | tf_op jit(solution)/shard_map/ppermute | solution.py:70
  37.3 5.4 %collective-permute-done.6.refs_3_ = bf16[3,144,384]{2,1,0:T(8,128)(2,1)S(1)} collective-permute-done((bf16[3,144,384]{2,1,0:T(8,128)(2,1)S(1)}, bf16[3,144,384]{2,1,0:T(8,128)(2,1)S(1)}, u32[]{:S(2)}, u32[]{:S(2)}) %collective-permute-start.6) | collective-permute-done | bytes 331808 | tf_op jit(solution)/shard_map/ppermute | solution.py:70
  42.7 4.3 %collective-permute-done.5.refs_2_ = bf16[3,144,384]{2,1,0:T(8,128)(2,1)S(1)} collective-permute-done((bf16[3,144,384]{2,1,0:T(8,128)(2,1)S(1)}, bf16[3,144,384]{2,1,0:T(8,128)(2,1)S(1)}, u32[]{:S(2)}, u32[]{:S(2)}) %collective-permute-start.5) | collective-permute-done | bytes 331808 | tf_op jit(solution)/shard_map/ppermute | solution.py:70
  64.5 6.5 %collective-permute-done.7.ko_ref.vo_ref = bf16[1024,256]{1,0:T(8,128)(2,1)} collective-permute-done((bf16[1024,256]{1,0:T(8,128)(2,1)}, bf16[1024,256]{1,0:T(8,128)(2,1)}, u32[]{:S(2)}, u32[]{:S(2)}) %collective-permute-start.7) | collective-permute-done | bytes 524320 | tf_op jit(solution)/shard_map/ppermute | solution.py:639
  72.8 11.6 %attend_forward.3 = (bf16[1024,128]{1,0:T(8,128)(2,1)}, f32[8,2048]{1,0:T(8,128)}) custom-call(s32[9]{0:T(128)} %pad_add_fusion.1.table, bf16[1024,1152]{1,0:T(8,128)(2,1)} %copy-done.2, bf16[1024,1152]{1,0:T(8,128)(2,1)} %copy-done.2, bf16[1024,1152]{1,0:T(8,128)(2,1)} %copy-done.2, bf16[1024,256]{1,0:T(8,128)(2,1)} %collective-permute-done.7.ko_ref.vo_ref, ...), custom_call_target="tpu_custom_call" | custom-call | flops 2147483648 | bytes 1048576 | tf_op jit(solution)/shard_map/attend_forward/pallas_call | solution.py:416
  86.3 11.2 %attend_forward.4 = (bf16[1024,128]{1,0:T(8,128)(2,1)}, f32[8,2048]{1,0:T(8,128)}) custom-call(s32[9]{0:T(128)} %pad_add_fusion.1.table, bf16[1024,1152]{1,0:T(8,128)(2,1)} %copy-done.2, bf16[1024,1152]{1,0:T(8,128)(2,1)} %copy-done.2, bf16[1024,1152]{1,0:T(8,128)(2,1)} %copy-done.2, bf16[1024,256]{1,0:T(8,128)(2,1)} %copy-done.10, ...), custom_call_target="tpu_custom_call" | custom-call | flops 2147483648 | bytes 1048576 | tf_op jit(solution)/shard_map/attend_forward/pallas_call | solution.py:416
  99.3 11.2 %attend_forward.5 = (bf16[1024,128]{1,0:T(8,128)(2,1)}, f32[8,2048]{1,0:T(8,128)}) custom-call(s32[9]{0:T(128)} %pad_add_fusion.1.table, bf16[1024,1152]{1,0:T(8,128)(2,1)} %copy-done.2, bf16[1024,1152]{1,0:T(8,128)(2,1)} %copy-done.2, bf16[1024,1152]{1,0:T(8,128)(2,1)} %copy-done.2, bf16[1024,256]{1,0:T(8,128)(2,1)} %copy-done.11, ...), custom_call_target="tpu_custom_call" | custom-call | flops 2147483648 | bytes 1048576 | tf_op jit(solution)/shard_map/attend_forward/pallas_call | solution.py:416
  110.5 5.3 %shard_map.255 = (bf16[1536,768]{1,0:T(8,128)(2,1)}, bf16[768,1536]{1,0:T(8,128)(2,1)}, bf16[384,768]{1,0:T(8,128)(2,1)}) custom-call(s32[2]{0:T(128)} %pad_add_fusion.2.places, bf16[384,768]{1,0:T(8,128)(2,1)} %own_down.1, bf16[192,1536]{1,0:T(8,128)(2,1)} %own_in.1, bf16[96,768]{1,0:T(8,128)(2,1)} %own_out.1, bf16[3,432,384]{2,1,0:T(8,128)(2,1)} %copy-done.3, ...), custom_call_target="tpu_custom_call" | custom-call | bytes 4194304 | tf_op jit(solution)/shard_map/pallas_call | solution.py:137
  146.4 4.6 %multiply_reduce_fusion = (f32[768]{0:T(1024)S(1)}, f32[512]{0:T(512)S(1)}, f32[512]{0:T(512)S(1)}, f32[768]{0:T(1024)S(1)}, f32[512,768]{1,0:T(8,128)S(1)}) fusion(f32[512,768]{1,0:T(8,128)S(1)} %get-tuple-element.145, f32[512]{0:T(512)S(1)} %add_rsqrt_fusion.1, f32[512]{0:T(512)S(1)} %broadcast_multiply_fusion.5, f32[768]{0:T(1024)S(1)} %get-tuple-element.156, ...), kind=kOutput, calls=%fused_computation.48 | convolution fusion | flops 1212282368 | bytes 10241024 | tf_op jit(solution)/shard_map/dot_general | solution.py:37
  179.6 12.3 %attend_backward.5 = (bf16[1024,128]{1,0:T(8,128)(2,1)}, f32[1024,128]{1,0:T(8,128)}, f32[1024,128]{1,0:T(8,128)}, bf16[1024,256]{1,0:T(8,128)(2,1)}) custom-call(s32[9]{0:T(128)} %pad_add_fusion.1.table, bf16[1024,1152]{1,0:T(8,128)(2,1)} %copy-done.2, bf16[1024,1152]{1,0:T(8,128)(2,1)} %copy-done.2, bf16[1024,1152]{1,0:T(8,128)(2,1)} %copy-done.2, ...), custom_call_target="tpu_custom_call" | custom-call | flops 5368709120 | bytes 2097152 | tf_op jit(solution)/shard_map/attend_backward/pallas_call | solution.py:443
  196.0 12.5 %attend_backward.3 = (bf16[1024,128]{1,0:T(8,128)(2,1)}, f32[1024,128]{1,0:T(8,128)}, f32[1024,128]{1,0:T(8,128)}, bf16[1024,256]{1,0:T(8,128)(2,1)}) custom-call(s32[9]{0:T(128)} %pad_add_fusion.1.table, bf16[1024,1152]{1,0:T(8,128)(2,1)} %copy-done.2, bf16[1024,1152]{1,0:T(8,128)(2,1)} %copy-done.2, bf16[1024,1152]{1,0:T(8,128)(2,1)} %copy-done.2, ...), custom_call_target="tpu_custom_call" | custom-call | flops 5368709120 | bytes 2097152 | tf_op jit(solution)/shard_map/attend_backward/pallas_call | solution.py:443
  209.5 12.3 %attend_backward.4 = (bf16[1024,128]{1,0:T(8,128)(2,1)}, f32[1024,128]{1,0:T(8,128)}, f32[1024,128]{1,0:T(8,128)}, bf16[1024,256]{1,0:T(8,128)(2,1)}) custom-call(s32[9]{0:T(128)} %pad_add_fusion.1.table, bf16[1024,1152]{1,0:T(8,128)(2,1)} %copy-done.2, bf16[1024,1152]{1,0:T(8,128)(2,1)} %copy-done.2, bf16[1024,1152]{1,0:T(8,128)(2,1)} %copy-done.2, ...), custom_call_target="tpu_custom_call" | custom-call | flops 5368709120 | bytes 2097152 | tf_op jit(solution)/shard_map/attend_backward/pallas_call | solution.py:443
  228.0 8.0 %collective-permute-done.30 = bf16[1024,256]{1,0:T(8,128)(2,1)S(1)} collective-permute-done((bf16[1024,256]{1,0:T(8,128)(2,1)}, bf16[1024,256]{1,0:T(8,128)(2,1)S(1)}, u32[]{:S(2)}, u32[]{:S(2)}) %collective-permute-start.30) | collective-permute-done | bytes 524320 | tf_op jit(solution)/shard_map/ppermute | solution.py:791
  242.3 5.1 %convolution_convert_fusion = bf16[768,1152]{1,0:T(8,128)(2,1)} fusion(bf16[1024,768]{1,0:T(8,128)(2,1)S(1)} %copy-done.7, bf16[1024,1152]{1,0:T(8,128)(2,1)} %fusion.43), kind=kOutput, calls=%fused_computation.5 | convolution fusion | flops 1812824064 | bytes 5701632 | tf_op jit(solution)/shard_map/dot_general | solution.py:31
  250.0 8.6 %collective-permute-start.33 = (bf16[4,160,384]{2,1,0:T(8,128)(2,1)S(1)}, bf16[4,160,384]{2,1,0:T(8,128)(2,1)S(1)}, u32[]{:S(2)}, u32[]{:S(2)}) collective-permute-start(bf16[4,160,384]{2,1,0:T(8,128)(2,1)S(1)} %get-tuple-element.90), channel_id=1, source_target_pairs={{0,8},{8,0},{16,24},{24,16},{1,9},{9,1},{17,25},{25,17},{2,10},{10... | collective-permute-start | bytes 1474568 | tf_op jit(solution)/shard_map/ppermute | solution.py:70
  266.5 4.2 %collective-permute-done.33 = bf16[4,160,384]{2,1,0:T(8,128)(2,1)S(1)} collective-permute-done((bf16[4,160,384]{2,1,0:T(8,128)(2,1)S(1)}, bf16[4,160,384]{2,1,0:T(8,128)(2,1)S(1)}, u32[]{:S(2)}, u32[]{:S(2)}) %collective-permute-start.33) | collective-permute-done | bytes 491552 | tf_op jit(solution)/shard_map/ppermute | solution.py:70
  271.5 11.1 %collective-permute-done.34 = bf16[4,160,384]{2,1,0:T(8,128)(2,1)S(1)} collective-permute-done((bf16[4,160,384]{2,1,0:T(8,128)(2,1)S(1)}, bf16[4,160,384]{2,1,0:T(8,128)(2,1)S(1)}, u32[]{:S(2)}, u32[]{:S(2)}) %collective-permute-start.34) | collective-permute-done | bytes 491552 | tf_op jit(solution)/shard_map/ppermute | solution.py:70
  300.2 41.8 %collective-permute-done.41.refs_3_ = bf16[160,384]{1,0:T(8,128)(2,1)S(1)} collective-permute-done((bf16[160,384]{1,0:T(8,128)(2,1)S(1)}, bf16[160,384]{1,0:T(8,128)(2,1)S(1)}, u32[]{:S(2)}, u32[]{:S(2)}) %collective-permute-start.41) | collective-permute-done | bytes 122912 | tf_op jit(solution)/shard_map/ppermute | solution.py:70
  356.7 11.6 %collective-permute-done.45 = bf16[448,384]{1,0:T(8,128)(2,1)} collective-permute-done((bf16[448,384]{1,0:T(8,128)(2,1)}, bf16[448,384]{1,0:T(8,128)(2,1)}, u32[]{:S(2)}, u32[]{:S(2)}) %collective-permute-start.45) | collective-permute-done | bytes 344096 | tf_op jit(solution)/shard_map/ppermute | solution.py:70
  368.2 15.9 %collective-permute-done.46 = bf16[448,384]{1,0:T(8,128)(2,1)} collective-permute-done((bf16[448,384]{1,0:T(8,128)(2,1)}, bf16[448,384]{1,0:T(8,128)(2,1)}, u32[]{:S(2)}, u32[]{:S(2)}) %collective-permute-start.46) | collective-permute-done | bytes 344096 | tf_op jit(solution)/shard_map/ppermute | solution.py:70
  392.8 4.7 %collective-permute-done.50.refs_3_ = bf16[448,384]{1,0:T(8,128)(2,1)S(1)} collective-permute-done((bf16[448,384]{1,0:T(8,128)(2,1)S(1)}, bf16[448,384]{1,0:T(8,128)(2,1)S(1)}, u32[]{:S(2)}, u32[]{:S(2)}) %collective-permute-start.50) | collective-permute-done | bytes 344096 | tf_op jit(solution)/shard_map/ppermute | solution.py:70
  397.5 5.4 %collective-permute-done.49.refs_2_ = bf16[448,384]{1,0:T(8,128)(2,1)S(1)} collective-permute-done((bf16[448,384]{1,0:T(8,128)(2,1)S(1)}, bf16[448,384]{1,0:T(8,128)(2,1)S(1)}, u32[]{:S(2)}, u32[]{:S(2)}) %collective-permute-start.49) | collective-permute-done | bytes 344096 | tf_op jit(solution)/shard_map/ppermute | solution.py:70
  (419 shorter events, 174.9 us)
Async XLA Ops:
  12.5 18.4 %collective-permute-start.2 = (bf16[160,384]{1,0:T(8,128)(2,1)S(1)}, bf16[160,384]{1,0:T(8,128)(2,1)S(1)}, u32[]{:S(2)}, u32[]{:S(2)}) collective-permute-start(bf16[160,384]{1,0:T(8,128)(2,1)S(1)} %pad_maximum_fusion.4), channel_id=1, source_target_pairs={{0,2},{1,3},{2,0},{3,1},{4,6},{5,7},{6,4},{7,5},{8,10},{9,11},{10,... | collective-permute-start | bytes 368648 | tf_op jit(solution)/shard_map/ppermute | solution.py:70
  12.5 18.4 %collective-permute-start.1 = (bf16[160,384]{1,0:T(8,128)(2,1)S(1)}, bf16[160,384]{1,0:T(8,128)(2,1)S(1)}, u32[]{:S(2)}, u32[]{:S(2)}) collective-permute-start(bf16[160,384]{1,0:T(8,128)(2,1)S(1)} %pad_maximum_fusion.4), channel_id=1, source_target_pairs={{0,1},{1,0},{2,3},{3,2},{4,5},{5,4},{6,7},{7,6},{8,9},{9,8},{10,11... | collective-permute-start | bytes 368648 | tf_op jit(solution)/shard_map/ppermute | solution.py:70
  16.6 41.7 %collective-permute-start.12 = (bf16[432,384]{1,0:T(8,128)(2,1)}, bf16[432,384]{1,0:T(8,128)(2,1)}, u32[]{:S(2)}, u32[]{:S(2)}) collective-permute-start(bf16[432,384]{1,0:T(8,128)(2,1)} %pad_maximum_fusion.3), channel_id=1, source_target_pairs={{0,3},{1,2},{2,1},{3,0},{4,7},{5,6},{6,5},{7,4},{8,11},{9,10},{10,... | collective-permute-start | bytes 995336 | tf_op jit(solution)/shard_map/ppermute | solution.py:70
  20.4 30.4 %collective-permute-start = (bf16[1024,384]{1,0:T(8,128)(2,1)S(1)}, bf16[1024,384]{1,0:T(8,128)(2,1)S(1)}, u32[]{:S(2)}, u32[]{:S(2)}) collective-permute-start(bf16[1024,384]{1,0:T(8,128)(2,1)S(1)} %copy-done.26), channel_id=1, source_target_pairs={{0,4},{4,0},{1,5},{5,1},{2,6},{6,2},{3,7},{7,3},{8,12},{12,8},{9,1... | collective-permute-start | bytes 2359304 | tf_op jit(solution)/shard_map/ppermute | solution.py:43
  60.3 50.2 %collective-permute-start.15 = (bf16[3,432,384]{2,1,0:T(8,128)(2,1)S(1)}, bf16[3,432,384]{2,1,0:T(8,128)(2,1)}, u32[]{:S(2)}, u32[]{:S(2)}) collective-permute-start(bf16[3,432,384]{2,1,0:T(8,128)(2,1)S(1)} %pad_maximum_fusion.1.refs_0_), channel_id=1, source_target_pairs={{0,24},{8,16},{16,8},{24,0},{1,25},{9,17},{17,9},{25,1},{2,26},{10... | collective-permute-start | bytes 2985992 | tf_op jit(solution)/shard_map/ppermute | solution.py:70
  62.9 47.6 %collective-permute-start.14 = (bf16[3,432,384]{2,1,0:T(8,128)(2,1)S(1)}, bf16[3,432,384]{2,1,0:T(8,128)(2,1)}, u32[]{:S(2)}, u32[]{:S(2)}) collective-permute-start(bf16[3,432,384]{2,1,0:T(8,128)(2,1)S(1)} %pad_maximum_fusion.1.refs_0_), channel_id=1, source_target_pairs={{0,16},{8,24},{16,0},{24,8},{1,17},{9,25},{17,1},{25,9},{2,18},{10... | collective-permute-start | bytes 2985992 | tf_op jit(solution)/shard_map/ppermute | solution.py:70
  63.4 47.1 %collective-permute-start.13 = (bf16[3,432,384]{2,1,0:T(8,128)(2,1)S(1)}, bf16[3,432,384]{2,1,0:T(8,128)(2,1)}, u32[]{:S(2)}, u32[]{:S(2)}) collective-permute-start(bf16[3,432,384]{2,1,0:T(8,128)(2,1)S(1)} %pad_maximum_fusion.1.refs_0_), channel_id=1, source_target_pairs={{0,8},{8,0},{16,24},{24,16},{1,9},{9,1},{17,25},{25,17},{2,10},{10... | collective-permute-start | bytes 2985992 | tf_op jit(solution)/shard_map/ppermute | solution.py:70
  63.9 21.6 %collective-permute-start.8 = (bf16[1024,256]{1,0:T(8,128)(2,1)}, bf16[1024,256]{1,0:T(8,128)(2,1)S(1)}, u32[]{:S(2)}, u32[]{:S(2)}) collective-permute-start(bf16[1024,256]{1,0:T(8,128)(2,1)} %get-tuple-element.88), channel_id=1, source_target_pairs={{1,0},{0,1},{3,2},{2,3},{5,4},{4,5},{7,6},{6,7},{9,8},{8,9},{11,10... | collective-permute-start | bytes 1572872 | tf_op jit(solution)/shard_map/ppermute | solution.py:639
  70.9 27.6 %collective-permute-start.9 = (bf16[1024,256]{1,0:T(8,128)(2,1)}, bf16[1024,256]{1,0:T(8,128)(2,1)S(1)}, u32[]{:S(2)}, u32[]{:S(2)}) collective-permute-start(bf16[1024,256]{1,0:T(8,128)(2,1)} %get-tuple-element.87), channel_id=1, source_target_pairs={{1,0},{0,1},{3,2},{2,3},{5,4},{4,5},{7,6},{6,7},{9,8},{8,9},{11,10... | collective-permute-start | bytes 1572872 | tf_op jit(solution)/shard_map/ppermute | solution.py:639
  85.5 46.0 %collective-permute-start.22 = (bf16[512,384]{1,0:T(8,128)(2,1)}, bf16[512,384]{1,0:T(8,128)(2,1)S(1)}, u32[]{:S(2)}, u32[]{:S(2)}) collective-permute-start(bf16[512,384]{1,0:T(8,128)(2,1)} %get-tuple-element.103), channel_id=1, source_target_pairs={{0,4},{4,0},{1,5},{5,1},{2,6},{6,2},{3,7},{7,3},{8,12},{12,8},{9,1... | collective-permute-start | bytes 1179656 | tf_op jit(solution)/shard_map/ppermute | solution.py:43
  163.6 97.8 %collective-permute-start.21 = (bf16[512,384]{1,0:T(8,128)(2,1)}, bf16[512,384]{1,0:T(8,128)(2,1)}, u32[]{:S(2)}, u32[]{:S(2)}) collective-permute-start(bf16[512,384]{1,0:T(8,128)(2,1)} %get-tuple-element.106), channel_id=1, source_target_pairs={{0,4},{4,0},{1,5},{5,1},{2,6},{6,2},{3,7},{7,3},{8,12},{12,8},{9,1... | collective-permute-start | bytes 1179656 | tf_op jit(solution)/shard_map/ppermute | solution.py:43
  192.0 46.5 %collective-permute-start.31 = (bf16[1024,256]{1,0:T(8,128)(2,1)}, bf16[1024,256]{1,0:T(8,128)(2,1)S(1)}, u32[]{:S(2)}, u32[]{:S(2)}) collective-permute-start(bf16[1024,256]{1,0:T(8,128)(2,1)} %get-tuple-element.60), channel_id=1, source_target_pairs={{0,1},{1,0},{2,3},{3,2},{4,5},{5,4},{6,7},{7,6},{8,9},{9,8},{10,11... | collective-permute-start | bytes 1572872 | tf_op jit(solution)/shard_map/ppermute | solution.py:791
  250.0 20.7 %collective-permute-start.33 = (bf16[4,160,384]{2,1,0:T(8,128)(2,1)S(1)}, bf16[4,160,384]{2,1,0:T(8,128)(2,1)S(1)}, u32[]{:S(2)}, u32[]{:S(2)}) collective-permute-start(bf16[4,160,384]{2,1,0:T(8,128)(2,1)S(1)} %get-tuple-element.90), channel_id=1, source_target_pairs={{0,8},{8,0},{16,24},{24,16},{1,9},{9,1},{17,25},{25,17},{2,10},{10... | collective-permute-start | bytes 1474568 | tf_op jit(solution)/shard_map/ppermute | solution.py:70
  258.6 24.0 %collective-permute-start.34 = (bf16[4,160,384]{2,1,0:T(8,128)(2,1)S(1)}, bf16[4,160,384]{2,1,0:T(8,128)(2,1)S(1)}, u32[]{:S(2)}, u32[]{:S(2)}) collective-permute-start(bf16[4,160,384]{2,1,0:T(8,128)(2,1)S(1)} %get-tuple-element.91), channel_id=1, source_target_pairs={{0,16},{8,24},{16,0},{24,8},{1,17},{9,25},{17,1},{25,9},{2,18},{10... | collective-permute-start | bytes 1474568 | tf_op jit(solution)/shard_map/ppermute | solution.py:70
  259.4 23.2 %collective-permute-start.35 = (bf16[4,160,384]{2,1,0:T(8,128)(2,1)S(1)}, bf16[4,160,384]{2,1,0:T(8,128)(2,1)S(1)}, u32[]{:S(2)}, u32[]{:S(2)}) collective-permute-start(bf16[4,160,384]{2,1,0:T(8,128)(2,1)S(1)} %get-tuple-element.92), channel_id=1, source_target_pairs={{0,24},{8,16},{16,8},{24,0},{1,25},{9,17},{17,9},{25,1},{2,26},{10... | collective-permute-start | bytes 1474568 | tf_op jit(solution)/shard_map/ppermute | solution.py:70
  264.1 82.8 %collective-permute-start.42 = (bf16[4,448,384]{2,1,0:T(8,128)(2,1)S(1)}, bf16[4,448,384]{2,1,0:T(8,128)(2,1)S(1)}, u32[]{:S(2)}, u32[]{:S(2)}) collective-permute-start(bf16[4,448,384]{2,1,0:T(8,128)(2,1)S(1)} %get-tuple-element.84), channel_id=1, source_target_pairs={{0,8},{8,0},{16,24},{24,16},{1,9},{9,1},{17,25},{25,17},{2,10},{10... | collective-permute-start | bytes 4128776 | tf_op jit(solution)/shard_map/ppermute | solution.py:70
  266.1 82.5 %collective-permute-start.44 = (bf16[4,448,384]{2,1,0:T(8,128)(2,1)S(1)}, bf16[4,448,384]{2,1,0:T(8,128)(2,1)S(1)}, u32[]{:S(2)}, u32[]{:S(2)}) collective-permute-start(bf16[4,448,384]{2,1,0:T(8,128)(2,1)S(1)} %get-tuple-element.85), channel_id=1, source_target_pairs={{0,24},{8,16},{16,8},{24,0},{1,25},{9,17},{17,9},{25,1},{2,26},{10... | collective-permute-start | bytes 4128776 | tf_op jit(solution)/shard_map/ppermute | solution.py:70
  270.7 78.0 %collective-permute-start.43 = (bf16[4,448,384]{2,1,0:T(8,128)(2,1)S(1)}, bf16[4,448,384]{2,1,0:T(8,128)(2,1)S(1)}, u32[]{:S(2)}, u32[]{:S(2)}) collective-permute-start(bf16[4,448,384]{2,1,0:T(8,128)(2,1)S(1)} %get-tuple-element.86), channel_id=1, source_target_pairs={{0,16},{8,24},{16,0},{24,8},{1,17},{9,25},{17,1},{25,9},{2,18},{10... | collective-permute-start | bytes 4128776 | tf_op jit(solution)/shard_map/ppermute | solution.py:70
  294.3 92.3 %collective-permute-start.23 = (f32[512,384]{1,0:T(8,128)}, f32[512,384]{1,0:T(8,128)}, u32[]{:S(2)}, u32[]{:S(2)}) collective-permute-start(f32[512,384]{1,0:T(8,128)} %get-tuple-element.98), channel_id=1, source_target_pairs={{0,4},{4,0},{1,5},{5,1},{2,6},{6,2},{3,7},{7,3},{8,12},{12,8},{9,1... | collective-permute-start | bytes 2359304 | tf_op jit(solution)/shard_map/ppermute | solution.py:43
  298.1 44.0 %collective-permute-start.41 = (bf16[160,384]{1,0:T(8,128)(2,1)S(1)}, bf16[160,384]{1,0:T(8,128)(2,1)S(1)}, u32[]{:S(2)}, u32[]{:S(2)}) collective-permute-start(bf16[160,384]{1,0:T(8,128)(2,1)S(1)} %fusion.46.refs_0_), channel_id=1, source_target_pairs={{0,24},{8,16},{16,8},{24,0},{1,25},{9,17},{17,9},{25,1},{2,26},{10... | collective-permute-start | bytes 368648 | tf_op jit(solution)/shard_map/ppermute | solution.py:70
  346.9 39.7 %collective-permute-start.32 = (bf16[1024,384]{1,0:T(8,128)(2,1)S(1)}, bf16[1024,384]{1,0:T(8,128)(2,1)}, u32[]{:S(2)}, u32[]{:S(2)}) collective-permute-start(bf16[1024,384]{1,0:T(8,128)(2,1)S(1)} %dynamic-slice_convert_fusion), channel_id=1, source_target_pairs={{0,4},{4,0},{1,5},{5,1},{2,6},{6,2},{3,7},{7,3},{8,12},{12,8},{9,1... | collective-permute-start | bytes 2359304 | tf_op jit(solution)/shard_map/ppermute | solution.py:43
  350.4 17.8 %collective-permute-start.45 = (bf16[448,384]{1,0:T(8,128)(2,1)}, bf16[448,384]{1,0:T(8,128)(2,1)}, u32[]{:S(2)}, u32[]{:S(2)}) collective-permute-start(bf16[448,384]{1,0:T(8,128)(2,1)} %get-tuple-element.99), channel_id=1, source_target_pairs={{0,1},{1,0},{2,3},{3,2},{4,5},{5,4},{6,7},{7,6},{8,9},{9,8},{10,11... | collective-permute-start | bytes 1032200 | tf_op jit(solution)/shard_map/ppermute | solution.py:70
  351.0 17.3 %collective-permute-start.47 = (bf16[448,384]{1,0:T(8,128)(2,1)}, bf16[448,384]{1,0:T(8,128)(2,1)}, u32[]{:S(2)}, u32[]{:S(2)}) collective-permute-start(bf16[448,384]{1,0:T(8,128)(2,1)} %get-tuple-element.100), channel_id=1, source_target_pairs={{0,3},{1,2},{2,1},{3,0},{4,7},{5,6},{6,5},{7,4},{8,11},{9,10},{10,... | collective-permute-start | bytes 1032200 | tf_op jit(solution)/shard_map/ppermute | solution.py:70
  352.7 31.5 %collective-permute-start.46 = (bf16[448,384]{1,0:T(8,128)(2,1)}, bf16[448,384]{1,0:T(8,128)(2,1)}, u32[]{:S(2)}, u32[]{:S(2)}) collective-permute-start(bf16[448,384]{1,0:T(8,128)(2,1)} %get-tuple-element.101), channel_id=1, source_target_pairs={{0,2},{1,3},{2,0},{3,1},{4,6},{5,7},{6,4},{7,5},{8,10},{9,11},{10,... | collective-permute-start | bytes 1032200 | tf_op jit(solution)/shard_map/ppermute | solution.py:70
  (94 other events, 792.6 us)
where the time goes:
time: 413 us; the launch traced here: 407 us
  waiting for transfers between devices  143 us (35%)
  Pallas kernels  84.4 us (20%)
  starting transfers between devices  57.6 us (14%)
  matrix products  51.4 us (12%)
  local copies, waits for them, and re-layouts  41.8 us (10%)
  other arithmetic  27.5 us (7%)
    ppermute x30, waiting for transfers between devices, xor_swap(): return lax.ppermute(value, axis, [(i, i ^ mask) for i in range(count)])  125 us
    ppermute x30, starting transfers between devices, xor_swap(): return lax.ppermute(value, axis, [(i, i ^ mask) for i in range(count)])  44 us
    pallas_call x3, Pallas kernels, attend_backward(): pl.pallas_call(functools.partial(backward_kernel, blocks), out_shape=(jax...  37.1 us
    pallas_call x3, Pallas kernels, attend_forward(): pl.pallas_call(functools.partial(forward_kernel, blocks), out_shape=(jax....  34 us
    dot_general x7, matrix products, left_inner(): lax.dot_general(left_mat, right_mat, (((0,), (0,)), ((), ())), preferred_...  20.4 us
    dot_general x7, matrix products, right_inner(): lax.dot_general(left_mat, right_mat, (((1,), (1,)), ((), ())), preferred_...  19.9 us
    unnamed x148, local copies, waits for them, and re-layouts  14.8 us
    pallas_call x4, Pallas kernels, local_call(): pl.pallas_call(kernel, out_shape=outs, in_specs=[pl.BlockSpec(memory_spac...  13.3 us
  transfers between devices with their start and end apart: 51, of which 21 were waited for; matrix products, arithmetic and copies ran while one was open for 21% of the time, Pallas kernels for 20%

commit v1 on v0

--- a/solution.py
+++ b/solution.py
@@ -103,12 +103,14 @@
 
 
 def two_level(piece, used):
-    arrived = [xor_swap(piece, "col", k) for k in range(1, lax.axis_size("col"))]
+    arrived = []
+    for k in range(1, lax.axis_size("col")):
+        arrived.append(xor_swap(piece, "col", k))
     ours = jnp.stack([one[:used] for one in arrived])
     return arrived, [ours] + [xor_swap(ours, "dp", j) for j in range(1, 4)]
 
 
-def reduce_all(quarters):
+def reduce_dp(quarters):
     own = lax.axis_index("dp")
 
     def part(k):
@@ -120,7 +122,11 @@
     total = part(0).astype(F32)
     for one in arrived:
         total = total + one.astype(F32)
-    piece = scattered(total.astype(BF), "col", 0).astype(BF)
+    return total.astype(BF)
+
+
+def reduce_col(ours):
+    piece = scattered(ours, "col", 0).astype(BF)
     return [piece] + [xor_swap(piece, "dp", k) for k in range(1, 4)]
 
 
@@ -552,33 +558,28 @@
     qkv_piece = jnp.swapaxes(dp_part(w_qkv, own_dp), 0, 1)
     depth = qkv_piece.shape[1]
     vectors = jnp.concatenate(
-        [
-            bias_qv.reshape(-1),
-            bias_out,
-            gain_attn,
-            shift_attn,
-            bias_down,
-            gain_ffn,
-            shift_ffn,
-            bias_in,
-        ]
+        [bias_out, gain_attn, shift_attn, bias_down, gain_ffn, shift_ffn, bias_in]
     )
     share = bias_out.shape[0]
     vector_rows = 16
     first_piece = jnp.concatenate(
-        [qkv_piece.reshape(3 * depth, WIDE), padded_rows(vectors[None], vector_rows)[0]], axis=0
+        [
+            qkv_piece.reshape(3 * depth, WIDE),
+            jnp.pad(bias_qv, ((0, vector_rows - 2), (0, WIDE - share))),
+        ],
+        axis=0,
     )
     places = places_of()
     if col_grid > 4:
         first_cols = gathered(first_piece, "col")
-        vectors_col = first_cols[:, 3 * depth :]
+        bias_col = first_cols[:, 3 * depth :]
         qkv_parts = gathered(first_cols[:, : 3 * depth], "dp")
         w_qkv_half = jnp.transpose(
             qkv_parts.reshape(4, col_grid, 3, depth, PAIRS, LANES), (1, 0, 3, 4, 2, 5)
         ).reshape(D, 3 * WIDE)
     else:
         first_arrived, first_parts = two_level(first_piece, 3 * depth)
-        vectors_col = jnp.stack(
+        bias_col = jnp.stack(
             picked([one[3 * depth :] for one in [first_piece] + first_arrived], "col")
         )
         w_qkv_half = local_call(
@@ -587,27 +588,8 @@
             [jnp.swapaxes(w_qkv, 0, 1)] + first_parts,
             jax.ShapeDtypeStruct((D, 3 * WIDE), BF),
         )
-    vectors_col = vectors_col.reshape(col_grid, vector_rows * WIDE)[:, : vectors.shape[0]]
-    vectors_both = swap(vectors_col)
-
-    def vector(at, count=1):
-        mine = vectors_col[:, at * share : (at + count) * share].reshape(-1)
-        other = vectors_both[:, at * share : (at + count) * share].reshape(-1)
-        return mine.astype(F32), other.astype(F32)
-
-    def whole_vector(at):
-        mine, other = vector(at)
-        return ordered(row, mine, other, 0)[None]
-
-    bias_q = vectors_col[:, :share].reshape(-1).astype(F32)
-    bias_v = vectors_col[:, share : 2 * share].reshape(-1).astype(F32)
-    bias_out_f = whole_vector(2)
-    gain_attn_f = whole_vector(3)
-    shift_attn_f = whole_vector(4)
-    bias_down_f = whole_vector(5)
-    gain_ffn_f = whole_vector(6)
-    shift_ffn_f = whole_vector(7)
-    bias_in_mine, bias_in_other = vector(8, 4)
+    bias_q = bias_col[:, 0, :share].reshape(-1).astype(F32)
+    bias_v = bias_col[:, 1, :share].reshape(-1).astype(F32)
 
     input_full = ordered(row, layer_input, swap(layer_input), 1)
     input_tokens = half_of(input_full, row, 0).astype(F32)
@@ -634,12 +616,8 @@
     kv_others = []
     for pair in range(PAIRS):
         kv_local = qkv_low[:, (3 * pair + 1) * LANES : (3 * pair + 3) * LANES]
-        kv_others.append(
-            jnp.concatenate(
-                [lax.ppermute(kv_local, "col", group_perm(j, False)) for j in range(1, group)],
-                axis=0,
-            )
-        )
+        arrived = [lax.ppermute(kv_local, "col", group_perm(j, False)) for j in range(1, group)]
+        kv_others.append(jnp.concatenate(arrived, axis=0))
 
     down_piece = lanes_to_rows(dp_part(w_down, own_dp)[None])[0]
     in_piece = lanes_to_rows(dp_part(w_in, own_dp)[None])[0]
@@ -647,6 +625,7 @@
         out_piece = lanes_to_rows(dp_part(w_out, own_dp)[None])[0]
         later_piece = jnp.concatenate([down_piece, in_piece, out_piece], axis=0)
         later_parts = gathered(gathered(later_piece, "col"), "dp")
+        vectors_col = gathered(vectors, "col")
         cut_down = down_piece.shape[0]
         cut_in = cut_down + in_piece.shape[0]
 
@@ -662,8 +641,15 @@
         out_piece = lax.dynamic_slice(
             w_out, (own_dp % 2 * out_half, own_dp // 2 * WIDE), (out_half, WIDE)
         )
-        later_piece = jnp.concatenate([down_piece, in_piece, out_piece], axis=0)
-        _, later_parts = two_level(later_piece, later_piece.shape[0])
+        used = down_piece.shape[0] + in_piece.shape[0] + out_half
+        later_piece = jnp.concatenate(
+            [down_piece, in_piece, out_piece, padded_rows(vectors[None], vector_rows)[0]], axis=0
+        )
+        later_arrived, later_parts = two_level(later_piece, used)
+        vectors_col = jnp.stack(
+            picked([one[used:] for one in [later_piece] + later_arrived], "col")
+        )
+        vectors_col = vectors_col.reshape(col_grid, -1)[:, : vectors.shape[0]]
         w_down_mine, w_in_mine, w_out_mine = local_call(
             later_kernel,
             places,
@@ -674,6 +660,25 @@
                 jax.ShapeDtypeStruct((4 * w_out.shape[0], D), BF),
             ),
         )
+    vectors_both = swap(vectors_col)
+
+    def vector(at, count=1):
+        mine = vectors_col[:, at * share : (at + count) * share].reshape(-1)
+        other = vectors_both[:, at * share : (at + count) * share].reshape(-1)
+        return mine.astype(F32), other.astype(F32)
+
+    def whole_vector(at):
+        mine, other = vector(at)
+        return ordered(row, mine, other, 0)[None]
+
+    bias_out_f = whole_vector(0)
+    gain_attn_f = whole_vector(1)
+    shift_attn_f = whole_vector(2)
+    bias_down_f = whole_vector(3)
+    gain_ffn_f = whole_vector(4)
+    shift_ffn_f = whole_vector(5)
+    bias_in_mine, bias_in_other = vector(6, 4)
+
     w_out_other, w_in_other, w_down_other = swap(w_out_mine), swap(w_in_mine), swap(w_down_mine)
 
     own_lengths = lax.dynamic_index_in_dim(lengths, start_row // LEN, 0, keepdims=False)
@@ -779,7 +784,7 @@
         axis=2,
     )
     early, grad_attended = lax.optimization_barrier((early, grad_attended))
-    early_parts = reduce_all(early)
+    early_dp = reduce_dp(early)
 
     grad_pairs = []
     for pair in range(PAIRS):
@@ -807,7 +812,9 @@
         ],
         axis=2,
     )
-    late_parts = reduce_all(late)
+    late, early_dp = lax.optimization_barrier((late, early_dp))
+    early_parts = reduce_col(early_dp)
+    late_parts = reduce_col(reduce_dp(late))
 
     partial = right_inner(grad_qkv, w_qkv_half)
     arrived = swap(half_of(partial, 1 - row, 1).astype(BF)).astype(F32)

time: 413 us -> 385 us (0.932)
  waiting for transfers between devices: 143 us -> 104 us
  local copies, waits for them, and re-layouts: 41.8 us -> 49.3 us
  starting transfers between devices: 57.6 us -> 63.9 us
    ppermute x30, waiting for transfers between devices: 125 us -> 92.7 us  [xor_swap(): return lax.ppermute(value, axis, [(i, i ^ mask) for i in range(count)])]
    ppermute x3, waiting for transfers between devices: 7.99 us -> 0.31 us  [body(): lax.ppermute(others[(j - 1) * rows:j * rows], 'col', group_perm(j, True))]
    ppermute x30, starting transfers between devices: 44 us -> 49.5 us  [xor_swap(): return lax.ppermute(value, axis, [(i, i ^ mask) for i in range(count)])]
    unnamed x148 -> x146, local copies, waits for them, and re-layouts: 14.8 us -> 11.8 us
  transfers between devices with their start and end apart: 51 -> 51, of which waited for: 21 -> 16; matrix products, arithmetic and copies ran while one was open for 21% -> 25% of each run, Pallas kernels for 20% -> 22%
where the time goes in v1:
time: 385 us; the launch traced here: 379 us
  waiting for transfers between devices  104 us (27%)
  Pallas kernels  84.5 us (22%)
  starting transfers between devices  63.9 us (17%)
  local copies, waits for them, and re-layouts  49.3 us (13%)
  matrix products  48 us (12%)
  other arithmetic  27.6 us (7%)
    ppermute x30, waiting for transfers between devices, xor_swap(): return lax.ppermute(value, axis, [(i, i ^ mask) for i in range(count)])  92.7 us
    ppermute x30, starting transfers between devices, xor_swap(): return lax.ppermute(value, axis, [(i, i ^ mask) for i in range(count)])  49.5 us
    pallas_call x3, Pallas kernels, attend_backward(): pl.pallas_call(functools.partial(backward_kernel, blocks), out_shape=(jax...  37.2 us
    pallas_call x3, Pallas kernels, attend_forward(): pl.pallas_call(functools.partial(forward_kernel, blocks), out_shape=(jax....  34.1 us
    dot_general x7, matrix products, right_inner(): lax.dot_general(left_mat, right_mat, (((1,), (1,)), ((), ())), preferred_...  18.9 us
    dot_general x7, matrix products, left_inner(): lax.dot_general(left_mat, right_mat, (((0,), (0,)), ((), ())), preferred_...  18.9 us
    pallas_call x4, Pallas kernels, local_call(): pl.pallas_call(kernel, out_shape=outs, in_specs=[pl.BlockSpec(memory_spac...  13.2 us
    unnamed x146, local copies, waits for them, and re-layouts  11.8 us
  transfers between devices with their start and end apart: 51, of which 16 were waited for; matrix products, arithmetic and copies ran while one was open for 25% of the time, Pallas kernels for 22%

profile of v1, /device:TPU:0, one launch (start us, length us, event | category | flops | bytes accessed | tf_op | source)
XLA Modules:
  0.0 379.2 jit_solution(2938500874511421895)
XLA Ops:
  3.0 5.1 %collective-permute-start.3 = (bf16[160,384]{1,0:T(8,128)(2,1)}, bf16[160,384]{1,0:T(8,128)(2,1)S(1)}, u32[]{:S(2)}, u32[]{:S(2)}) collective-permute-start(bf16[160,384]{1,0:T(8,128)(2,1)} %pad_maximum_fusion.4), channel_id=1, source_target_pairs={{0,3},{1,2},{2,1},{3,0},{4,7},{5,6},{6,5},{7,4},{8,11},{9,10},{10,... | collective-permute-start | bytes 368648 | tf_op jit(solution)/shard_map/ppermute | solution.py:70
  8.6 4.8 %concatenate.162 = bf16[960]{0:T(1024)(128)(2,1)S(1)} concatenate(bf16[96]{0:T(256)(128)(2,1)} %param.20, bf16[96]{0:T(256)(128)(2,1)} %param.21, bf16[96]{0:T(256)(128)(2,1)} %param.22, bf16[96]{0:T(256)(128)(2,1)} %param.26, bf16[96]{0:T(256)(128)(2,1)} %param.27, bf16[96]{0:T(256)(128)(2,1)} %param.28, bf16[384]{0:T(512)(128)(2,1)} %param.24), dimensions={0} | concatenate | bytes 3840 | tf_op jit(solution)/shard_map/concatenate | solution.py:560
  16.3 3.9 %collective-permute-start.12 = (bf16[448,384]{1,0:T(8,128)(2,1)S(1)}, bf16[448,384]{1,0:T(8,128)(2,1)}, u32[]{:S(2)}, u32[]{:S(2)}) collective-permute-start(bf16[448,384]{1,0:T(8,128)(2,1)S(1)} %pad_maximum_fusion.2), channel_id=1, source_target_pairs={{0,3},{1,2},{2,1},{3,0},{4,7},{5,6},{6,5},{7,4},{8,11},{9,10},{10,... | collective-permute-start | bytes 1032200 | tf_op jit(solution)/shard_map/ppermute | solution.py:70
  31.8 17.0 %collective-permute-done.11 = bf16[448,384]{1,0:T(8,128)(2,1)} collective-permute-done((bf16[448,384]{1,0:T(8,128)(2,1)S(1)}, bf16[448,384]{1,0:T(8,128)(2,1)}, u32[]{:S(2)}, u32[]{:S(2)}) %collective-permute-start.11) | collective-permute-done | bytes 344096 | tf_op jit(solution)/shard_map/ppermute | solution.py:70
  72.9 8.9 %collective-permute-done.7.ko_ref.vo_ref = bf16[1024,256]{1,0:T(8,128)(2,1)} collective-permute-done((bf16[1024,256]{1,0:T(8,128)(2,1)}, bf16[1024,256]{1,0:T(8,128)(2,1)}, u32[]{:S(2)}, u32[]{:S(2)}) %collective-permute-start.7) | collective-permute-done | bytes 524320 | tf_op jit(solution)/shard_map/ppermute | solution.py:619
  81.8 11.7 %attend_forward.3 = (bf16[1024,128]{1,0:T(8,128)(2,1)}, f32[8,2048]{1,0:T(8,128)}) custom-call(s32[9]{0:T(128)} %pad_add_fusion.1.table, bf16[1024,1152]{1,0:T(8,128)(2,1)} %copy-done.2, bf16[1024,1152]{1,0:T(8,128)(2,1)} %copy-done.2, bf16[1024,1152]{1,0:T(8,128)(2,1)} %copy-done.2, bf16[1024,256]{1,0:T(8,128)(2,1)} %collective-permute-done.7.ko_ref.vo_ref, ...), custom_call_target="tpu_custom_call" | custom-call | flops 2147483648 | bytes 1048576 | tf_op jit(solution)/shard_map/attend_forward/pallas_call | solution.py:422
  94.5 11.2 %attend_forward.4 = (bf16[1024,128]{1,0:T(8,128)(2,1)}, f32[8,2048]{1,0:T(8,128)}) custom-call(s32[9]{0:T(128)} %pad_add_fusion.1.table, bf16[1024,1152]{1,0:T(8,128)(2,1)} %copy-done.2, bf16[1024,1152]{1,0:T(8,128)(2,1)} %copy-done.2, bf16[1024,1152]{1,0:T(8,128)(2,1)} %copy-done.2, bf16[1024,256]{1,0:T(8,128)(2,1)} %collective-permute-done.8.ko_ref.vo_ref, ...), custom_call_target="tpu_custom_call" | custom-call | flops 2147483648 | bytes 1048576 | tf_op jit(solution)/shard_map/attend_forward/pallas_call | solution.py:422
  106.7 11.2 %attend_forward.5 = (bf16[1024,128]{1,0:T(8,128)(2,1)}, f32[8,2048]{1,0:T(8,128)}) custom-call(s32[9]{0:T(128)} %pad_add_fusion.1.table, bf16[1024,1152]{1,0:T(8,128)(2,1)} %copy-done.2, bf16[1024,1152]{1,0:T(8,128)(2,1)} %copy-done.2, bf16[1024,1152]{1,0:T(8,128)(2,1)} %copy-done.2, bf16[1024,256]{1,0:T(8,128)(2,1)} %collective-permute-done.9.ko_ref.vo_ref, ...), custom_call_target="tpu_custom_call" | custom-call | flops 2147483648 | bytes 1048576 | tf_op jit(solution)/shard_map/attend_forward/pallas_call | solution.py:422
  118.0 5.3 %shard_map.255 = (bf16[1536,768]{1,0:T(8,128)(2,1)}, bf16[768,1536]{1,0:T(8,128)(2,1)}, bf16[384,768]{1,0:T(8,128)(2,1)}) custom-call(s32[2]{0:T(128)} %pad_add_fusion.2.places, bf16[384,768]{1,0:T(8,128)(2,1)} %own_down.1, bf16[192,1536]{1,0:T(8,128)(2,1)} %own_in.1, bf16[96,768]{1,0:T(8,128)(2,1)} %own_out.1, bf16[3,432,384]{2,1,0:T(8,128)(2,1)} %copy-done.3, ...), custom_call_target="tpu_custom_call" | custom-call | bytes 4194304 | tf_op jit(solution)/shard_map/pallas_call | solution.py:143
  153.1 4.6 %multiply_reduce_fusion = (f32[768]{0:T(1024)S(1)}, f32[512]{0:T(512)S(1)}, f32[512]{0:T(512)S(1)}, f32[768]{0:T(1024)S(1)}, f32[512,768]{1,0:T(8,128)S(1)}) fusion(f32[512,768]{1,0:T(8,128)S(1)} %get-tuple-element.155, f32[512]{0:T(512)S(1)} %add_rsqrt_fusion.1, f32[512]{0:T(512)S(1)} %broadcast_multiply_fusion.5, f32[768]{0:T(1024)S(1)} %maximum_select_fusion.6, ...), kind=kOutput, calls=%fused_computation.48 | convolution fusion | flops 1212282368 | bytes 10241024 | tf_op jit(solution)/shard_map/dot_general | solution.py:37
  186.2 12.3 %attend_backward.5 = (bf16[1024,128]{1,0:T(8,128)(2,1)}, f32[1024,128]{1,0:T(8,128)}, f32[1024,128]{1,0:T(8,128)}, bf16[1024,256]{1,0:T(8,128)(2,1)}) custom-call(s32[9]{0:T(128)} %pad_add_fusion.1.table, bf16[1024,1152]{1,0:T(8,128)(2,1)} %copy-done.2, bf16[1024,1152]{1,0:T(8,128)(2,1)} %copy-done.2, bf16[1024,1152]{1,0:T(8,128)(2,1)} %copy-done.2, ...), custom_call_target="tpu_custom_call" | custom-call | flops 5368709120 | bytes 2097152 | tf_op jit(solution)/shard_map/attend_backward/pallas_call | solution.py:449
  198.6 6.0 %collective-permute-start.31 = (bf16[1024,256]{1,0:T(8,128)(2,1)}, bf16[1024,256]{1,0:T(8,128)(2,1)S(1)}, u32[]{:S(2)}, u32[]{:S(2)}) collective-permute-start(bf16[1024,256]{1,0:T(8,128)(2,1)} %get-tuple-element.62), channel_id=1, source_target_pairs={{0,1},{1,0},{2,3},{3,2},{4,5},{5,4},{6,7},{7,6},{8,9},{9,8},{10,11... | collective-permute-start | bytes 1572872 | tf_op jit(solution)/shard_map/ppermute | solution.py:796
  204.6 12.5 %attend_backward.3 = (bf16[1024,128]{1,0:T(8,128)(2,1)}, f32[1024,128]{1,0:T(8,128)}, f32[1024,128]{1,0:T(8,128)}, bf16[1024,256]{1,0:T(8,128)(2,1)}) custom-call(s32[9]{0:T(128)} %pad_add_fusion.1.table, bf16[1024,1152]{1,0:T(8,128)(2,1)} %copy-done.2, bf16[1024,1152]{1,0:T(8,128)(2,1)} %copy-done.2, bf16[1024,1152]{1,0:T(8,128)(2,1)} %copy-done.2, ...), custom_call_target="tpu_custom_call" | custom-call | flops 5368709120 | bytes 2097152 | tf_op jit(solution)/shard_map/attend_backward/pallas_call | solution.py:449
  218.1 12.4 %attend_backward.4 = (bf16[1024,128]{1,0:T(8,128)(2,1)}, f32[1024,128]{1,0:T(8,128)}, f32[1024,128]{1,0:T(8,128)}, bf16[1024,256]{1,0:T(8,128)(2,1)}) custom-call(s32[9]{0:T(128)} %pad_add_fusion.1.table, bf16[1024,1152]{1,0:T(8,128)(2,1)} %copy-done.2, bf16[1024,1152]{1,0:T(8,128)(2,1)} %copy-done.2, bf16[1024,1152]{1,0:T(8,128)(2,1)} %copy-done.2, ...), custom_call_target="tpu_custom_call" | custom-call | flops 5368709120 | bytes 2097152 | tf_op jit(solution)/shard_map/attend_backward/pallas_call | solution.py:449
  233.2 4.3 %dynamic-slice_bitcast_fusion.2 = (bf16[4,448,384]{2,1,0:T(8,128)(2,1)}, bf16[4,448,384]{2,1,0:T(8,128)(2,1)}, bf16[4,448,384]{2,1,0:T(8,128)(2,1)}) fusion(bf16[4,4,448,384]{3,2,0,1:T(8,128)(2,1)} %copy.94, s32[]{:T(128)S(6)} %select_n.246, s32[]{:T(128)S(6)} %select_n.248, s32[]{:T(128)S(6)} %select_n.247), kind=kLoop, calls=%fused_computation.65 | loop fusion | bytes 8257548 | tf_op jit(solution)/shard_map/jit(dynamic_index_in_dim)/squeeze | solution.py:117
  237.5 4.3 %collective-permute-start.33 = (bf16[4,448,384]{2,1,0:T(8,128)(2,1)}, bf16[4,448,384]{2,1,0:T(8,128)(2,1)S(1)}, u32[]{:S(2)}, u32[]{:S(2)}) collective-permute-start(bf16[4,448,384]{2,1,0:T(8,128)(2,1)} %get-tuple-element.90), channel_id=1, source_target_pairs={{0,8},{8,0},{16,24},{24,16},{1,9},{9,1},{17,25},{25,17},{2,10},{10... | collective-permute-start | bytes 4128776 | tf_op jit(solution)/shard_map/ppermute | solution.py:70
  244.6 8.4 %collective-permute-start.35 = (bf16[4,448,384]{2,1,0:T(8,128)(2,1)}, bf16[4,448,384]{2,1,0:T(8,128)(2,1)}, u32[]{:S(2)}, u32[]{:S(2)}) collective-permute-start(bf16[4,448,384]{2,1,0:T(8,128)(2,1)} %get-tuple-element.91), channel_id=1, source_target_pairs={{0,24},{8,16},{16,8},{24,0},{1,25},{9,17},{17,9},{25,1},{2,26},{10... | collective-permute-start | bytes 4128776 | tf_op jit(solution)/shard_map/ppermute | solution.py:70
  259.9 3.9 %convolution_convert_fusion = bf16[768,1152]{1,0:T(8,128)(2,1)S(1)} fusion(bf16[1024,768]{1,0:T(8,128)(2,1)S(1)} %copy-done.7, bf16[1024,1152]{1,0:T(8,128)(2,1)} %fusion.43), kind=kOutput, calls=%fused_computation.5 | convolution fusion | flops 1812824064 | bytes 5701632 | tf_op jit(solution)/shard_map/dot_general | solution.py:31
  265.8 3.9 %fusion.77 = f32[1024,768]{1,0:T(8,128)S(1)} fusion(bf16[1024,1152]{1,0:T(8,128)(2,1)} %fusion.43, bf16[768,1152]{1,0:T(8,128)(2,1)S(1)} %copy-done.11), kind=kOutput, calls=%fused_computation.270 | convolution fusion | flops 1811939328 | bytes 7274496 | tf_op jit(solution)/shard_map/dot_general | solution.py:37
  273.1 31.2 %collective-permute-done.35 = bf16[4,448,384]{2,1,0:T(8,128)(2,1)} collective-permute-done((bf16[4,448,384]{2,1,0:T(8,128)(2,1)}, bf16[4,448,384]{2,1,0:T(8,128)(2,1)}, u32[]{:S(2)}, u32[]{:S(2)}) %collective-permute-start.35) | collective-permute-done | bytes 1376288 | tf_op jit(solution)/shard_map/ppermute | solution.py:70
  304.4 12.3 %collective-permute-done.34 = bf16[4,448,384]{2,1,0:T(8,128)(2,1)} collective-permute-done((bf16[4,448,384]{2,1,0:T(8,128)(2,1)}, bf16[4,448,384]{2,1,0:T(8,128)(2,1)}, u32[]{:S(2)}, u32[]{:S(2)}) %collective-permute-start.34) | collective-permute-done | bytes 1376288 | tf_op jit(solution)/shard_map/ppermute | solution.py:70
  332.6 7.5 %collective-permute-done.47 = bf16[448,384]{1,0:T(8,128)(2,1)S(1)} collective-permute-done((bf16[448,384]{1,0:T(8,128)(2,1)S(1)}, bf16[448,384]{1,0:T(8,128)(2,1)S(1)}, u32[]{:S(2)}, u32[]{:S(2)}) %collective-permute-start.47) | collective-permute-done | bytes 344096 | tf_op jit(solution)/shard_map/ppermute | solution.py:70
  340.0 13.7 %collective-permute-done.46 = bf16[448,384]{1,0:T(8,128)(2,1)S(1)} collective-permute-done((bf16[448,384]{1,0:T(8,128)(2,1)S(1)}, bf16[448,384]{1,0:T(8,128)(2,1)S(1)}, u32[]{:S(2)}, u32[]{:S(2)}) %collective-permute-start.46) | collective-permute-done | bytes 344096 | tf_op jit(solution)/shard_map/ppermute | solution.py:70
  363.3 4.1 %collective-permute-done.40 = bf16[160,384]{1,0:T(8,128)(2,1)S(1)} collective-permute-done((bf16[160,384]{1,0:T(8,128)(2,1)S(1)}, bf16[160,384]{1,0:T(8,128)(2,1)S(1)}, u32[]{:S(2)}, u32[]{:S(2)}) %collective-permute-start.40) | collective-permute-done | bytes 122912 | tf_op jit(solution)/shard_map/ppermute | solution.py:70
  (428 shorter events, 156.4 us)
Async XLA Ops:
  3.0 20.8 %collective-permute-start.3 = (bf16[160,384]{1,0:T(8,128)(2,1)}, bf16[160,384]{1,0:T(8,128)(2,1)S(1)}, u32[]{:S(2)}, u32[]{:S(2)}) collective-permute-start(bf16[160,384]{1,0:T(8,128)(2,1)} %pad_maximum_fusion.4), channel_id=1, source_target_pairs={{0,3},{1,2},{2,1},{3,0},{4,7},{5,6},{6,5},{7,4},{8,11},{9,10},{10,... | collective-permute-start | bytes 368648 | tf_op jit(solution)/shard_map/ppermute | solution.py:70
  20.2 28.5 %collective-permute-start.11 = (bf16[448,384]{1,0:T(8,128)(2,1)S(1)}, bf16[448,384]{1,0:T(8,128)(2,1)}, u32[]{:S(2)}, u32[]{:S(2)}) collective-permute-start(bf16[448,384]{1,0:T(8,128)(2,1)S(1)} %pad_maximum_fusion.2), channel_id=1, source_target_pairs={{0,2},{1,3},{2,0},{3,1},{4,6},{5,7},{6,4},{7,5},{8,10},{9,11},{10,... | collective-permute-start | bytes 1032200 | tf_op jit(solution)/shard_map/ppermute | solution.py:70
  23.7 27.2 %collective-permute-start.10 = (bf16[448,384]{1,0:T(8,128)(2,1)S(1)}, bf16[448,384]{1,0:T(8,128)(2,1)S(1)}, u32[]{:S(2)}, u32[]{:S(2)}) collective-permute-start(bf16[448,384]{1,0:T(8,128)(2,1)S(1)} %pad_maximum_fusion.2), channel_id=1, source_target_pairs={{0,1},{1,0},{2,3},{3,2},{4,5},{5,4},{6,7},{7,6},{8,9},{9,8},{10,11... | collective-permute-start | bytes 1032200 | tf_op jit(solution)/shard_map/ppermute | solution.py:70
  24.4 37.3 %collective-permute-start = (bf16[1024,384]{1,0:T(8,128)(2,1)S(1)}, bf16[1024,384]{1,0:T(8,128)(2,1)S(1)}, u32[]{:S(2)}, u32[]{:S(2)}) collective-permute-start(bf16[1024,384]{1,0:T(8,128)(2,1)S(1)} %copy-done.24), channel_id=1, source_target_pairs={{0,4},{4,0},{1,5},{5,1},{2,6},{6,2},{3,7},{7,3},{8,12},{12,8},{9,1... | collective-permute-start | bytes 2359304 | tf_op jit(solution)/shard_map/ppermute | solution.py:43
  26.5 30.2 %collective-permute-start.6 = (bf16[3,144,384]{2,1,0:T(8,128)(2,1)S(1)}, bf16[3,144,384]{2,1,0:T(8,128)(2,1)}, u32[]{:S(2)}, u32[]{:S(2)}) collective-permute-start(bf16[3,144,384]{2,1,0:T(8,128)(2,1)S(1)} %pad_maximum_fusion.3.refs_0_), channel_id=1, source_target_pairs={{0,24},{8,16},{16,8},{24,0},{1,25},{9,17},{17,9},{25,1},{2,26},{10... | collective-permute-start | bytes 995336 | tf_op jit(solution)/shard_map/ppermute | solution.py:70
  29.3 27.9 %collective-permute-start.5 = (bf16[3,144,384]{2,1,0:T(8,128)(2,1)S(1)}, bf16[3,144,384]{2,1,0:T(8,128)(2,1)}, u32[]{:S(2)}, u32[]{:S(2)}) collective-permute-start(bf16[3,144,384]{2,1,0:T(8,128)(2,1)S(1)} %pad_maximum_fusion.3.refs_0_), channel_id=1, source_target_pairs={{0,16},{8,24},{16,0},{24,8},{1,17},{9,25},{17,1},{25,9},{2,18},{10... | collective-permute-start | bytes 995336 | tf_op jit(solution)/shard_map/ppermute | solution.py:70
  55.2 62.9 %collective-permute-start.15 = (bf16[3,432,384]{2,1,0:T(8,128)(2,1)S(1)}, bf16[3,432,384]{2,1,0:T(8,128)(2,1)}, u32[]{:S(2)}, u32[]{:S(2)}) collective-permute-start(bf16[3,432,384]{2,1,0:T(8,128)(2,1)S(1)} %pad_maximum_fusion.1.refs_0_), channel_id=1, source_target_pairs={{0,24},{8,16},{16,8},{24,0},{1,25},{9,17},{17,9},{25,1},{2,26},{10... | collective-permute-start | bytes 2985992 | tf_op jit(solution)/shard_map/ppermute | solution.py:70
  56.7 61.3 %collective-permute-start.14 = (bf16[3,432,384]{2,1,0:T(8,128)(2,1)S(1)}, bf16[3,432,384]{2,1,0:T(8,128)(2,1)}, u32[]{:S(2)}, u32[]{:S(2)}) collective-permute-start(bf16[3,432,384]{2,1,0:T(8,128)(2,1)S(1)} %pad_maximum_fusion.1.refs_0_), channel_id=1, source_target_pairs={{0,16},{8,24},{16,0},{24,8},{1,17},{9,25},{17,1},{25,9},{2,18},{10... | collective-permute-start | bytes 2985992 | tf_op jit(solution)/shard_map/ppermute | solution.py:70
  57.2 60.8 %collective-permute-start.13 = (bf16[3,432,384]{2,1,0:T(8,128)(2,1)S(1)}, bf16[3,432,384]{2,1,0:T(8,128)(2,1)}, u32[]{:S(2)}, u32[]{:S(2)}) collective-permute-start(bf16[3,432,384]{2,1,0:T(8,128)(2,1)S(1)} %pad_maximum_fusion.1.refs_0_), channel_id=1, source_target_pairs={{0,8},{8,0},{16,24},{24,16},{1,9},{9,1},{17,25},{25,17},{2,10},{10... | collective-permute-start | bytes 2985992 | tf_op jit(solution)/shard_map/ppermute | solution.py:70
  66.9 27.5 %collective-permute-start.8 = (bf16[1024,256]{1,0:T(8,128)(2,1)}, bf16[1024,256]{1,0:T(8,128)(2,1)}, u32[]{:S(2)}, u32[]{:S(2)}) collective-permute-start(bf16[1024,256]{1,0:T(8,128)(2,1)} %get-tuple-element.94), channel_id=1, source_target_pairs={{1,0},{0,1},{3,2},{2,3},{5,4},{4,5},{7,6},{6,7},{9,8},{8,9},{11,10... | collective-permute-start | bytes 1572872 | tf_op jit(solution)/shard_map/ppermute | solution.py:619
  81.8 24.9 %collective-permute-start.9 = (bf16[1024,256]{1,0:T(8,128)(2,1)}, bf16[1024,256]{1,0:T(8,128)(2,1)}, u32[]{:S(2)}, u32[]{:S(2)}) collective-permute-start(bf16[1024,256]{1,0:T(8,128)(2,1)} %get-tuple-element.93), channel_id=1, source_target_pairs={{1,0},{0,1},{3,2},{2,3},{5,4},{4,5},{7,6},{6,7},{9,8},{8,9},{11,10... | collective-permute-start | bytes 1572872 | tf_op jit(solution)/shard_map/ppermute | solution.py:619
  94.5 42.8 %collective-permute-start.22 = (bf16[512,384]{1,0:T(8,128)(2,1)}, bf16[512,384]{1,0:T(8,128)(2,1)S(1)}, u32[]{:S(2)}, u32[]{:S(2)}) collective-permute-start(bf16[512,384]{1,0:T(8,128)(2,1)} %get-tuple-element.109), channel_id=1, source_target_pairs={{0,4},{4,0},{1,5},{5,1},{2,6},{6,2},{3,7},{7,3},{8,12},{12,8},{9,1... | collective-permute-start | bytes 1179656 | tf_op jit(solution)/shard_map/ppermute | solution.py:43
  170.3 150.1 %collective-permute-start.21 = (bf16[512,384]{1,0:T(8,128)(2,1)}, bf16[512,384]{1,0:T(8,128)(2,1)}, u32[]{:S(2)}, u32[]{:S(2)}) collective-permute-start(bf16[512,384]{1,0:T(8,128)(2,1)} %get-tuple-element.112), channel_id=1, source_target_pairs={{0,4},{4,0},{1,5},{5,1},{2,6},{6,2},{3,7},{7,3},{8,12},{12,8},{9,1... | collective-permute-start | bytes 1179656 | tf_op jit(solution)/shard_map/ppermute | solution.py:43
  171.6 154.5 %collective-permute-start.23 = (f32[512,384]{1,0:T(8,128)}, f32[512,384]{1,0:T(8,128)}, u32[]{:S(2)}, u32[]{:S(2)}) collective-permute-start(f32[512,384]{1,0:T(8,128)} %get-tuple-element.104), channel_id=1, source_target_pairs={{0,4},{4,0},{1,5},{5,1},{2,6},{6,2},{3,7},{7,3},{8,12},{12,8},{9,1... | collective-permute-start | bytes 2359304 | tf_op jit(solution)/shard_map/ppermute | solution.py:43
  198.6 56.9 %collective-permute-start.31 = (bf16[1024,256]{1,0:T(8,128)(2,1)}, bf16[1024,256]{1,0:T(8,128)(2,1)S(1)}, u32[]{:S(2)}, u32[]{:S(2)}) collective-permute-start(bf16[1024,256]{1,0:T(8,128)(2,1)} %get-tuple-element.62), channel_id=1, source_target_pairs={{0,1},{1,0},{2,3},{3,2},{4,5},{5,4},{6,7},{7,6},{8,9},{9,8},{10,11... | collective-permute-start | bytes 1572872 | tf_op jit(solution)/shard_map/ppermute | solution.py:796
  217.1 20.4 %collective-permute-start.29 = (bf16[1024,256]{1,0:T(8,128)(2,1)}, bf16[1024,256]{1,0:T(8,128)(2,1)S(1)}, u32[]{:S(2)}, u32[]{:S(2)}) collective-permute-start(bf16[1024,256]{1,0:T(8,128)(2,1)} %get-tuple-element.52), channel_id=1, source_target_pairs={{0,1},{1,0},{2,3},{3,2},{4,5},{5,4},{6,7},{7,6},{8,9},{9,8},{10,11... | collective-permute-start | bytes 1572872 | tf_op jit(solution)/shard_map/ppermute | solution.py:796
  237.5 35.6 %collective-permute-start.33 = (bf16[4,448,384]{2,1,0:T(8,128)(2,1)}, bf16[4,448,384]{2,1,0:T(8,128)(2,1)S(1)}, u32[]{:S(2)}, u32[]{:S(2)}) collective-permute-start(bf16[4,448,384]{2,1,0:T(8,128)(2,1)} %get-tuple-element.90), channel_id=1, source_target_pairs={{0,8},{8,0},{16,24},{24,16},{1,9},{9,1},{17,25},{25,17},{2,10},{10... | collective-permute-start | bytes 4128776 | tf_op jit(solution)/shard_map/ppermute | solution.py:70
  244.6 59.8 %collective-permute-start.35 = (bf16[4,448,384]{2,1,0:T(8,128)(2,1)}, bf16[4,448,384]{2,1,0:T(8,128)(2,1)}, u32[]{:S(2)}, u32[]{:S(2)}) collective-permute-start(bf16[4,448,384]{2,1,0:T(8,128)(2,1)} %get-tuple-element.91), channel_id=1, source_target_pairs={{0,24},{8,16},{16,8},{24,0},{1,25},{9,17},{17,9},{25,1},{2,26},{10... | collective-permute-start | bytes 4128776 | tf_op jit(solution)/shard_map/ppermute | solution.py:70
  255.5 61.1 %collective-permute-start.34 = (bf16[4,448,384]{2,1,0:T(8,128)(2,1)}, bf16[4,448,384]{2,1,0:T(8,128)(2,1)}, u32[]{:S(2)}, u32[]{:S(2)}) collective-permute-start(bf16[4,448,384]{2,1,0:T(8,128)(2,1)} %get-tuple-element.92), channel_id=1, source_target_pairs={{0,16},{8,24},{16,0},{24,8},{1,17},{9,25},{17,1},{25,9},{2,18},{10... | collective-permute-start | bytes 4128776 | tf_op jit(solution)/shard_map/ppermute | solution.py:70
  273.1 53.0 %collective-permute-start.32 = (bf16[1024,384]{1,0:T(8,128)(2,1)S(1)}, bf16[1024,384]{1,0:T(8,128)(2,1)S(1)}, u32[]{:S(2)}, u32[]{:S(2)}) collective-permute-start(bf16[1024,384]{1,0:T(8,128)(2,1)S(1)} %dynamic-slice_convert_fusion), channel_id=1, source_target_pairs={{0,4},{4,0},{1,5},{5,1},{2,6},{6,2},{3,7},{7,3},{8,12},{12,8},{9,1... | collective-permute-start | bytes 2359304 | tf_op jit(solution)/shard_map/ppermute | solution.py:43
  325.9 27.9 %collective-permute-start.46 = (bf16[448,384]{1,0:T(8,128)(2,1)S(1)}, bf16[448,384]{1,0:T(8,128)(2,1)S(1)}, u32[]{:S(2)}, u32[]{:S(2)}) collective-permute-start(bf16[448,384]{1,0:T(8,128)(2,1)S(1)} %get-tuple-element.107), channel_id=1, source_target_pairs={{0,2},{1,3},{2,0},{3,1},{4,6},{5,7},{6,4},{7,5},{8,10},{9,11},{10,... | collective-permute-start | bytes 1032200 | tf_op jit(solution)/shard_map/ppermute | solution.py:70
  326.1 29.1 %collective-permute-start.36 = (bf16[4,160,384]{2,1,0:T(8,128)(2,1)S(1)}, bf16[4,160,384]{2,1,0:T(8,128)(2,1)S(1)}, u32[]{:S(2)}, u32[]{:S(2)}) collective-permute-start(bf16[4,160,384]{2,1,0:T(8,128)(2,1)S(1)} %get-tuple-element.96), channel_id=1, source_target_pairs={{0,8},{8,0},{16,24},{24,16},{1,9},{9,1},{17,25},{25,17},{2,10},{10... | collective-permute-start | bytes 1474568 | tf_op jit(solution)/shard_map/ppermute | solution.py:70
  326.2 29.0 %collective-permute-start.38 = (bf16[4,160,384]{2,1,0:T(8,128)(2,1)S(1)}, bf16[4,160,384]{2,1,0:T(8,128)(2,1)S(1)}, u32[]{:S(2)}, u32[]{:S(2)}) collective-permute-start(bf16[4,160,384]{2,1,0:T(8,128)(2,1)S(1)} %get-tuple-element.97), channel_id=1, source_target_pairs={{0,24},{8,16},{16,8},{24,0},{1,25},{9,17},{17,9},{25,1},{2,26},{10... | collective-permute-start | bytes 1474568 | tf_op jit(solution)/shard_map/ppermute | solution.py:70
  329.0 26.2 %collective-permute-start.37 = (bf16[4,160,384]{2,1,0:T(8,128)(2,1)S(1)}, bf16[4,160,384]{2,1,0:T(8,128)(2,1)S(1)}, u32[]{:S(2)}, u32[]{:S(2)}) collective-permute-start(bf16[4,160,384]{2,1,0:T(8,128)(2,1)S(1)} %get-tuple-element.98), channel_id=1, source_target_pairs={{0,16},{8,24},{16,0},{24,8},{1,17},{9,25},{17,1},{25,9},{2,18},{10... | collective-permute-start | bytes 1474568 | tf_op jit(solution)/shard_map/ppermute | solution.py:70
  (93 other events, 632.2 us)

commit v2 on v1

--- a/solution.py
+++ b/solution.py
@@ -84,22 +84,6 @@
         return lax.all_gather(value, axis, axis=0)
     parts = [value] + [xor_swap(value, axis, k) for k in range(1, count)]
     return jnp.stack(picked(parts, axis))
-
-
-def scattered(value, axis, dim):
-    count = lax.axis_size(axis)
-    if count > 4:
-        return lax.psum_scatter(value, axis, scatter_dimension=dim, tiled=False).astype(F32)
-    own = lax.axis_index(axis)
-
-    def part(k):
-        return lax.dynamic_index_in_dim(value, own ^ k, dim, keepdims=False)
-
-    arrived = [xor_swap(part(k), axis, k) for k in range(1, count)]
-    total = part(0).astype(F32)
-    for one in arrived:
-        total = total + one.astype(F32)
-    return total
 
 
 def two_level(piece, used):
@@ -126,8 +110,28 @@
 
 
 def reduce_col(ours):
-    piece = scattered(ours, "col", 0).astype(BF)
-    return [piece] + [xor_swap(piece, "dp", k) for k in range(1, 4)]
+    count = lax.axis_size("col")
+    if count > 4:
+        return lax.psum_scatter(ours, "col", scatter_dimension=0, tiled=False)
+    own = lax.axis_index("col")
+
+    def part(k):
+        return lax.dynamic_index_in_dim(ours, own ^ k, 0, keepdims=False)
+
+    arrived = []
+    for k in range(1, count):
+        arrived.append(xor_swap(part(k), "col", k))
+    total = part(0).astype(F32)
+    for one in arrived:
+        total = total + one.astype(F32)
+    return total.astype(BF)
+
+
+def spread_dp(piece):
+    parts = [piece]
+    for k in range(1, 4):
+        parts.append(xor_swap(piece, "dp", k))
+    return parts
 
 
 def places_of():
@@ -194,18 +198,23 @@
             out[rows, lanes] = part[at : at + count, :]
 
 
-def early_out_kernel(places, *refs):
-    parts, (down, inner, out) = refs[:-3], refs[-3:]
+def down_out_kernel(places, *refs):
+    parts, down = refs[:-1], refs[-1]
+    dp = places[1]
+    count = down.shape[0] // 4
+    for j in range(4):
+        for i in range(2):
+            down[at_rows((dp ^ j) * count, count), i * WIDE : (i + 1) * WIDE] = parts[j][
+                i * count : (i + 1) * count, :
+            ].astype(F32)
+
+
+def in_out_kernel(places, *refs):
+    parts, (inner, out) = refs[:-2], refs[-2:]
     dp = places[1]
     for j in range(4):
         there = dp ^ j
-        count, at = down.shape[0] // 4, 0
-        for i in range(2):
-            down[at_rows(there * count, count), i * WIDE : (i + 1) * WIDE] = parts[j][
-                at : at + count, :
-            ].astype(F32)
-            at += count
-        count = inner.shape[0] // 4
+        count, at = inner.shape[0] // 4, 0
         for i in range(4):
             inner[at_rows(there * count, count), i * WIDE : (i + 1) * WIDE] = parts[j][
                 at : at + count, :
@@ -218,16 +227,18 @@
         ].astype(F32)
 
 
-def late_out_kernel(places, *refs):
-    parts, out = refs[:-1], refs[-1]
+def qkv_out_kernel(first_row, places, *refs):
+    parts, last_parts, out = refs[:4], refs[4:8], refs[8]
     dp = places[1]
     count = out.shape[1] // 4
     for j in range(4):
         rows = at_rows((dp ^ j) * count, count)
         for pair in range(PAIRS):
+            source = last_parts[j] if pair == PAIRS - 1 else parts[j]
+            start = 0 if pair == PAIRS - 1 else first_row + pair * count
             for kind in range(3):
-                out[kind, rows, pair * LANES : (pair + 1) * LANES] = parts[j][
-                    pair * count : (pair + 1) * count, kind * LANES : (kind + 1) * LANES
+                out[kind, rows, pair * LANES : (pair + 1) * LANES] = source[
+                    start : start + count, kind * LANES : (kind + 1) * LANES
                 ].astype(F32)
 
 
@@ -249,8 +260,8 @@
     return jnp.pad(flat, ((0, 0), (0, 4 * rows * WIDE - size))).reshape(count, 4, rows, WIDE)
 
 
-def first_quarter(parts, rows):
-    stacked = jnp.stack([one[-rows:] for one in parts])
+def first_quarter(parts, start, rows):
+    stacked = jnp.stack([one[start : start + rows] for one in parts])
     return lax.dynamic_index_in_dim(
         stacked, lax.axis_index("dp"), 0, keepdims=False
     ).astype(F32).reshape(-1)
@@ -746,9 +757,10 @@
         return (mine + swap(other.astype(BF)).astype(F32)).astype(BF)
 
     grad_down = both_tokens(left_inner(act_mine, grad_ffn), left_inner(act_other, grad_ffn))
-    grad_in = both_tokens(
-        left_inner(normed_low, grad_hidden_mine), left_inner(normed_low, grad_hidden_other)
-    )
+    down_dp = reduce_dp(quartered_rows(grad_down, col_grid))
+    grad_in_mine = left_inner(normed_low, grad_hidden_mine)
+    grad_in_other = left_inner(normed_low, grad_hidden_other).astype(BF)
+    grad_in = both_tokens(grad_in_mine, grad_in_other)
     grad_out_w = both_tokens(left_inner(att_mine, grad_proj), left_inner(att_other, grad_proj))
     by_row = jnp.stack(
         [
@@ -774,7 +786,6 @@
     vec_pad = 16
     early = jnp.concatenate(
         [
-            quartered_rows(grad_down, col_grid),
             quartered_rows(grad_in, col_grid),
             quartered_halves(grad_out_w, col_grid)
             if col_grid <= 4
@@ -785,8 +796,9 @@
     )
     early, grad_attended = lax.optimization_barrier((early, grad_attended))
     early_dp = reduce_dp(early)
-
-    grad_pairs = []
+    down_parts = spread_dp(reduce_col(down_dp))
+
+    grad_pairs, grad_w_pairs, bias_sums = [], [], []
     for pair in range(PAIRS):
         out, logs = attended[pair]
         grad_query, key_own, value_own, others = attend_backward(
@@ -798,56 +810,73 @@
             ).astype(F32)
             key_own = key_own + arrived[:, :LANES]
             value_own = value_own + arrived[:, LANES:]
-        grad_pairs += [grad_query, key_own.astype(BF), value_own.astype(BF)]
+        grad_pair = jnp.concatenate(
+            [grad_query, key_own.astype(BF), value_own.astype(BF)], axis=1
+        )
+        grad_pairs.append(grad_pair)
+        grad_w_pairs.append(left_inner(input_full, grad_pair).astype(BF))
+        bias_sums.append(jnp.sum(grad_pair, axis=0, dtype=F32))
     grad_qkv = jnp.concatenate(grad_pairs, axis=1)
 
-    grad_w_qkv = left_inner(input_full, grad_qkv).astype(BF)
-    bias_sums = jnp.sum(grad_qkv, axis=0, dtype=F32).reshape(PAIRS, 3, LANES)
-    bias_pair = jnp.stack([bias_sums[:, 0].reshape(-1), bias_sums[:, 2].reshape(-1)])
+    bias_pair = jnp.stack(
+        [
+            jnp.concatenate([one[:LANES] for one in bias_sums]),
+            jnp.concatenate([one[2 * LANES :] for one in bias_sums]),
+        ]
+    )
     bias_pair = jnp.swapaxes(bias_pair.reshape(2, col_grid, share), 0, 1).reshape(col_grid, -1)
+    pairs_dp = reduce_dp(
+        jnp.concatenate([quartered_rows(one, col_grid) for one in grad_w_pairs[:-1]], axis=2),
+    )
+    early_piece = reduce_col(jnp.concatenate([early_dp, pairs_dp], axis=1))
+    early_parts = spread_dp(early_piece)
     late = jnp.concatenate(
         [
-            quartered_rows(grad_w_qkv, col_grid),
+            quartered_rows(grad_w_pairs[-1], col_grid),
             quartered_vector(bias_pair.astype(BF), vec_pad),
         ],
         axis=2,
     )
-    late, early_dp = lax.optimization_barrier((late, early_dp))
-    early_parts = reduce_col(early_dp)
-    late_parts = reduce_col(reduce_dp(late))
+    late_parts = spread_dp(reduce_col(reduce_dp(late)))
 
     partial = right_inner(grad_qkv, w_qkv_half)
     arrived = swap(half_of(partial, 1 - row, 1).astype(BF)).astype(F32)
     grad_input = grad_first_features + half_of(partial, row, 1) + arrived
 
+    cut_in = w_in.shape[0]
+    cut_out = cut_in + w_out.shape[0] // 2
+    cut_vec = cut_out + vec_pad
     if col_grid > 4:
+        down_all = jnp.stack(picked(down_parts, "dp")).astype(F32)
         early_all = jnp.stack(picked(early_parts, "dp")).astype(F32)
         late_all = jnp.stack(picked(late_parts, "dp")).astype(F32)
-        cut_down = 2 * w_down.shape[0] // 4
-        cut_in = cut_down + w_in.shape[0]
-        grad_down_own = rows_to_lanes(early_all[:, :cut_down], 2).reshape(w_down.shape)
-        grad_in_own = rows_to_lanes(early_all[:, cut_down:cut_in], 4).reshape(w_in.shape)
-        grad_out_own = rows_to_lanes(early_all[:, cut_in:-vec_pad], 2).reshape(w_out.shape)
-        qkv_own = late_all[:, :-vec_pad].reshape(4, PAIRS, depth, 3, LANES)
+        grad_down_own = rows_to_lanes(down_all, 2).reshape(w_down.shape)
+        grad_in_own = rows_to_lanes(early_all[:, :cut_in], 4).reshape(w_in.shape)
+        grad_out_own = rows_to_lanes(early_all[:, cut_in:cut_out], 2).reshape(w_out.shape)
+        qkv_own = jnp.concatenate([early_all[:, cut_vec:], late_all[:, :-vec_pad]], axis=1)
+        qkv_own = qkv_own.reshape(4, PAIRS, depth, 3, LANES)
         qkv_own = jnp.transpose(qkv_own, (0, 2, 3, 1, 4)).reshape(w_qkv.shape)
     else:
-        grad_down_own, grad_in_own, grad_out_own = local_call(
-            early_out_kernel,
+        grad_down_own = local_call(
+            down_out_kernel, places, down_parts, jax.ShapeDtypeStruct(w_down.shape, F32)
+        )
+        grad_in_own, grad_out_own = local_call(
+            in_out_kernel,
             places,
             early_parts,
-            tuple(jax.ShapeDtypeStruct(one.shape, F32) for one in (w_down, w_in, w_out)),
+            tuple(jax.ShapeDtypeStruct(one.shape, F32) for one in (w_in, w_out)),
         )
         qkv_own = local_call(
-            late_out_kernel,
+            functools.partial(qkv_out_kernel, cut_vec),
             places,
-            late_parts,
+            early_parts + late_parts,
             jax.ShapeDtypeStruct((3, w_qkv.shape[0], WIDE), F32),
         )
         qkv_own = jnp.swapaxes(qkv_own, 0, 1)
-    vec_own = first_quarter(early_parts, vec_pad)
+    vec_own = first_quarter(early_parts, cut_out, vec_pad)
     vecs = [vec_own[i * share : (i + 1) * share] for i in range(6)]
     bias_in_own = vec_own[6 * share : 10 * share]
-    bias_own = first_quarter(late_parts, vec_pad)[: 2 * share].reshape(2, share)
+    bias_own = first_quarter(late_parts, depth, vec_pad)[: 2 * share].reshape(2, share)
     return (
         result,
         grad_input,

time: 385 us -> 410 us (1.065)
  the two profiles are of different devices: /device:TPU:0 before, /device:TPU:10 now
where the time goes in v2:
time: 410 us; the launch traced here: 404 us
  waiting for transfers between devices  106 us (26%)
  starting transfers between devices  83.9 us (20%)
  Pallas kernels  80.5 us (20%)
  matrix products  50.7 us (12%)
  local copies, waits for them, and re-layouts  46.7 us (11%)
  other arithmetic  34.4 us (8%)
    ppermute x42, waiting for transfers between devices, xor_swap(): return lax.ppermute(value, axis, [(i, i ^ mask) for i in range(count)])  84.5 us
    ppermute x42, starting transfers between devices, xor_swap(): return lax.ppermute(value, axis, [(i, i ^ mask) for i in range(count)])  60.7 us
    pallas_call x3, Pallas kernels, attend_backward(): pl.pallas_call(functools.partial(backward_kernel, blocks), out_shape=(jax...  34.2 us
    pallas_call x3, Pallas kernels, attend_forward(): pl.pallas_call(functools.partial(forward_kernel, blocks), out_shape=(jax....  31.1 us
    dot_general x9, matrix products, left_inner(): lax.dot_general(left_mat, right_mat, (((0,), (0,)), ((), ())), preferred_...  20.5 us
    dot_general x7, matrix products, right_inner(): lax.dot_general(left_mat, right_mat, (((1,), (1,)), ((), ())), preferred_...  20.1 us
    unnamed x170, local copies, waits for them, and re-layouts  15.8 us
    pallas_call x5, Pallas kernels, local_call(): pl.pallas_call(kernel, out_shape=outs, in_specs=[pl.BlockSpec(memory_spac...  15.2 us
  transfers between devices with their start and end apart: 63, of which 25 were waited for; matrix products, arithmetic and copies ran while one was open for 23% of the time, Pallas kernels for 19%

profile of v2, /device:TPU:10, one launch (start us, length us, event | category | flops | bytes accessed | tf_op | source)
XLA Modules:
  0.0 404.1 jit_solution(3574351071232675453)
XLA Ops:
  7.6 4.8 %concatenate.189 = bf16[960]{0:T(1024)(128)(2,1)S(1)} concatenate(bf16[96]{0:T(256)(128)(2,1)} %param.20, bf16[96]{0:T(256)(128)(2,1)} %param.21, bf16[96]{0:T(256)(128)(2,1)} %param.22, bf16[96]{0:T(256)(128)(2,1)} %param.26, bf16[96]{0:T(256)(128)(2,1)} %param.27, bf16[96]{0:T(256)(128)(2,1)} %param.28, bf16[384]{0:T(512)(128)(2,1)} %param.24), dimensions={0} | concatenate | bytes 3840 | tf_op jit(solution)/shard_map/concatenate | solution.py:571
  27.5 12.7 %collective-permute-done.12 = bf16[448,384]{1,0:T(8,128)(2,1)S(1)} collective-permute-done((bf16[448,384]{1,0:T(8,128)(2,1)S(1)}, bf16[448,384]{1,0:T(8,128)(2,1)S(1)}, u32[]{:S(2)}, u32[]{:S(2)}) %collective-permute-start.12) | collective-permute-done | bytes 344096 | tf_op jit(solution)/shard_map/ppermute | solution.py:70
  41.8 3.8 collective-permute-done.11
  68.1 11.5 %collective-permute-done.7.ko_ref.vo_ref = bf16[1024,256]{1,0:T(8,128)(2,1)S(1)} collective-permute-done((bf16[1024,256]{1,0:T(8,128)(2,1)S(1)}, bf16[1024,256]{1,0:T(8,128)(2,1)S(1)}, u32[]{:S(2)}, u32[]{:S(2)}) %collective-permute-start.7) | collective-permute-done | bytes 524320 | tf_op jit(solution)/shard_map/ppermute | solution.py:630
  81.6 10.6 %attend_forward.3 = (bf16[1024,128]{1,0:T(8,128)(2,1)}, f32[8,2048]{1,0:T(8,128)}) custom-call(s32[9]{0:T(128)} %pad_add_fusion.1.table, bf16[1024,1152]{1,0:T(8,128)(2,1)} %copy-done.2, bf16[1024,1152]{1,0:T(8,128)(2,1)} %copy-done.2, bf16[1024,1152]{1,0:T(8,128)(2,1)} %copy-done.2, bf16[1024,256]{1,0:T(8,128)(2,1)} %copy-done.21, ...), custom_call_target="tpu_custom_call" | custom-call | flops 2147483648 | bytes 1048576 | tf_op jit(solution)/shard_map/attend_forward/pallas_call | solution.py:433
  94.7 10.2 %attend_forward.4 = (bf16[1024,128]{1,0:T(8,128)(2,1)}, f32[8,2048]{1,0:T(8,128)}) custom-call(s32[9]{0:T(128)} %pad_add_fusion.1.table, bf16[1024,1152]{1,0:T(8,128)(2,1)} %copy-done.2, bf16[1024,1152]{1,0:T(8,128)(2,1)} %copy-done.2, bf16[1024,1152]{1,0:T(8,128)(2,1)} %copy-done.2, bf16[1024,256]{1,0:T(8,128)(2,1)} %copy-done.20, ...), custom_call_target="tpu_custom_call" | custom-call | flops 2147483648 | bytes 1048576 | tf_op jit(solution)/shard_map/attend_forward/pallas_call | solution.py:433
  107.4 10.2 %attend_forward.5 = (bf16[1024,128]{1,0:T(8,128)(2,1)}, f32[8,2048]{1,0:T(8,128)}) custom-call(s32[9]{0:T(128)} %pad_add_fusion.1.table, bf16[1024,1152]{1,0:T(8,128)(2,1)} %copy-done.2, bf16[1024,1152]{1,0:T(8,128)(2,1)} %copy-done.2, bf16[1024,1152]{1,0:T(8,128)(2,1)} %copy-done.2, bf16[1024,256]{1,0:T(8,128)(2,1)} %copy-done.22, ...), custom_call_target="tpu_custom_call" | custom-call | flops 2147483648 | bytes 1048576 | tf_op jit(solution)/shard_map/attend_forward/pallas_call | solution.py:433
  117.7 5.4 %shard_map.255 = (bf16[1536,768]{1,0:T(8,128)(2,1)}, bf16[768,1536]{1,0:T(8,128)(2,1)}, bf16[384,768]{1,0:T(8,128)(2,1)}) custom-call(s32[2]{0:T(128)} %pad_add_fusion.2.places, bf16[384,768]{1,0:T(8,128)(2,1)} %own_down.1, bf16[192,1536]{1,0:T(8,128)(2,1)} %own_in.1, bf16[96,768]{1,0:T(8,128)(2,1)} %own_out.1, bf16[3,432,384]{2,1,0:T(8,128)(2,1)} %copy-done.9, ...), custom_call_target="tpu_custom_call" | custom-call | bytes 4194304 | tf_op jit(solution)/shard_map/pallas_call | solution.py:147
  151.4 3.3 convert_reduce_fusion
  155.3 4.6 %multiply_reduce_fusion = (f32[768]{0:T(1024)S(1)}, f32[512]{0:T(512)S(1)}, f32[512]{0:T(512)S(1)}, f32[768]{0:T(1024)S(1)}, f32[512,768]{1,0:T(8,128)S(1)}) fusion(f32[512,768]{1,0:T(8,128)S(1)} %get-tuple-element.173, f32[512]{0:T(512)S(1)} %add_rsqrt_fusion.1, f32[512]{0:T(512)S(1)} %broadcast_multiply_fusion.5, f32[768]{0:T(1024)S(1)} %maximum_select_fusion.6, ...), kind=kOutput, calls=%fused_computation.66 | convolution fusion | flops 1212282368 | bytes 10241024 | tf_op jit(solution)/shard_map/dot_general | solution.py:37
  186.8 5.7 %collective-permute-start.54 = (bf16[4,192,384]{2,1,0:T(8,128)(2,1)}, bf16[4,192,384]{2,1,0:T(8,128)(2,1)}, u32[]{:S(2)}, u32[]{:S(2)}) collective-permute-start(bf16[4,192,384]{2,1,0:T(8,128)(2,1)} %get-tuple-element.97), channel_id=1, source_target_pairs={{0,8},{8,0},{16,24},{24,16},{1,9},{9,1},{17,25},{25,17},{2,10},{10... | collective-permute-start | bytes 1769480 | tf_op jit(solution)/shard_map/ppermute | solution.py:70
  198.0 11.3 %attend_backward.5 = (bf16[1024,128]{1,0:T(8,128)(2,1)}, f32[1024,128]{1,0:T(8,128)}, f32[1024,128]{1,0:T(8,128)}, bf16[1024,256]{1,0:T(8,128)(2,1)}) custom-call(s32[9]{0:T(128)} %pad_add_fusion.1.table, bf16[1024,1152]{1,0:T(8,128)(2,1)} %copy-done.2, bf16[1024,1152]{1,0:T(8,128)(2,1)} %copy-done.2, bf16[1024,1152]{1,0:T(8,128)(2,1)} %copy-done.2, ...), custom_call_target="tpu_custom_call" | custom-call | flops 5368709120 | bytes 2097152 | tf_op jit(solution)/shard_map/attend_backward/pallas_call | solution.py:460
  209.3 9.1 %collective-permute-start.30 = (bf16[1024,256]{1,0:T(8,128)(2,1)}, bf16[1024,256]{1,0:T(8,128)(2,1)}, u32[]{:S(2)}, u32[]{:S(2)}) collective-permute-start(bf16[1024,256]{1,0:T(8,128)(2,1)} %get-tuple-element.59), channel_id=1, source_target_pairs={{0,1},{1,0},{2,3},{3,2},{4,5},{5,4},{6,7},{7,6},{8,9},{9,8},{10,11... | collective-permute-start | bytes 1572872 | tf_op jit(solution)/shard_map/ppermute | solution.py:808
  218.4 11.6 %attend_backward.3 = (bf16[1024,128]{1,0:T(8,128)(2,1)}, f32[1024,128]{1,0:T(8,128)}, f32[1024,128]{1,0:T(8,128)}, bf16[1024,256]{1,0:T(8,128)(2,1)}) custom-call(s32[9]{0:T(128)} %pad_add_fusion.1.table, bf16[1024,1152]{1,0:T(8,128)(2,1)} %copy-done.2, bf16[1024,1152]{1,0:T(8,128)(2,1)} %copy-done.2, bf16[1024,1152]{1,0:T(8,128)(2,1)} %copy-done.2, ...), custom_call_target="tpu_custom_call" | custom-call | flops 5368709120 | bytes 2097152 | tf_op jit(solution)/shard_map/attend_backward/pallas_call | solution.py:460
  235.1 11.4 %attend_backward.4 = (bf16[1024,128]{1,0:T(8,128)(2,1)}, f32[1024,128]{1,0:T(8,128)}, f32[1024,128]{1,0:T(8,128)}, bf16[1024,256]{1,0:T(8,128)(2,1)}) custom-call(s32[9]{0:T(128)} %pad_add_fusion.1.table, bf16[1024,1152]{1,0:T(8,128)(2,1)} %copy-done.2, bf16[1024,1152]{1,0:T(8,128)(2,1)} %copy-done.2, bf16[1024,1152]{1,0:T(8,128)(2,1)} %copy-done.2, ...), custom_call_target="tpu_custom_call" | custom-call | flops 5368709120 | bytes 2097152 | tf_op jit(solution)/shard_map/attend_backward/pallas_call | solution.py:460
  253.0 8.3 %collective-permute-done.29 = bf16[1024,256]{1,0:T(8,128)(2,1)S(1)} collective-permute-done((bf16[1024,256]{1,0:T(8,128)(2,1)}, bf16[1024,256]{1,0:T(8,128)(2,1)S(1)}, u32[]{:S(2)}, u32[]{:S(2)}) %collective-permute-start.29) | collective-permute-done | bytes 524320 | tf_op jit(solution)/shard_map/ppermute | solution.py:808
  278.6 4.1 %fusion.127 = f32[1024,768]{1,0:T(8,128)S(1)} fusion(bf16[1024,1152]{1,0:T(8,128)(2,1)} %get-tuple-element.75, bf16[768,1152]{1,0:T(8,128)(2,1)S(1)} %copy-done.25), kind=kOutput, calls=%fused_computation.354 | convolution fusion | flops 1811939328 | bytes 7274496 | tf_op jit(solution)/shard_map/dot_general | solution.py:37
  288.1 14.8 %collective-permute-done.44 = bf16[4,64,384]{2,1,0:T(8,128)(2,1)S(1)} collective-permute-done((bf16[4,64,384]{2,1,0:T(8,128)(2,1)S(1)}, bf16[4,64,384]{2,1,0:T(8,128)(2,1)S(1)}, u32[]{:S(2)}, u32[]{:S(2)}) %collective-permute-start.44) | collective-permute-done | bytes 196640 | tf_op jit(solution)/shard_map/ppermute | solution.py:70
  311.4 6.1 %collective-permute-done.59 = bf16[192,384]{1,0:T(8,128)(2,1)S(1)} collective-permute-done((bf16[192,384]{1,0:T(8,128)(2,1)S(1)}, bf16[192,384]{1,0:T(8,128)(2,1)S(1)}, u32[]{:S(2)}, u32[]{:S(2)}) %collective-permute-start.59) | collective-permute-done | bytes 147488 | tf_op jit(solution)/shard_map/ppermute | solution.py:70
  332.1 4.5 %collective-permute-done.35 = bf16[4,96,384]{2,1,0:T(8,128)(2,1)S(1)} collective-permute-done((bf16[4,96,384]{2,1,0:T(8,128)(2,1)S(1)}, bf16[4,96,384]{2,1,0:T(8,128)(2,1)S(1)}, u32[]{:S(2)}, u32[]{:S(2)}) %collective-permute-start.35) | collective-permute-done | bytes 294944 | tf_op jit(solution)/shard_map/ppermute | solution.py:70
  336.6 9.2 %collective-permute-done.36 = bf16[4,96,384]{2,1,0:T(8,128)(2,1)S(1)} collective-permute-done((bf16[4,96,384]{2,1,0:T(8,128)(2,1)S(1)}, bf16[4,96,384]{2,1,0:T(8,128)(2,1)S(1)}, u32[]{:S(2)}, u32[]{:S(2)}) %collective-permute-start.36) | collective-permute-done | bytes 294944 | tf_op jit(solution)/shard_map/ppermute | solution.py:70
  373.2 7.1 %collective-permute-done.39 = bf16[352,384]{1,0:T(8,128)(2,1)S(1)} collective-permute-done((bf16[352,384]{1,0:T(8,128)(2,1)}, bf16[352,384]{1,0:T(8,128)(2,1)S(1)}, u32[]{:S(2)}, u32[]{:S(2)}) %collective-permute-start.39) | collective-permute-done | bytes 270368 | tf_op jit(solution)/shard_map/ppermute | solution.py:70
  380.3 4.5 %collective-permute-done.40 = bf16[352,384]{1,0:T(8,128)(2,1)S(1)} collective-permute-done((bf16[352,384]{1,0:T(8,128)(2,1)S(1)}, bf16[352,384]{1,0:T(8,128)(2,1)S(1)}, u32[]{:S(2)}, u32[]{:S(2)}) %collective-permute-start.40) | collective-permute-done | bytes 270368 | tf_op jit(solution)/shard_map/ppermute | solution.py:70
  388.6 3.7 fusion.18
  (488 shorter events, 213.5 us)
Async XLA Ops:
  15.2 25.1 %collective-permute-start.12 = (bf16[448,384]{1,0:T(8,128)(2,1)S(1)}, bf16[448,384]{1,0:T(8,128)(2,1)S(1)}, u32[]{:S(2)}, u32[]{:S(2)}) collective-permute-start(bf16[448,384]{1,0:T(8,128)(2,1)S(1)} %pad_maximum_fusion.4), channel_id=1, source_target_pairs={{0,3},{1,2},{2,1},{3,0},{4,7},{5,6},{6,5},{7,4},{8,11},{9,10},{10,... | collective-permute-start | bytes 1032200 | tf_op jit(solution)/shard_map/ppermute | solution.py:70
  16.7 28.9 %collective-permute-start.11 = (bf16[448,384]{1,0:T(8,128)(2,1)S(1)}, bf16[448,384]{1,0:T(8,128)(2,1)}, u32[]{:S(2)}, u32[]{:S(2)}) collective-permute-start(bf16[448,384]{1,0:T(8,128)(2,1)S(1)} %pad_maximum_fusion.4), channel_id=1, source_target_pairs={{0,2},{1,3},{2,0},{3,1},{4,6},{5,7},{6,4},{7,5},{8,10},{9,11},{10,... | collective-permute-start | bytes 1032200 | tf_op jit(solution)/shard_map/ppermute | solution.py:70
  22.0 24.9 %collective-permute-start.10 = (bf16[448,384]{1,0:T(8,128)(2,1)S(1)}, bf16[448,384]{1,0:T(8,128)(2,1)}, u32[]{:S(2)}, u32[]{:S(2)}) collective-permute-start(bf16[448,384]{1,0:T(8,128)(2,1)S(1)} %pad_maximum_fusion.4), channel_id=1, source_target_pairs={{0,1},{1,0},{2,3},{3,2},{4,5},{5,4},{6,7},{7,6},{8,9},{9,8},{10,11... | collective-permute-start | bytes 1032200 | tf_op jit(solution)/shard_map/ppermute | solution.py:70
  23.2 35.0 %collective-permute-start = (bf16[1024,384]{1,0:T(8,128)(2,1)S(1)}, bf16[1024,384]{1,0:T(8,128)(2,1)S(1)}, u32[]{:S(2)}, u32[]{:S(2)}) collective-permute-start(bf16[1024,384]{1,0:T(8,128)(2,1)S(1)} %copy-done.43), channel_id=1, source_target_pairs={{0,4},{4,0},{1,5},{5,1},{2,6},{6,2},{3,7},{7,3},{8,12},{12,8},{9,1... | collective-permute-start | bytes 2359304 | tf_op jit(solution)/shard_map/ppermute | solution.py:43
  26.0 27.1 %collective-permute-start.6 = (bf16[3,144,384]{2,1,0:T(8,128)(2,1)S(1)}, bf16[3,144,384]{2,1,0:T(8,128)(2,1)}, u32[]{:S(2)}, u32[]{:S(2)}) collective-permute-start(bf16[3,144,384]{2,1,0:T(8,128)(2,1)S(1)} %pad_maximum_fusion.5.refs_0_), channel_id=1, source_target_pairs={{0,24},{8,16},{16,8},{24,0},{1,25},{9,17},{17,9},{25,1},{2,26},{10... | collective-permute-start | bytes 995336 | tf_op jit(solution)/shard_map/ppermute | solution.py:70
  50.6 67.1 %collective-permute-start.15 = (bf16[3,432,384]{2,1,0:T(8,128)(2,1)S(1)}, bf16[3,432,384]{2,1,0:T(8,128)(2,1)}, u32[]{:S(2)}, u32[]{:S(2)}) collective-permute-start(bf16[3,432,384]{2,1,0:T(8,128)(2,1)S(1)} %pad_maximum_fusion.refs_0_), channel_id=1, source_target_pairs={{0,24},{8,16},{16,8},{24,0},{1,25},{9,17},{17,9},{25,1},{2,26},{10... | collective-permute-start | bytes 2985992 | tf_op jit(solution)/shard_map/ppermute | solution.py:70
  53.1 64.6 %collective-permute-start.14 = (bf16[3,432,384]{2,1,0:T(8,128)(2,1)S(1)}, bf16[3,432,384]{2,1,0:T(8,128)(2,1)}, u32[]{:S(2)}, u32[]{:S(2)}) collective-permute-start(bf16[3,432,384]{2,1,0:T(8,128)(2,1)S(1)} %pad_maximum_fusion.refs_0_), channel_id=1, source_target_pairs={{0,16},{8,24},{16,0},{24,8},{1,17},{9,25},{17,1},{25,9},{2,18},{10... | collective-permute-start | bytes 2985992 | tf_op jit(solution)/shard_map/ppermute | solution.py:70
  53.6 64.1 %collective-permute-start.13 = (bf16[3,432,384]{2,1,0:T(8,128)(2,1)S(1)}, bf16[3,432,384]{2,1,0:T(8,128)(2,1)}, u32[]{:S(2)}, u32[]{:S(2)}) collective-permute-start(bf16[3,432,384]{2,1,0:T(8,128)(2,1)S(1)} %pad_maximum_fusion.refs_0_), channel_id=1, source_target_pairs={{0,8},{8,0},{16,24},{24,16},{1,9},{9,1},{17,25},{25,17},{2,10},{10... | collective-permute-start | bytes 2985992 | tf_op jit(solution)/shard_map/ppermute | solution.py:70
  67.0 26.9 %collective-permute-start.8 = (bf16[1024,256]{1,0:T(8,128)(2,1)}, bf16[1024,256]{1,0:T(8,128)(2,1)S(1)}, u32[]{:S(2)}, u32[]{:S(2)}) collective-permute-start(bf16[1024,256]{1,0:T(8,128)(2,1)} %get-tuple-element.103), channel_id=1, source_target_pairs={{1,0},{0,1},{3,2},{2,3},{5,4},{4,5},{7,6},{6,7},{9,8},{8,9},{11,10... | collective-permute-start | bytes 1572872 | tf_op jit(solution)/shard_map/ppermute | solution.py:630
  79.6 27.1 %collective-permute-start.9 = (bf16[1024,256]{1,0:T(8,128)(2,1)S(1)}, bf16[1024,256]{1,0:T(8,128)(2,1)S(1)}, u32[]{:S(2)}, u32[]{:S(2)}) collective-permute-start(bf16[1024,256]{1,0:T(8,128)(2,1)S(1)} %get-tuple-element.102), channel_id=1, source_target_pairs={{1,0},{0,1},{3,2},{2,3},{5,4},{4,5},{7,6},{6,7},{9,8},{8,9},{11,10... | collective-permute-start | bytes 1572872 | tf_op jit(solution)/shard_map/ppermute | solution.py:630
  93.9 44.1 %collective-permute-start.22 = (bf16[512,384]{1,0:T(8,128)(2,1)}, bf16[512,384]{1,0:T(8,128)(2,1)S(1)}, u32[]{:S(2)}, u32[]{:S(2)}) collective-permute-start(bf16[512,384]{1,0:T(8,128)(2,1)} %get-tuple-element.118), channel_id=1, source_target_pairs={{0,4},{4,0},{1,5},{5,1},{2,6},{6,2},{3,7},{7,3},{8,12},{12,8},{9,1... | collective-permute-start | bytes 1179656 | tf_op jit(solution)/shard_map/ppermute | solution.py:43
  169.6 24.3 %collective-permute-start.24 = (bf16[768,1536]{1,0:T(8,128)(2,1)}, bf16[768,1536]{1,0:T(8,128)(2,1)}, u32[]{:S(2)}, u32[]{:S(2)}) collective-permute-start(bf16[768,1536]{1,0:T(8,128)(2,1)} %convolution_convert_fusion.1), channel_id=1, source_target_pairs={{0,4},{4,0},{1,5},{5,1},{2,6},{6,2},{3,7},{7,3},{8,12},{12,8},{9,1... | collective-permute-start | bytes 7077896 | tf_op jit(solution)/shard_map/ppermute | solution.py:43
  186.8 95.9 %collective-permute-start.54 = (bf16[4,192,384]{2,1,0:T(8,128)(2,1)}, bf16[4,192,384]{2,1,0:T(8,128)(2,1)}, u32[]{:S(2)}, u32[]{:S(2)}) collective-permute-start(bf16[4,192,384]{2,1,0:T(8,128)(2,1)} %get-tuple-element.97), channel_id=1, source_target_pairs={{0,8},{8,0},{16,24},{24,16},{1,9},{9,1},{17,25},{25,17},{2,10},{10... | collective-permute-start | bytes 1769480 | tf_op jit(solution)/shard_map/ppermute | solution.py:70
  192.5 90.5 %collective-permute-start.55 = (bf16[4,192,384]{2,1,0:T(8,128)(2,1)}, bf16[4,192,384]{2,1,0:T(8,128)(2,1)}, u32[]{:S(2)}, u32[]{:S(2)}) collective-permute-start(bf16[4,192,384]{2,1,0:T(8,128)(2,1)} %get-tuple-element.98), channel_id=1, source_target_pairs={{0,16},{8,24},{16,0},{24,8},{1,17},{9,25},{17,1},{25,9},{2,18},{10... | collective-permute-start | bytes 1769480 | tf_op jit(solution)/shard_map/ppermute | solution.py:70
  192.5 91.0 %collective-permute-start.56 = (bf16[4,192,384]{2,1,0:T(8,128)(2,1)}, bf16[4,192,384]{2,1,0:T(8,128)(2,1)}, u32[]{:S(2)}, u32[]{:S(2)}) collective-permute-start(bf16[4,192,384]{2,1,0:T(8,128)(2,1)} %get-tuple-element.99), channel_id=1, source_target_pairs={{0,24},{8,16},{16,8},{24,0},{1,25},{9,17},{17,9},{25,1},{2,26},{10... | collective-permute-start | bytes 1769480 | tf_op jit(solution)/shard_map/ppermute | solution.py:70
  209.3 54.6 %collective-permute-start.30 = (bf16[1024,256]{1,0:T(8,128)(2,1)}, bf16[1024,256]{1,0:T(8,128)(2,1)}, u32[]{:S(2)}, u32[]{:S(2)}) collective-permute-start(bf16[1024,256]{1,0:T(8,128)(2,1)} %get-tuple-element.59), channel_id=1, source_target_pairs={{0,1},{1,0},{2,3},{3,2},{4,5},{5,4},{6,7},{7,6},{8,9},{9,8},{10,11... | collective-permute-start | bytes 1572872 | tf_op jit(solution)/shard_map/ppermute | solution.py:808
  261.2 65.4 %collective-permute-start.32 = (bf16[4,256,384]{2,1,0:T(8,128)(2,1)}, bf16[4,256,384]{2,1,0:T(8,128)(2,1)}, u32[]{:S(2)}, u32[]{:S(2)}) collective-permute-start(bf16[4,256,384]{2,1,0:T(8,128)(2,1)} %get-tuple-element.94), channel_id=1, source_target_pairs={{0,8},{8,0},{16,24},{24,16},{1,9},{9,1},{17,25},{25,17},{2,10},{10... | collective-permute-start | bytes 2359304 | tf_op jit(solution)/shard_map/ppermute | solution.py:70
  263.9 63.1 %collective-permute-start.34 = (bf16[4,256,384]{2,1,0:T(8,128)(2,1)}, bf16[4,256,384]{2,1,0:T(8,128)(2,1)}, u32[]{:S(2)}, u32[]{:S(2)}) collective-permute-start(bf16[4,256,384]{2,1,0:T(8,128)(2,1)} %get-tuple-element.95), channel_id=1, source_target_pairs={{0,24},{8,16},{16,8},{24,0},{1,25},{9,17},{17,9},{25,1},{2,26},{10... | collective-permute-start | bytes 2359304 | tf_op jit(solution)/shard_map/ppermute | solution.py:70
  282.7 20.2 %collective-permute-start.44 = (bf16[4,64,384]{2,1,0:T(8,128)(2,1)S(1)}, bf16[4,64,384]{2,1,0:T(8,128)(2,1)S(1)}, u32[]{:S(2)}, u32[]{:S(2)}) collective-permute-start(bf16[4,64,384]{2,1,0:T(8,128)(2,1)S(1)} %get-tuple-element.114), channel_id=1, source_target_pairs={{0,8},{8,0},{16,24},{24,16},{1,9},{9,1},{17,25},{25,17},{2,10},{10... | collective-permute-start | bytes 589832 | tf_op jit(solution)/shard_map/ppermute | solution.py:70
  282.9 21.6 %collective-permute-start.45 = (bf16[4,64,384]{2,1,0:T(8,128)(2,1)S(1)}, bf16[4,64,384]{2,1,0:T(8,128)(2,1)S(1)}, u32[]{:S(2)}, u32[]{:S(2)}) collective-permute-start(bf16[4,64,384]{2,1,0:T(8,128)(2,1)S(1)} %get-tuple-element.115), channel_id=1, source_target_pairs={{0,16},{8,24},{16,0},{24,8},{1,17},{9,25},{17,1},{25,9},{2,18},{10... | collective-permute-start | bytes 589832 | tf_op jit(solution)/shard_map/ppermute | solution.py:70
  283.4 22.7 %collective-permute-start.46 = (bf16[4,64,384]{2,1,0:T(8,128)(2,1)S(1)}, bf16[4,64,384]{2,1,0:T(8,128)(2,1)S(1)}, u32[]{:S(2)}, u32[]{:S(2)}) collective-permute-start(bf16[4,64,384]{2,1,0:T(8,128)(2,1)S(1)} %get-tuple-element.116), channel_id=1, source_target_pairs={{0,24},{8,16},{16,8},{24,0},{1,25},{9,17},{17,9},{25,1},{2,26},{10... | collective-permute-start | bytes 589832 | tf_op jit(solution)/shard_map/ppermute | solution.py:70
  324.3 64.2 %collective-permute-start.23 = (f32[512,384]{1,0:T(8,128)}, f32[512,384]{1,0:T(8,128)}, u32[]{:S(2)}, u32[]{:S(2)}) collective-permute-start(f32[512,384]{1,0:T(8,128)} %get-tuple-element.107), channel_id=1, source_target_pairs={{0,4},{4,0},{1,5},{5,1},{2,6},{6,2},{3,7},{7,3},{8,12},{12,8},{9,1... | collective-permute-start | bytes 2359304 | tf_op jit(solution)/shard_map/ppermute | solution.py:43
  326.6 61.9 %collective-permute-start.31 = (bf16[1024,384]{1,0:T(8,128)(2,1)}, bf16[1024,384]{1,0:T(8,128)(2,1)}, u32[]{:S(2)}, u32[]{:S(2)}) collective-permute-start(bf16[1024,384]{1,0:T(8,128)(2,1)} %dynamic-slice_convert_fusion), channel_id=1, source_target_pairs={{0,4},{4,0},{1,5},{5,1},{2,6},{6,2},{3,7},{7,3},{8,12},{12,8},{9,1... | collective-permute-start | bytes 2359304 | tf_op jit(solution)/shard_map/ppermute | solution.py:43
  336.6 25.0 %collective-permute-start.62 = (bf16[192,384]{1,0:T(8,128)(2,1)S(1)}, bf16[192,384]{1,0:T(8,128)(2,1)S(1)}, u32[]{:S(2)}, u32[]{:S(2)}) collective-permute-start(bf16[192,384]{1,0:T(8,128)(2,1)S(1)} %fusion.65.refs_0_), channel_id=1, source_target_pairs={{0,24},{8,16},{16,8},{24,0},{1,25},{9,17},{17,9},{25,1},{2,26},{10... | collective-permute-start | bytes 442376 | tf_op jit(solution)/shard_map/ppermute | solution.py:70
  (118 other events, 1048.6 us)

commit v3 on v2

--- a/solution.py
+++ b/solution.py
@@ -345,12 +345,46 @@
         )
 
 
-def backward_kernel(
+def backward_block(blocks, rows, at, refs, key_at, spans_of_keys, before):
+    q_ref, span_ref, out_ref, log_ref, grad_ref, keys, values, key_sum, value_sum = refs
+    block = rows // blocks
+    here = pl.ds(pl.multiple_of(at * block, block), block)
+    wide = pl.ds(pl.multiple_of(at * 2 * block, 2 * block), 2 * block)
+    query = stack_heads((q_ref[here, :].astype(F32) * 0.125).astype(BF))
+    grad = stack_heads(grad_ref[here, :])
+    along = (grad_ref[here, :].astype(F32) * out_ref[here, :].astype(F32)).T
+    dots = jnp.concatenate(
+        [
+            jnp.sum(along[:HD], axis=0, keepdims=True),
+            jnp.sum(along[HD:], axis=0, keepdims=True),
+        ],
+        axis=1,
+    )
+    logs = log_ref[0:1, wide]
+    first_key = span_ref[0:1, here]
+    past_key = span_ref[1:2, here]
+
+    def step(place, summed):
+        rows_at = pl.ds(pl.multiple_of(key_at(place) * KEY_BLOCK, KEY_BLOCK), KEY_BLOCK)
+        key = keys[rows_at, :]
+        scores = right_inner(key, query)
+        scores = scores + mask_bias(place * KEY_BLOCK, first_key, past_key)
+        weights = jnp.exp(scores - logs)
+        grad_weights = right_inner(values[rows_at, :], grad)
+        value_sum[rows_at, :] += matmul(weights.astype(BF), grad)
+        grad_scores = (weights * (grad_weights - dots)).astype(BF)
+        key_sum[rows_at, :] += matmul(grad_scores, query)
+        return summed + left_inner(key, grad_scores)
+
+    for low, high in spans_of_keys:
+        before = lax.fori_loop(low, high, step, before)
+    return here, before
+
+
+def backward_others_kernel(
     blocks,
     table,
     q_ref,
-    k_ref,
-    v_ref,
     ko_ref,
     vo_ref,
     span_ref,
@@ -358,63 +392,72 @@
     log_ref,
     grad_ref,
     dq_ref,
-    dk_ref,
-    dv_ref,
     others_ref,
-    keys,
-    values,
     key_sum,
     value_sum,
 ):
     rows = q_ref.shape[0]
     block = rows // blocks
-    copy_blocks(keys, k_ref, ko_ref, rows)
-    copy_blocks(values, v_ref, vo_ref, rows)
-    slots = keys.shape[0] // KEY_BLOCK
+    own = rows // KEY_BLOCK
+    slots = own + ko_ref.shape[0] // KEY_BLOCK
     base = table[2 * blocks]
     key_sum[...] = jnp.zeros_like(key_sum)
     value_sum[...] = jnp.zeros_like(value_sum)
+    refs = (q_ref, span_ref, out_ref, log_ref, grad_ref, ko_ref, vo_ref, key_sum, value_sum)
+
+    def key_at(place):
+        return lax.rem(place - base + slots, slots) - own
 
     @pl.loop(0, blocks)
     def _(at):
-        here = pl.ds(pl.multiple_of(at * block, block), block)
-        wide = pl.ds(pl.multiple_of(at * 2 * block, 2 * block), 2 * block)
-        query = stack_heads((q_ref[here, :].astype(F32) * 0.125).astype(BF))
-        grad = stack_heads(grad_ref[here, :])
-        along = (grad_ref[here, :].astype(F32) * out_ref[here, :].astype(F32)).T
-        dots = jnp.concatenate(
-            [
-                jnp.sum(along[:HD], axis=0, keepdims=True),
-                jnp.sum(along[HD:], axis=0, keepdims=True),
-            ],
-            axis=1,
-        )
-        logs = log_ref[0:1, wide]
-        first_key = span_ref[0:1, here]
-        past_key = span_ref[1:2, here]
-
-        def step(place, summed):
-            slot = lax.rem(place - base + slots, slots)
-            rows_at = pl.ds(pl.multiple_of(slot * KEY_BLOCK, KEY_BLOCK), KEY_BLOCK)
-            key = keys[rows_at, :]
-            scores = right_inner(key, query)
-            scores = scores + mask_bias(place * KEY_BLOCK, first_key, past_key)
-            weights = jnp.exp(scores - logs)
-            grad_weights = right_inner(values[rows_at, :], grad)
-            value_sum[rows_at, :] += matmul(weights.astype(BF), grad)
-            grad_scores = (weights * (grad_weights - dots)).astype(BF)
-            key_sum[rows_at, :] += matmul(grad_scores, query)
-            return summed + left_inner(key, grad_scores)
-
-        summed = lax.fori_loop(
-            table[at], table[blocks + at], step, jnp.zeros((LANES, 2 * block), F32)
-        )
-        dq_ref[here, :] = (join_heads(summed, block) * 0.125).astype(BF)
-
-    dk_ref[...] = key_sum[:rows, :]
-    dv_ref[...] = value_sum[:rows, :]
-    others_ref[:, :LANES] = key_sum[rows:, :].astype(BF)
-    others_ref[:, LANES:] = value_sum[rows:, :].astype(BF)
+        low, high = table[at], table[blocks + at]
+        ranges = ((low, jnp.minimum(high, base)), (jnp.maximum(low, base + own), high))
+        here, summed = backward_block(
+            blocks, rows, at, refs, key_at, ranges, jnp.zeros((LANES, 2 * block), F32)
+        )
+        dq_ref[here, :] = join_heads(summed, block)
+
+    others_ref[:, :LANES] = key_sum[...].astype(BF)
+    others_ref[:, LANES:] = value_sum[...].astype(BF)
+
+
+def backward_own_kernel(
+    blocks,
+    table,
+    q_ref,
+    k_ref,
+    v_ref,
+    span_ref,
+    out_ref,
+    log_ref,
+    grad_ref,
+    part_ref,
+    dq_ref,
+    dk_ref,
+    dv_ref,
+):
+    rows = q_ref.shape[0]
+    block = rows // blocks
+    own = rows // KEY_BLOCK
+    base = table[2 * blocks]
+    dk_ref[...] = jnp.zeros_like(dk_ref)
+    dv_ref[...] = jnp.zeros_like(dv_ref)
+    refs = (q_ref, span_ref, out_ref, log_ref, grad_ref, k_ref, v_ref, dk_ref, dv_ref)
+
+    @pl.loop(0, blocks)
+    def _(at):
+        low, high = table[at], table[blocks + at]
+        ranges = ((jnp.maximum(low, base), jnp.minimum(high, base + own)),)
+        here, summed = backward_block(
+            blocks,
+            rows,
+            at,
+            refs,
+            lambda place: place - base,
+            ranges,
+            jnp.zeros((LANES, 2 * block), F32),
+        )
+        dq_ref[here, :] = ((part_ref[here, :] + join_heads(summed, block)) * 0.125).astype(BF)
 
 
 def attention_specs(rows, others, pair):
@@ -453,37 +496,64 @@
     )(table, qkv, qkv, qkv, kv_others, kv_others, spans)
 
 
-def attend_backward(table, qkv, kv_others, spans, out, logs, grad, blocks, pair):
+def backward_call(kernel, table, inputs, in_specs, outs, out_specs, scratch, rows):
+    return pl.pallas_call(
+        kernel,
+        out_shape=outs,
+        grid_spec=pltpu.PrefetchScalarGridSpec(
+            num_scalar_prefetch=1,
+            grid=(1,),
+            in_specs=in_specs,
+            out_specs=out_specs,
+            scratch_shapes=scratch,
+        ),
+        cost_estimate=pl.CostEstimate(
+            flops=10 * rows * LEN * LANES, bytes_accessed=16 * rows * LANES, transcendentals=0
+        ),
+    )(table, *inputs)
+
+
+def attend_backward_others(table, qkv, kv_others, spans, out, logs, grad, blocks, pair):
     rows, others = qkv.shape[0], kv_others.shape[0]
+    specs = attention_specs(rows, others, pair)
     whole = pl.BlockSpec((rows, LANES), lambda g, t: (0, 0))
     mine = pl.BlockSpec((rows, LANES), lambda g, t: (0, pair))
-    return pl.pallas_call(
-        functools.partial(backward_kernel, blocks),
-        out_shape=(
+    logs_spec = pl.BlockSpec((8, 2 * rows), lambda g, t: (0, 0))
+    return backward_call(
+        functools.partial(backward_others_kernel, blocks),
+        table,
+        (qkv, kv_others, kv_others, spans, out, logs, grad),
+        [specs[0]] + specs[3:] + [whole, logs_spec, mine],
+        (
+            jax.ShapeDtypeStruct((rows, LANES), F32),
+            jax.ShapeDtypeStruct((others, 2 * LANES), BF),
+        ),
+        (whole, pl.BlockSpec((others, 2 * LANES), lambda g, t: (0, 0))),
+        [pltpu.VMEM((others, LANES), F32)] * 2,
+        rows,
+    )
+
+
+def attend_backward_own(table, qkv, spans, out, logs, grad, part, blocks, pair):
+    rows = qkv.shape[0]
+    specs = attention_specs(rows, rows, pair)
+    whole = pl.BlockSpec((rows, LANES), lambda g, t: (0, 0))
+    mine = pl.BlockSpec((rows, LANES), lambda g, t: (0, pair))
+    logs_spec = pl.BlockSpec((8, 2 * rows), lambda g, t: (0, 0))
+    return backward_call(
+        functools.partial(backward_own_kernel, blocks),
+        table,
+        (qkv, qkv, qkv, spans, out, logs, grad, part),
+        specs[:3] + [specs[5], whole, logs_spec, mine, whole],
+        (
             jax.ShapeDtypeStruct((rows, LANES), BF),
             jax.ShapeDtypeStruct((rows, LANES), F32),
             jax.ShapeDtypeStruct((rows, LANES), F32),
-            jax.ShapeDtypeStruct((others, 2 * LANES), BF),
         ),
-        grid_spec=pltpu.PrefetchScalarGridSpec(
-            num_scalar_prefetch=1,
-            grid=(1,),
-            in_specs=attention_specs(rows, others, pair)
-            + [whole, pl.BlockSpec((8, 2 * rows), lambda g, t: (0, 0)), mine],
-            out_specs=(
-                whole,
-                whole,
-                whole,
-                pl.BlockSpec((others, 2 * LANES), lambda g, t: (0, 0)),
-            ),
-            scratch_shapes=[pltpu.VMEM((rows + others, LANES), BF)] * 2
-            + [pltpu.VMEM((rows + others, LANES), F32)] * 2,
-        ),
-        cost_estimate=pl.CostEstimate(
-            flops=20 * rows * LEN * LANES, bytes_accessed=16 * rows * LANES, transcendentals=0
-        ),
-        name="attend_backward",
-    )(table, qkv, qkv, qkv, kv_others, kv_others, spans, out, logs, grad)
+        (whole, whole, whole),
+        [],
+        rows,
+    )
 
 
 def norm_forward(summed, gain_vec, shift_vec):
@@ -798,11 +868,21 @@
     early_dp = reduce_dp(early)
     down_parts = spread_dp(reduce_col(down_dp))
 
+    first_pass = []
+    for pair in range(PAIRS):
+        out, logs = attended[pair]
+        first_pass.append(
+            attend_backward_others(
+                table, qkv_low, kv_others[pair], spans, out, logs, grad_attended, blocks, pair
+            )
+        )
+    query_parts = lax.optimization_barrier(tuple(part for part, _ in first_pass))
     grad_pairs, grad_w_pairs, bias_sums = [], [], []
     for pair in range(PAIRS):
         out, logs = attended[pair]
-        grad_query, key_own, value_own, others = attend_backward(
-            table, qkv_low, kv_others[pair], spans, out, logs, grad_attended, blocks, pair
+        others = first_pass[pair][1]
+        grad_query, key_own, value_own = attend_backward_own(
+            table, qkv_low, spans, out, logs, grad_attended, query_parts[pair], blocks, pair
         )
         for j in range(1, group):
             arrived = lax.ppermute(

time: 410 us -> 414 us (level)
  Pallas kernels: 80.5 us -> 91.4 us
  waiting for transfers between devices: 106 us -> 101 us
    pallas_call x3 -> x6, Pallas kernels: 34.2 us -> 45.1 us  [backward_call(): pl.pallas_call(kernel, out_shape=outs, grid_spec=pltpu.PrefetchScalarGrid...]
    ppermute x42, starting transfers between devices: 60.7 us -> 55.6 us  [xor_swap(): return lax.ppermute(value, axis, [(i, i ^ mask) for i in range(count)])]
    ppermute x3, waiting for transfers between devices: 8.26 us -> 4.1 us  [body(): lax.ppermute(others[(j - 1) * rows:j * rows], 'col', group_perm(j, True))]
  transfers between devices with their start and end apart: 63 -> 63, of which waited for: 25 -> 24; matrix products, arithmetic and copies ran while one was open for 23% -> 23% of each run, Pallas kernels for 19% -> 21%
where the time goes in v3:
time: 414 us; the launch traced here: 407 us
  waiting for transfers between devices  101 us (24%)
  Pallas kernels  91.4 us (22%)
  starting transfers between devices  80.9 us (20%)
  matrix products  50.7 us (12%)
  local copies, waits for them, and re-layouts  46.6 us (11%)
  other arithmetic  34.4 us (8%)
    ppermute x42, waiting for transfers between devices, xor_swap(): return lax.ppermute(value, axis, [(i, i ^ mask) for i in range(count)])  84.2 us
    ppermute x42, starting transfers between devices, xor_swap(): return lax.ppermute(value, axis, [(i, i ^ mask) for i in range(count)])  55.6 us
    pallas_call x6, Pallas kernels, backward_call(): pl.pallas_call(kernel, out_shape=outs, grid_spec=pltpu.PrefetchScalarGrid...  45.1 us
    pallas_call x3, Pallas kernels, attend_forward(): pl.pallas_call(functools.partial(forward_kernel, blocks), out_shape=(jax....  31.1 us
    dot_general x9, matrix products, left_inner(): lax.dot_general(left_mat, right_mat, (((0,), (0,)), ((), ())), preferred_...  20.5 us
    dot_general x7, matrix products, right_inner(): lax.dot_general(left_mat, right_mat, (((1,), (1,)), ((), ())), preferred_...  20 us
    ppermute x3, starting transfers between devices, body(): lax.ppermute(others[(j - 1) * rows:j * rows], 'col', group_perm(j, True))  17.1 us
    unnamed x170, local copies, waits for them, and re-layouts  15.7 us
  transfers between devices with their start and end apart: 63, of which 24 were waited for; matrix products, arithmetic and copies ran while one was open for 23% of the time, Pallas kernels for 21%

profile of v3, /device:TPU:10, one launch (start us, length us, event | category | flops | bytes accessed | tf_op | source)
XLA Modules:
  0.0 407.4 jit_solution(6278000481289935471)
XLA Ops:
  7.6 4.8 %concatenate.189 = bf16[960]{0:T(1024)(128)(2,1)S(1)} concatenate(bf16[96]{0:T(256)(128)(2,1)} %param.20, bf16[96]{0:T(256)(128)(2,1)} %param.21, bf16[96]{0:T(256)(128)(2,1)} %param.22, bf16[96]{0:T(256)(128)(2,1)} %param.26, bf16[96]{0:T(256)(128)(2,1)} %param.27, bf16[96]{0:T(256)(128)(2,1)} %param.28, bf16[384]{0:T(512)(128)(2,1)} %param.24), dimensions={0} | concatenate | bytes 3840 | tf_op jit(solution)/shard_map/concatenate | solution.py:641
  27.5 12.8 %collective-permute-done.12 = bf16[448,384]{1,0:T(8,128)(2,1)S(1)} collective-permute-done((bf16[448,384]{1,0:T(8,128)(2,1)S(1)}, bf16[448,384]{1,0:T(8,128)(2,1)S(1)}, u32[]{:S(2)}, u32[]{:S(2)}) %collective-permute-start.12) | collective-permute-done | bytes 344096 | tf_op jit(solution)/shard_map/ppermute | solution.py:70
  68.1 11.5 %collective-permute-done.7.ko_ref.vo_ref = bf16[1024,256]{1,0:T(8,128)(2,1)S(1)} collective-permute-done((bf16[1024,256]{1,0:T(8,128)(2,1)S(1)}, bf16[1024,256]{1,0:T(8,128)(2,1)S(1)}, u32[]{:S(2)}, u32[]{:S(2)}) %collective-permute-start.7) | collective-permute-done | bytes 524320 | tf_op jit(solution)/shard_map/ppermute | solution.py:700
  81.6 10.6 %attend_forward.3 = (bf16[1024,128]{1,0:T(8,128)(2,1)}, f32[8,2048]{1,0:T(8,128)}) custom-call(s32[9]{0:T(128)} %pad_add_fusion.1.table, bf16[1024,1152]{1,0:T(8,128)(2,1)} %copy-done.2, bf16[1024,1152]{1,0:T(8,128)(2,1)} %copy-done.2, bf16[1024,1152]{1,0:T(8,128)(2,1)} %copy-done.2, bf16[1024,256]{1,0:T(8,128)(2,1)} %copy-done.20, ...), custom_call_target="tpu_custom_call" | custom-call | flops 2147483648 | bytes 1048576 | tf_op jit(solution)/shard_map/attend_forward/pallas_call | solution.py:476
  94.7 10.2 %attend_forward.4 = (bf16[1024,128]{1,0:T(8,128)(2,1)}, f32[8,2048]{1,0:T(8,128)}) custom-call(s32[9]{0:T(128)} %pad_add_fusion.1.table, bf16[1024,1152]{1,0:T(8,128)(2,1)} %copy-done.2, bf16[1024,1152]{1,0:T(8,128)(2,1)} %copy-done.2, bf16[1024,1152]{1,0:T(8,128)(2,1)} %copy-done.2, bf16[1024,256]{1,0:T(8,128)(2,1)} %copy-done.21, ...), custom_call_target="tpu_custom_call" | custom-call | flops 2147483648 | bytes 1048576 | tf_op jit(solution)/shard_map/attend_forward/pallas_call | solution.py:476
  107.4 10.2 %attend_forward.5 = (bf16[1024,128]{1,0:T(8,128)(2,1)}, f32[8,2048]{1,0:T(8,128)}) custom-call(s32[9]{0:T(128)} %pad_add_fusion.1.table, bf16[1024,1152]{1,0:T(8,128)(2,1)} %copy-done.2, bf16[1024,1152]{1,0:T(8,128)(2,1)} %copy-done.2, bf16[1024,1152]{1,0:T(8,128)(2,1)} %copy-done.2, bf16[1024,256]{1,0:T(8,128)(2,1)} %copy-done.22, ...), custom_call_target="tpu_custom_call" | custom-call | flops 2147483648 | bytes 1048576 | tf_op jit(solution)/shard_map/attend_forward/pallas_call | solution.py:476
  117.7 5.4 %shard_map.255 = (bf16[1536,768]{1,0:T(8,128)(2,1)}, bf16[768,1536]{1,0:T(8,128)(2,1)}, bf16[384,768]{1,0:T(8,128)(2,1)}) custom-call(s32[2]{0:T(128)} %pad_add_fusion.2.places, bf16[384,768]{1,0:T(8,128)(2,1)} %own_down.1, bf16[192,1536]{1,0:T(8,128)(2,1)} %own_in.1, bf16[96,768]{1,0:T(8,128)(2,1)} %own_out.1, bf16[3,432,384]{2,1,0:T(8,128)(2,1)} %copy-done.9, ...), custom_call_target="tpu_custom_call" | custom-call | bytes 4194304 | tf_op jit(solution)/shard_map/pallas_call | solution.py:147
  155.3 4.6 %multiply_reduce_fusion = (f32[768]{0:T(1024)S(1)}, f32[512]{0:T(512)S(1)}, f32[512]{0:T(512)S(1)}, f32[768]{0:T(1024)S(1)}, f32[512,768]{1,0:T(8,128)S(1)}) fusion(f32[512,768]{1,0:T(8,128)S(1)} %get-tuple-element.185, f32[512]{0:T(512)S(1)} %add_rsqrt_fusion.1, f32[512]{0:T(512)S(1)} %broadcast_multiply_fusion.5, f32[768]{0:T(1024)S(1)} %maximum_select_fusion.6, ...), kind=kOutput, calls=%fused_computation.66 | convolution fusion | flops 1212282368 | bytes 10241024 | tf_op jit(solution)/shard_map/dot_general | solution.py:37
  186.8 5.6 %collective-permute-start.54 = (bf16[4,192,384]{2,1,0:T(8,128)(2,1)}, bf16[4,192,384]{2,1,0:T(8,128)(2,1)}, u32[]{:S(2)}, u32[]{:S(2)}) collective-permute-start(bf16[4,192,384]{2,1,0:T(8,128)(2,1)} %get-tuple-element.109), channel_id=1, source_target_pairs={{0,8},{8,0},{16,24},{24,16},{1,9},{9,1},{17,25},{25,17},{2,10},{10... | collective-permute-start | bytes 1769480 | tf_op jit(solution)/shard_map/ppermute | solution.py:70
  197.9 5.9 %shard_map.258 = (f32[1024,128]{1,0:T(8,128)}, bf16[1024,256]{1,0:T(8,128)(2,1)}) custom-call(s32[9]{0:T(128)} %pad_add_fusion.1.table, bf16[1024,1152]{1,0:T(8,128)(2,1)} %copy-done.2, bf16[1024,256]{1,0:T(8,128)(2,1)} %copy-done.22, bf16[1024,256]{1,0:T(8,128)(2,1)} %copy-done.22, s32[8,1024]{1,0:T(8,128)} %pad.21.span_ref, ...), custom_call_target="tpu_custom_call" | custom-call | flops 2684354560 | bytes 2097152 | tf_op jit(solution)/shard_map/pallas_call | solution.py:500
  203.8 6.1 %shard_map.257 = (f32[1024,128]{1,0:T(8,128)}, bf16[1024,256]{1,0:T(8,128)(2,1)}) custom-call(s32[9]{0:T(128)} %pad_add_fusion.1.table, bf16[1024,1152]{1,0:T(8,128)(2,1)} %copy-done.2, bf16[1024,256]{1,0:T(8,128)(2,1)} %copy-done.21, bf16[1024,256]{1,0:T(8,128)(2,1)} %copy-done.21, s32[8,1024]{1,0:T(8,128)} %pad.21.span_ref, ...), custom_call_target="tpu_custom_call" | custom-call | flops 2684354560 | bytes 2097152 | tf_op jit(solution)/shard_map/pallas_call | solution.py:500
  210.0 5.9 %shard_map.256 = (f32[1024,128]{1,0:T(8,128)}, bf16[1024,256]{1,0:T(8,128)(2,1)}) custom-call(s32[9]{0:T(128)} %pad_add_fusion.1.table, bf16[1024,1152]{1,0:T(8,128)(2,1)} %copy-done.2, bf16[1024,256]{1,0:T(8,128)(2,1)} %copy-done.20, bf16[1024,256]{1,0:T(8,128)(2,1)} %copy-done.20, s32[8,1024]{1,0:T(8,128)} %pad.21.span_ref, ...), custom_call_target="tpu_custom_call" | custom-call | flops 2684354560 | bytes 2097152 | tf_op jit(solution)/shard_map/pallas_call | solution.py:500
  215.9 9.1 %shard_map.259 = (bf16[1024,128]{1,0:T(8,128)(2,1)}, f32[1024,128]{1,0:T(8,128)}, f32[1024,128]{1,0:T(8,128)}) custom-call(s32[9]{0:T(128)} %pad_add_fusion.1.table, bf16[1024,1152]{1,0:T(8,128)(2,1)} %copy-done.2, bf16[1024,1152]{1,0:T(8,128)(2,1)} %copy-done.2, bf16[1024,1152]{1,0:T(8,128)(2,1)} %copy-done.2, s32[8,1024]{1,0:T(8,128)} %pad.21.span_ref, ...), custom_call_target="tpu_custom_call" | custom-call | flops 2684354560 | bytes 2097152 | tf_op jit(solution)/shard_map/pallas_call | solution.py:500
  225.0 9.1 %collective-permute-start.28 = (bf16[1024,256]{1,0:T(8,128)(2,1)}, bf16[1024,256]{1,0:T(8,128)(2,1)}, u32[]{:S(2)}, u32[]{:S(2)}) collective-permute-start(bf16[1024,256]{1,0:T(8,128)(2,1)} %get-tuple-element.61), channel_id=1, source_target_pairs={{0,1},{1,0},{2,3},{3,2},{4,5},{5,4},{6,7},{7,6},{8,9},{9,8},{10,11... | collective-permute-start | bytes 1572872 | tf_op jit(solution)/shard_map/ppermute | solution.py:888
  236.5 9.0 %shard_map.260 = (bf16[1024,128]{1,0:T(8,128)(2,1)}, f32[1024,128]{1,0:T(8,128)}, f32[1024,128]{1,0:T(8,128)}) custom-call(s32[9]{0:T(128)} %pad_add_fusion.1.table, bf16[1024,1152]{1,0:T(8,128)(2,1)} %copy-done.2, bf16[1024,1152]{1,0:T(8,128)(2,1)} %copy-done.2, bf16[1024,1152]{1,0:T(8,128)(2,1)} %copy-done.2, s32[8,1024]{1,0:T(8,128)} %pad.21.span_ref, ...), custom_call_target="tpu_custom_call" | custom-call | flops 2684354560 | bytes 2097152 | tf_op jit(solution)/shard_map/pallas_call | solution.py:500
  245.5 9.0 %shard_map.261 = (bf16[1024,128]{1,0:T(8,128)(2,1)}, f32[1024,128]{1,0:T(8,128)}, f32[1024,128]{1,0:T(8,128)}) custom-call(s32[9]{0:T(128)} %pad_add_fusion.1.table, bf16[1024,1152]{1,0:T(8,128)(2,1)} %copy-done.2, bf16[1024,1152]{1,0:T(8,128)(2,1)} %copy-done.2, bf16[1024,1152]{1,0:T(8,128)(2,1)} %copy-done.2, s32[8,1024]{1,0:T(8,128)} %pad.21.span_ref, ...), custom_call_target="tpu_custom_call" | custom-call | flops 2684354560 | bytes 2097152 | tf_op jit(solution)/shard_map/pallas_call | solution.py:500
  254.5 7.8 %collective-permute-start.30 = (bf16[1024,256]{1,0:T(8,128)(2,1)}, bf16[1024,256]{1,0:T(8,128)(2,1)S(1)}, u32[]{:S(2)}, u32[]{:S(2)}) collective-permute-start(bf16[1024,256]{1,0:T(8,128)(2,1)} %get-tuple-element.71), channel_id=1, source_target_pairs={{0,1},{1,0},{2,3},{3,2},{4,5},{5,4},{6,7},{7,6},{8,9},{9,8},{10,11... | collective-permute-start | bytes 1572872 | tf_op jit(solution)/shard_map/ppermute | solution.py:888
  269.5 4.1 %collective-permute-done.30 = bf16[1024,256]{1,0:T(8,128)(2,1)S(1)} collective-permute-done((bf16[1024,256]{1,0:T(8,128)(2,1)}, bf16[1024,256]{1,0:T(8,128)(2,1)S(1)}, u32[]{:S(2)}, u32[]{:S(2)}) %collective-permute-start.30) | collective-permute-done | bytes 524320 | tf_op jit(solution)/shard_map/ppermute | solution.py:888
  295.0 12.4 %collective-permute-done.44 = bf16[4,64,384]{2,1,0:T(8,128)(2,1)S(1)} collective-permute-done((bf16[4,64,384]{2,1,0:T(8,128)(2,1)S(1)}, bf16[4,64,384]{2,1,0:T(8,128)(2,1)S(1)}, u32[]{:S(2)}, u32[]{:S(2)}) %collective-permute-start.44) | collective-permute-done | bytes 196640 | tf_op jit(solution)/shard_map/ppermute | solution.py:70
  315.8 5.6 %collective-permute-done.59 = bf16[192,384]{1,0:T(8,128)(2,1)S(1)} collective-permute-done((bf16[192,384]{1,0:T(8,128)(2,1)S(1)}, bf16[192,384]{1,0:T(8,128)(2,1)S(1)}, u32[]{:S(2)}, u32[]{:S(2)}) %collective-permute-start.59) | collective-permute-done | bytes 147488 | tf_op jit(solution)/shard_map/ppermute | solution.py:70
  336.0 4.5 %collective-permute-done.35 = bf16[4,96,384]{2,1,0:T(8,128)(2,1)S(1)} collective-permute-done((bf16[4,96,384]{2,1,0:T(8,128)(2,1)S(1)}, bf16[4,96,384]{2,1,0:T(8,128)(2,1)S(1)}, u32[]{:S(2)}, u32[]{:S(2)}) %collective-permute-start.35) | collective-permute-done | bytes 294944 | tf_op jit(solution)/shard_map/ppermute | solution.py:70
  340.5 9.4 %collective-permute-done.36 = bf16[4,96,384]{2,1,0:T(8,128)(2,1)S(1)} collective-permute-done((bf16[4,96,384]{2,1,0:T(8,128)(2,1)S(1)}, bf16[4,96,384]{2,1,0:T(8,128)(2,1)S(1)}, u32[]{:S(2)}, u32[]{:S(2)}) %collective-permute-start.36) | collective-permute-done | bytes 294944 | tf_op jit(solution)/shard_map/ppermute | solution.py:70
  376.5 7.2 %collective-permute-done.39 = bf16[352,384]{1,0:T(8,128)(2,1)S(1)} collective-permute-done((bf16[352,384]{1,0:T(8,128)(2,1)}, bf16[352,384]{1,0:T(8,128)(2,1)S(1)}, u32[]{:S(2)}, u32[]{:S(2)}) %collective-permute-start.39) | collective-permute-done | bytes 270368 | tf_op jit(solution)/shard_map/ppermute | solution.py:70
  383.7 4.5 %collective-permute-done.40 = bf16[352,384]{1,0:T(8,128)(2,1)S(1)} collective-permute-done((bf16[352,384]{1,0:T(8,128)(2,1)S(1)}, bf16[352,384]{1,0:T(8,128)(2,1)S(1)}, u32[]{:S(2)}, u32[]{:S(2)}) %collective-permute-start.40) | collective-permute-done | bytes 270368 | tf_op jit(solution)/shard_map/ppermute | solution.py:70
  (491 shorter events, 219.7 us)
Async XLA Ops:
  15.2 25.1 %collective-permute-start.12 = (bf16[448,384]{1,0:T(8,128)(2,1)S(1)}, bf16[448,384]{1,0:T(8,128)(2,1)S(1)}, u32[]{:S(2)}, u32[]{:S(2)}) collective-permute-start(bf16[448,384]{1,0:T(8,128)(2,1)S(1)} %pad_maximum_fusion.4), channel_id=1, source_target_pairs={{0,3},{1,2},{2,1},{3,0},{4,7},{5,6},{6,5},{7,4},{8,11},{9,10},{10,... | collective-permute-start | bytes 1032200 | tf_op jit(solution)/shard_map/ppermute | solution.py:70
  16.7 28.9 %collective-permute-start.11 = (bf16[448,384]{1,0:T(8,128)(2,1)S(1)}, bf16[448,384]{1,0:T(8,128)(2,1)}, u32[]{:S(2)}, u32[]{:S(2)}) collective-permute-start(bf16[448,384]{1,0:T(8,128)(2,1)S(1)} %pad_maximum_fusion.4), channel_id=1, source_target_pairs={{0,2},{1,3},{2,0},{3,1},{4,6},{5,7},{6,4},{7,5},{8,10},{9,11},{10,... | collective-permute-start | bytes 1032200 | tf_op jit(solution)/shard_map/ppermute | solution.py:70
  21.9 25.0 %collective-permute-start.10 = (bf16[448,384]{1,0:T(8,128)(2,1)S(1)}, bf16[448,384]{1,0:T(8,128)(2,1)}, u32[]{:S(2)}, u32[]{:S(2)}) collective-permute-start(bf16[448,384]{1,0:T(8,128)(2,1)S(1)} %pad_maximum_fusion.4), channel_id=1, source_target_pairs={{0,1},{1,0},{2,3},{3,2},{4,5},{5,4},{6,7},{7,6},{8,9},{9,8},{10,11... | collective-permute-start | bytes 1032200 | tf_op jit(solution)/shard_map/ppermute | solution.py:70
  23.2 35.1 %collective-permute-start = (bf16[1024,384]{1,0:T(8,128)(2,1)S(1)}, bf16[1024,384]{1,0:T(8,128)(2,1)S(1)}, u32[]{:S(2)}, u32[]{:S(2)}) collective-permute-start(bf16[1024,384]{1,0:T(8,128)(2,1)S(1)} %copy-done.43), channel_id=1, source_target_pairs={{0,4},{4,0},{1,5},{5,1},{2,6},{6,2},{3,7},{7,3},{8,12},{12,8},{9,1... | collective-permute-start | bytes 2359304 | tf_op jit(solution)/shard_map/ppermute | solution.py:43
  25.9 27.2 %collective-permute-start.6 = (bf16[3,144,384]{2,1,0:T(8,128)(2,1)S(1)}, bf16[3,144,384]{2,1,0:T(8,128)(2,1)}, u32[]{:S(2)}, u32[]{:S(2)}) collective-permute-start(bf16[3,144,384]{2,1,0:T(8,128)(2,1)S(1)} %pad_maximum_fusion.5.refs_0_), channel_id=1, source_target_pairs={{0,24},{8,16},{16,8},{24,0},{1,25},{9,17},{17,9},{25,1},{2,26},{10... | collective-permute-start | bytes 995336 | tf_op jit(solution)/shard_map/ppermute | solution.py:70
  50.6 67.1 %collective-permute-start.15 = (bf16[3,432,384]{2,1,0:T(8,128)(2,1)S(1)}, bf16[3,432,384]{2,1,0:T(8,128)(2,1)}, u32[]{:S(2)}, u32[]{:S(2)}) collective-permute-start(bf16[3,432,384]{2,1,0:T(8,128)(2,1)S(1)} %pad_maximum_fusion.refs_0_), channel_id=1, source_target_pairs={{0,24},{8,16},{16,8},{24,0},{1,25},{9,17},{17,9},{25,1},{2,26},{10... | collective-permute-start | bytes 2985992 | tf_op jit(solution)/shard_map/ppermute | solution.py:70
  53.1 64.6 %collective-permute-start.14 = (bf16[3,432,384]{2,1,0:T(8,128)(2,1)S(1)}, bf16[3,432,384]{2,1,0:T(8,128)(2,1)}, u32[]{:S(2)}, u32[]{:S(2)}) collective-permute-start(bf16[3,432,384]{2,1,0:T(8,128)(2,1)S(1)} %pad_maximum_fusion.refs_0_), channel_id=1, source_target_pairs={{0,16},{8,24},{16,0},{24,8},{1,17},{9,25},{17,1},{25,9},{2,18},{10... | collective-permute-start | bytes 2985992 | tf_op jit(solution)/shard_map/ppermute | solution.py:70
  53.6 64.1 %collective-permute-start.13 = (bf16[3,432,384]{2,1,0:T(8,128)(2,1)S(1)}, bf16[3,432,384]{2,1,0:T(8,128)(2,1)}, u32[]{:S(2)}, u32[]{:S(2)}) collective-permute-start(bf16[3,432,384]{2,1,0:T(8,128)(2,1)S(1)} %pad_maximum_fusion.refs_0_), channel_id=1, source_target_pairs={{0,8},{8,0},{16,24},{24,16},{1,9},{9,1},{17,25},{25,17},{2,10},{10... | collective-permute-start | bytes 2985992 | tf_op jit(solution)/shard_map/ppermute | solution.py:70
  67.0 26.9 %collective-permute-start.8 = (bf16[1024,256]{1,0:T(8,128)(2,1)}, bf16[1024,256]{1,0:T(8,128)(2,1)S(1)}, u32[]{:S(2)}, u32[]{:S(2)}) collective-permute-start(bf16[1024,256]{1,0:T(8,128)(2,1)} %get-tuple-element.115), channel_id=1, source_target_pairs={{1,0},{0,1},{3,2},{2,3},{5,4},{4,5},{7,6},{6,7},{9,8},{8,9},{11,10... | collective-permute-start | bytes 1572872 | tf_op jit(solution)/shard_map/ppermute | solution.py:700
  79.6 27.0 %collective-permute-start.9 = (bf16[1024,256]{1,0:T(8,128)(2,1)S(1)}, bf16[1024,256]{1,0:T(8,128)(2,1)S(1)}, u32[]{:S(2)}, u32[]{:S(2)}) collective-permute-start(bf16[1024,256]{1,0:T(8,128)(2,1)S(1)} %get-tuple-element.114), channel_id=1, source_target_pairs={{1,0},{0,1},{3,2},{2,3},{5,4},{4,5},{7,6},{6,7},{9,8},{8,9},{11,10... | collective-permute-start | bytes 1572872 | tf_op jit(solution)/shard_map/ppermute | solution.py:700
  93.9 44.1 %collective-permute-start.22 = (bf16[512,384]{1,0:T(8,128)(2,1)}, bf16[512,384]{1,0:T(8,128)(2,1)S(1)}, u32[]{:S(2)}, u32[]{:S(2)}) collective-permute-start(bf16[512,384]{1,0:T(8,128)(2,1)} %get-tuple-element.130), channel_id=1, source_target_pairs={{0,4},{4,0},{1,5},{5,1},{2,6},{6,2},{3,7},{7,3},{8,12},{12,8},{9,1... | collective-permute-start | bytes 1179656 | tf_op jit(solution)/shard_map/ppermute | solution.py:43
  169.6 24.3 %collective-permute-start.24 = (bf16[768,1536]{1,0:T(8,128)(2,1)}, bf16[768,1536]{1,0:T(8,128)(2,1)}, u32[]{:S(2)}, u32[]{:S(2)}) collective-permute-start(bf16[768,1536]{1,0:T(8,128)(2,1)} %convolution_convert_fusion.1), channel_id=1, source_target_pairs={{0,4},{4,0},{1,5},{5,1},{2,6},{6,2},{3,7},{7,3},{8,12},{12,8},{9,1... | collective-permute-start | bytes 7077896 | tf_op jit(solution)/shard_map/ppermute | solution.py:43
  186.8 101.6 %collective-permute-start.54 = (bf16[4,192,384]{2,1,0:T(8,128)(2,1)}, bf16[4,192,384]{2,1,0:T(8,128)(2,1)}, u32[]{:S(2)}, u32[]{:S(2)}) collective-permute-start(bf16[4,192,384]{2,1,0:T(8,128)(2,1)} %get-tuple-element.109), channel_id=1, source_target_pairs={{0,8},{8,0},{16,24},{24,16},{1,9},{9,1},{17,25},{25,17},{2,10},{10... | collective-permute-start | bytes 1769480 | tf_op jit(solution)/shard_map/ppermute | solution.py:70
  192.4 99.2 %collective-permute-start.55 = (bf16[4,192,384]{2,1,0:T(8,128)(2,1)}, bf16[4,192,384]{2,1,0:T(8,128)(2,1)}, u32[]{:S(2)}, u32[]{:S(2)}) collective-permute-start(bf16[4,192,384]{2,1,0:T(8,128)(2,1)} %get-tuple-element.110), channel_id=1, source_target_pairs={{0,16},{8,24},{16,0},{24,8},{1,17},{9,25},{17,1},{25,9},{2,18},{10... | collective-permute-start | bytes 1769480 | tf_op jit(solution)/shard_map/ppermute | solution.py:70
  192.4 99.5 %collective-permute-start.56 = (bf16[4,192,384]{2,1,0:T(8,128)(2,1)}, bf16[4,192,384]{2,1,0:T(8,128)(2,1)}, u32[]{:S(2)}, u32[]{:S(2)}) collective-permute-start(bf16[4,192,384]{2,1,0:T(8,128)(2,1)} %get-tuple-element.111), channel_id=1, source_target_pairs={{0,24},{8,16},{16,8},{24,0},{1,25},{9,17},{17,9},{25,1},{2,26},{10... | collective-permute-start | bytes 1769480 | tf_op jit(solution)/shard_map/ppermute | solution.py:70
  225.0 29.5 %collective-permute-start.28 = (bf16[1024,256]{1,0:T(8,128)(2,1)}, bf16[1024,256]{1,0:T(8,128)(2,1)}, u32[]{:S(2)}, u32[]{:S(2)}) collective-permute-start(bf16[1024,256]{1,0:T(8,128)(2,1)} %get-tuple-element.61), channel_id=1, source_target_pairs={{0,1},{1,0},{2,3},{3,2},{4,5},{5,4},{6,7},{7,6},{8,9},{9,8},{10,11... | collective-permute-start | bytes 1572872 | tf_op jit(solution)/shard_map/ppermute | solution.py:888
  234.1 31.7 %collective-permute-start.29 = (bf16[1024,256]{1,0:T(8,128)(2,1)}, bf16[1024,256]{1,0:T(8,128)(2,1)}, u32[]{:S(2)}, u32[]{:S(2)}) collective-permute-start(bf16[1024,256]{1,0:T(8,128)(2,1)} %get-tuple-element.66), channel_id=1, source_target_pairs={{0,1},{1,0},{2,3},{3,2},{4,5},{5,4},{6,7},{7,6},{8,9},{9,8},{10,11... | collective-permute-start | bytes 1572872 | tf_op jit(solution)/shard_map/ppermute | solution.py:888
  254.5 19.1 %collective-permute-start.30 = (bf16[1024,256]{1,0:T(8,128)(2,1)}, bf16[1024,256]{1,0:T(8,128)(2,1)S(1)}, u32[]{:S(2)}, u32[]{:S(2)}) collective-permute-start(bf16[1024,256]{1,0:T(8,128)(2,1)} %get-tuple-element.71), channel_id=1, source_target_pairs={{0,1},{1,0},{2,3},{3,2},{4,5},{5,4},{6,7},{7,6},{8,9},{9,8},{10,11... | collective-permute-start | bytes 1572872 | tf_op jit(solution)/shard_map/ppermute | solution.py:888
  265.9 64.7 %collective-permute-start.32 = (bf16[4,256,384]{2,1,0:T(8,128)(2,1)}, bf16[4,256,384]{2,1,0:T(8,128)(2,1)}, u32[]{:S(2)}, u32[]{:S(2)}) collective-permute-start(bf16[4,256,384]{2,1,0:T(8,128)(2,1)} %get-tuple-element.106), channel_id=1, source_target_pairs={{0,8},{8,0},{16,24},{24,16},{1,9},{9,1},{17,25},{25,17},{2,10},{10... | collective-permute-start | bytes 2359304 | tf_op jit(solution)/shard_map/ppermute | solution.py:70
  273.6 57.1 %collective-permute-start.34 = (bf16[4,256,384]{2,1,0:T(8,128)(2,1)}, bf16[4,256,384]{2,1,0:T(8,128)(2,1)}, u32[]{:S(2)}, u32[]{:S(2)}) collective-permute-start(bf16[4,256,384]{2,1,0:T(8,128)(2,1)} %get-tuple-element.107), channel_id=1, source_target_pairs={{0,24},{8,16},{16,8},{24,0},{1,25},{9,17},{17,9},{25,1},{2,26},{10... | collective-permute-start | bytes 2359304 | tf_op jit(solution)/shard_map/ppermute | solution.py:70
  327.8 64.2 %collective-permute-start.23 = (f32[512,384]{1,0:T(8,128)}, f32[512,384]{1,0:T(8,128)}, u32[]{:S(2)}, u32[]{:S(2)}) collective-permute-start(f32[512,384]{1,0:T(8,128)} %get-tuple-element.119), channel_id=1, source_target_pairs={{0,4},{4,0},{1,5},{5,1},{2,6},{6,2},{3,7},{7,3},{8,12},{12,8},{9,1... | collective-permute-start | bytes 2359304 | tf_op jit(solution)/shard_map/ppermute | solution.py:43
  330.5 61.5 %collective-permute-start.31 = (bf16[1024,384]{1,0:T(8,128)(2,1)}, bf16[1024,384]{1,0:T(8,128)(2,1)}, u32[]{:S(2)}, u32[]{:S(2)}) collective-permute-start(bf16[1024,384]{1,0:T(8,128)(2,1)} %dynamic-slice_convert_fusion), channel_id=1, source_target_pairs={{0,4},{4,0},{1,5},{5,1},{2,6},{6,2},{3,7},{7,3},{8,12},{12,8},{9,1... | collective-permute-start | bytes 2359304 | tf_op jit(solution)/shard_map/ppermute | solution.py:43
  330.7 19.3 %collective-permute-start.36 = (bf16[4,96,384]{2,1,0:T(8,128)(2,1)S(1)}, bf16[4,96,384]{2,1,0:T(8,128)(2,1)S(1)}, u32[]{:S(2)}, u32[]{:S(2)}) collective-permute-start(bf16[4,96,384]{2,1,0:T(8,128)(2,1)S(1)} %get-tuple-element.121), channel_id=1, source_target_pairs={{0,16},{8,24},{16,0},{24,8},{1,17},{9,25},{17,1},{25,9},{2,18},{10... | collective-permute-start | bytes 884744 | tf_op jit(solution)/shard_map/ppermute | solution.py:70
  340.5 24.9 %collective-permute-start.62 = (bf16[192,384]{1,0:T(8,128)(2,1)S(1)}, bf16[192,384]{1,0:T(8,128)(2,1)S(1)}, u32[]{:S(2)}, u32[]{:S(2)}) collective-permute-start(bf16[192,384]{1,0:T(8,128)(2,1)S(1)} %fusion.65.refs_0_), channel_id=1, source_target_pairs={{0,24},{8,16},{16,8},{24,0},{1,25},{9,17},{17,9},{25,1},{2,26},{10... | collective-permute-start | bytes 442376 | tf_op jit(solution)/shard_map/ppermute | solution.py:70
  (118 other events, 1042.2 us)

commit v4 on v3

--- a/solution.py
+++ b/solution.py
@@ -227,18 +227,16 @@
         ].astype(F32)
 
 
-def qkv_out_kernel(first_row, places, *refs):
-    parts, last_parts, out = refs[:4], refs[4:8], refs[8]
+def qkv_out_kernel(places, *refs):
+    parts, out = refs[:-1], refs[-1]
     dp = places[1]
     count = out.shape[1] // 4
     for j in range(4):
         rows = at_rows((dp ^ j) * count, count)
         for pair in range(PAIRS):
-            source = last_parts[j] if pair == PAIRS - 1 else parts[j]
-            start = 0 if pair == PAIRS - 1 else first_row + pair * count
             for kind in range(3):
-                out[kind, rows, pair * LANES : (pair + 1) * LANES] = source[
-                    start : start + count, kind * LANES : (kind + 1) * LANES
+                out[kind, rows, pair * LANES : (pair + 1) * LANES] = parts[j][
+                    pair * count : (pair + 1) * count, kind * LANES : (kind + 1) * LANES
                 ].astype(F32)
 
 
@@ -511,6 +509,36 @@
             flops=10 * rows * LEN * LANES, bytes_accessed=16 * rows * LANES, transcendentals=0
         ),
     )(table, *inputs)
+
+
+def finish_kernel(dq_ref, dk_ref, dv_ref, *refs):
+    arrived, (grad_ref, sum_ref) = refs[:-2], refs[-2:]
+    key, value = dk_ref[...], dv_ref[...]
+    for one in arrived:
+        key = key + one[:, :LANES].astype(F32)
+        value = value + one[:, LANES:].astype(F32)
+    for i, part in enumerate((dq_ref[...], key.astype(BF), value.astype(BF))):
+        lanes = slice(i * LANES, (i + 1) * LANES)
+        grad_ref[:, lanes] = part
+        total = jnp.sum(part.astype(F32), axis=0, keepdims=True)
+        sum_ref[:, lanes] = jnp.broadcast_to(total, (8, LANES))
+
+
+def finish_pair(grad_query, key_own, value_own, arrived):
+    rows = grad_query.shape[0]
+    spec = pl.BlockSpec(memory_space=pltpu.VMEM)
+    grad_pair, sums = pl.pallas_call(
+        finish_kernel,
+        out_shape=(
+            jax.ShapeDtypeStruct((rows, 3 * LANES), BF),
+            jax.ShapeDtypeStruct((8, 3 * LANES), F32),
+        ),
+        in_specs=[spec] * (3 + len(arrived)),
+        out_specs=(spec, spec),
+        cost_estimate=pl.CostEstimate(flops=0, bytes_accessed=3 << 20, transcendentals=0),
+        name="finish_pair",
+    )(grad_query, key_own, value_own, *arrived)
+    return grad_pair, sums[0]
 
 
 def attend_backward_others(table, qkv, kv_others, spans, out, logs, grad, blocks, pair):
@@ -865,7 +893,7 @@
         axis=2,
     )
     early, grad_attended = lax.optimization_barrier((early, grad_attended))
-    early_dp = reduce_dp(early)
+    early_parts = spread_dp(reduce_col(reduce_dp(early)))
     down_parts = spread_dp(reduce_col(down_dp))
 
     first_pass = []
@@ -878,24 +906,25 @@
         )
     query_parts = lax.optimization_barrier(tuple(part for part, _ in first_pass))
     grad_pairs, grad_w_pairs, bias_sums = [], [], []
+    query_parts = list(query_parts)
     for pair in range(PAIRS):
         out, logs = attended[pair]
         others = first_pass[pair][1]
+        if pair:
+            query_parts[pair], grad_query = lax.optimization_barrier(
+                (query_parts[pair], grad_query)
+            )
         grad_query, key_own, value_own = attend_backward_own(
             table, qkv_low, spans, out, logs, grad_attended, query_parts[pair], blocks, pair
         )
-        for j in range(1, group):
-            arrived = lax.ppermute(
-                others[(j - 1) * rows : j * rows], "col", group_perm(j, True)
-            ).astype(F32)
-            key_own = key_own + arrived[:, :LANES]
-            value_own = value_own + arrived[:, LANES:]
-        grad_pair = jnp.concatenate(
-            [grad_query, key_own.astype(BF), value_own.astype(BF)], axis=1
-        )
+        arrived = [
+            lax.ppermute(others[(j - 1) * rows : j * rows], "col", group_perm(j, True))
+            for j in range(1, group)
+        ]
+        grad_pair, pair_sums = finish_pair(grad_query, key_own, value_own, arrived)
         grad_pairs.append(grad_pair)
         grad_w_pairs.append(left_inner(input_full, grad_pair).astype(BF))
-        bias_sums.append(jnp.sum(grad_pair, axis=0, dtype=F32))
+        bias_sums.append(pair_sums)
     grad_qkv = jnp.concatenate(grad_pairs, axis=1)
 
     bias_pair = jnp.stack(
@@ -908,8 +937,6 @@
     pairs_dp = reduce_dp(
         jnp.concatenate([quartered_rows(one, col_grid) for one in grad_w_pairs[:-1]], axis=2),
     )
-    early_piece = reduce_col(jnp.concatenate([early_dp, pairs_dp], axis=1))
-    early_parts = spread_dp(early_piece)
     late = jnp.concatenate(
         [
             quartered_rows(grad_w_pairs[-1], col_grid),
@@ -917,7 +944,8 @@
         ],
         axis=2,
     )
-    late_parts = spread_dp(reduce_col(reduce_dp(late)))
+    late_dp = jnp.concatenate([pairs_dp, reduce_dp(late)], axis=1)
+    late_parts = spread_dp(reduce_col(late_dp))
 
     partial = right_inner(grad_qkv, w_qkv_half)
     arrived = swap(half_of(partial, 1 - row, 1).astype(BF)).astype(F32)
@@ -925,7 +953,6 @@
 
     cut_in = w_in.shape[0]
     cut_out = cut_in + w_out.shape[0] // 2
-    cut_vec = cut_out + vec_pad
     if col_grid > 4:
         down_all = jnp.stack(picked(down_parts, "dp")).astype(F32)
         early_all = jnp.stack(picked(early_parts, "dp")).astype(F32)
@@ -933,8 +960,7 @@
         grad_down_own = rows_to_lanes(down_all, 2).reshape(w_down.shape)
         grad_in_own = rows_to_lanes(early_all[:, :cut_in], 4).reshape(w_in.shape)
         grad_out_own = rows_to_lanes(early_all[:, cut_in:cut_out], 2).reshape(w_out.shape)
-        qkv_own = jnp.concatenate([early_all[:, cut_vec:], late_all[:, :-vec_pad]], axis=1)
-        qkv_own = qkv_own.reshape(4, PAIRS, depth, 3, LANES)
+        qkv_own = late_all[:, :-vec_pad].reshape(4, PAIRS, depth, 3, LANES)
         qkv_own = jnp.transpose(qkv_own, (0, 2, 3, 1, 4)).reshape(w_qkv.shape)
     else:
         grad_down_own = local_call(
@@ -947,16 +973,13 @@
             tuple(jax.ShapeDtypeStruct(one.shape, F32) for one in (w_in, w_out)),
         )
         qkv_own = local_call(
-            functools.partial(qkv_out_kernel, cut_vec),
-            places,
-            early_parts + late_parts,
-            jax.ShapeDtypeStruct((3, w_qkv.shape[0], WIDE), F32),
+            qkv_out_kernel, places, late_parts, jax.ShapeDtypeStruct((3, w_qkv.shape[0], WIDE), F32)
         )
         qkv_own = jnp.swapaxes(qkv_own, 0, 1)
     vec_own = first_quarter(early_parts, cut_out, vec_pad)
     vecs = [vec_own[i * share : (i + 1) * share] for i in range(6)]
     bias_in_own = vec_own[6 * share : 10 * share]
-    bias_own = first_quarter(late_parts, depth, vec_pad)[: 2 * share].reshape(2, share)
+    bias_own = first_quarter(late_parts, PAIRS * depth, vec_pad)[: 2 * share].reshape(2, share)
     return (
         result,
         grad_input,

time: 414 us -> 416 us (level)
  the two profiles are of different devices: /device:TPU:10 before, /device:TPU:0 now
where the time goes in v4:
time: 416 us; the launch traced here: 410 us
  waiting for transfers between devices  110 us (26%)
  Pallas kernels  105 us (25%)
  starting transfers between devices  76.4 us (18%)
  matrix products  50.1 us (12%)
  local copies, waits for them, and re-layouts  37.2 us (9%)
  other arithmetic  29.9 us (7%)
    ppermute x42, waiting for transfers between devices, xor_swap(): return lax.ppermute(value, axis, [(i, i ^ mask) for i in range(count)])  94.4 us
    ppermute x42, starting transfers between devices, xor_swap(): return lax.ppermute(value, axis, [(i, i ^ mask) for i in range(count)])  68.4 us
    pallas_call x6, Pallas kernels, backward_call(): pl.pallas_call(kernel, out_shape=outs, grid_spec=pltpu.PrefetchScalarGrid...  48 us
    pallas_call x3, Pallas kernels, attend_forward(): pl.pallas_call(functools.partial(forward_kernel, blocks), out_shape=(jax....  34.1 us
    dot_general x9, matrix products, left_inner(): lax.dot_general(left_mat, right_mat, (((0,), (0,)), ((), ())), preferred_...  19.8 us
    dot_general x7, matrix products, right_inner(): lax.dot_general(left_mat, right_mat, (((1,), (1,)), ((), ())), preferred_...  19.2 us
    pallas_call x5, Pallas kernels, local_call(): pl.pallas_call(kernel, out_shape=outs, in_specs=[pl.BlockSpec(memory_spac...  15 us
    unnamed x137, local copies, waits for them, and re-layouts  12.6 us
  transfers between devices with their start and end apart: 63, of which 19 were waited for; matrix products, arithmetic and copies ran while one was open for 20% of the time, Pallas kernels for 26%

profile of v4, /device:TPU:0, one launch (start us, length us, event | category | flops | bytes accessed | tf_op | source)
XLA Modules:
  0.0 410.1 jit_solution(11227930657585586627)
XLA Ops:
  2.3 5.1 %collective-permute-start.3 = (bf16[160,384]{1,0:T(8,128)(2,1)S(1)}, bf16[160,384]{1,0:T(8,128)(2,1)S(1)}, u32[]{:S(2)}, u32[]{:S(2)}) collective-permute-start(bf16[160,384]{1,0:T(8,128)(2,1)S(1)} %pad_maximum_fusion.3), channel_id=1, source_target_pairs={{0,3},{1,2},{2,1},{3,0},{4,7},{5,6},{6,5},{7,4},{8,11},{9,10},{10,... | collective-permute-start | bytes 368648 | tf_op jit(solution)/shard_map/ppermute | solution.py:70
  8.1 4.8 %concatenate.179 = bf16[960]{0:T(1024)(128)(2,1)S(1)} concatenate(bf16[96]{0:T(256)(128)(2,1)} %param.20, bf16[96]{0:T(256)(128)(2,1)} %param.21, bf16[96]{0:T(256)(128)(2,1)} %param.22, bf16[96]{0:T(256)(128)(2,1)} %param.26, bf16[96]{0:T(256)(128)(2,1)} %param.27, bf16[96]{0:T(256)(128)(2,1)} %param.28, bf16[384]{0:T(512)(128)(2,1)} %param.24), dimensions={0} | concatenate | bytes 3840 | tf_op jit(solution)/shard_map/concatenate | solution.py:669
  30.2 17.7 %collective-permute-done.11 = bf16[448,384]{1,0:T(8,128)(2,1)S(1)} collective-permute-done((bf16[448,384]{1,0:T(8,128)(2,1)S(1)}, bf16[448,384]{1,0:T(8,128)(2,1)S(1)}, u32[]{:S(2)}, u32[]{:S(2)}) %collective-permute-start.11) | collective-permute-done | bytes 344096 | tf_op jit(solution)/shard_map/ppermute | solution.py:70
  54.7 4.1 collective-permute-done.4.refs_1_
  72.2 11.1 %collective-permute-done.7.ko_ref.vo_ref = bf16[1024,256]{1,0:T(8,128)(2,1)S(1)} collective-permute-done((bf16[1024,256]{1,0:T(8,128)(2,1)}, bf16[1024,256]{1,0:T(8,128)(2,1)S(1)}, u32[]{:S(2)}, u32[]{:S(2)}) %collective-permute-start.7) | collective-permute-done | bytes 524320 | tf_op jit(solution)/shard_map/ppermute | solution.py:728
  84.1 11.7 %attend_forward.3 = (bf16[1024,128]{1,0:T(8,128)(2,1)}, f32[8,2048]{1,0:T(8,128)}) custom-call(s32[9]{0:T(128)} %pad_add_fusion.1.table, bf16[1024,1152]{1,0:T(8,128)(2,1)} %copy-done.2, bf16[1024,1152]{1,0:T(8,128)(2,1)} %copy-done.2, bf16[1024,1152]{1,0:T(8,128)(2,1)} %copy-done.2, bf16[1024,256]{1,0:T(8,128)(2,1)} %copy-done.14, ...), custom_call_target="tpu_custom_call" | custom-call | flops 2147483648 | bytes 1048576 | tf_op jit(solution)/shard_map/attend_forward/pallas_call | solution.py:474
  97.5 11.2 %attend_forward.4 = (bf16[1024,128]{1,0:T(8,128)(2,1)}, f32[8,2048]{1,0:T(8,128)}) custom-call(s32[9]{0:T(128)} %pad_add_fusion.1.table, bf16[1024,1152]{1,0:T(8,128)(2,1)} %copy-done.2, bf16[1024,1152]{1,0:T(8,128)(2,1)} %copy-done.2, bf16[1024,1152]{1,0:T(8,128)(2,1)} %copy-done.2, bf16[1024,256]{1,0:T(8,128)(2,1)} %collective-permute-done.8.ko_ref.vo_ref, ...), custom_call_target="tpu_custom_call" | custom-call | flops 2147483648 | bytes 1048576 | tf_op jit(solution)/shard_map/attend_forward/pallas_call | solution.py:474
  110.3 11.2 %attend_forward.5 = (bf16[1024,128]{1,0:T(8,128)(2,1)}, f32[8,2048]{1,0:T(8,128)}) custom-call(s32[9]{0:T(128)} %pad_add_fusion.1.table, bf16[1024,1152]{1,0:T(8,128)(2,1)} %copy-done.2, bf16[1024,1152]{1,0:T(8,128)(2,1)} %copy-done.2, bf16[1024,1152]{1,0:T(8,128)(2,1)} %copy-done.2, bf16[1024,256]{1,0:T(8,128)(2,1)} %collective-permute-done.9.ko_ref.vo_ref, ...), custom_call_target="tpu_custom_call" | custom-call | flops 2147483648 | bytes 1048576 | tf_op jit(solution)/shard_map/attend_forward/pallas_call | solution.py:474
  121.6 5.4 %shard_map.255 = (bf16[1536,768]{1,0:T(8,128)(2,1)}, bf16[768,1536]{1,0:T(8,128)(2,1)}, bf16[384,768]{1,0:T(8,128)(2,1)}) custom-call(s32[2]{0:T(128)} %pad_add_fusion.2.places, bf16[384,768]{1,0:T(8,128)(2,1)} %own_down.1, bf16[192,1536]{1,0:T(8,128)(2,1)} %own_in.1, bf16[96,768]{1,0:T(8,128)(2,1)} %own_out.1, bf16[3,432,384]{2,1,0:T(8,128)(2,1)} %copy-done.7, ...), custom_call_target="tpu_custom_call" | custom-call | bytes 4194304 | tf_op jit(solution)/shard_map/pallas_call | solution.py:147
  158.4 4.6 %multiply_reduce_fusion = (f32[768]{0:T(1024)S(1)}, f32[512]{0:T(512)S(1)}, f32[512]{0:T(512)S(1)}, f32[768]{0:T(1024)S(1)}, f32[512,768]{1,0:T(8,128)S(1)}) fusion(f32[512,768]{1,0:T(8,128)S(1)} %get-tuple-element.189, f32[512]{0:T(512)S(1)} %add_rsqrt_fusion.1, f32[512]{0:T(512)S(1)} %broadcast_multiply_fusion.5, f32[768]{0:T(1024)S(1)} %maximum_select_fusion.6, ...), kind=kOutput, calls=%fused_computation.68 | convolution fusion | flops 1212282368 | bytes 10241024 | tf_op jit(solution)/shard_map/dot_general | solution.py:37
  189.8 7.5 %collective-permute-start.54 = (bf16[4,192,384]{2,1,0:T(8,128)(2,1)}, bf16[4,192,384]{2,1,0:T(8,128)(2,1)}, u32[]{:S(2)}, u32[]{:S(2)}) collective-permute-start(bf16[4,192,384]{2,1,0:T(8,128)(2,1)} %get-tuple-element.113), channel_id=1, source_target_pairs={{0,8},{8,0},{16,24},{24,16},{1,9},{9,1},{17,25},{25,17},{2,10},{10... | collective-permute-start | bytes 1769480 | tf_op jit(solution)/shard_map/ppermute | solution.py:70
  202.8 6.9 %shard_map.258 = (f32[1024,128]{1,0:T(8,128)}, bf16[1024,256]{1,0:T(8,128)(2,1)}) custom-call(s32[9]{0:T(128)} %pad_add_fusion.1.table, bf16[1024,1152]{1,0:T(8,128)(2,1)} %copy-done.2, bf16[1024,256]{1,0:T(8,128)(2,1)} %collective-permute-done.9.ko_ref.vo_ref, bf16[1024,256]{1,0:T(8,128)(2,1)} %collective-permute-done.9.ko_ref.vo_ref, ...), custom_call_target="tpu_custom_call" | custom-call | flops 2684354560 | bytes 2097152 | tf_op jit(solution)/shard_map/pallas_call | solution.py:498
  209.7 7.1 %shard_map.257 = (f32[1024,128]{1,0:T(8,128)}, bf16[1024,256]{1,0:T(8,128)(2,1)}) custom-call(s32[9]{0:T(128)} %pad_add_fusion.1.table, bf16[1024,1152]{1,0:T(8,128)(2,1)} %copy-done.2, bf16[1024,256]{1,0:T(8,128)(2,1)} %collective-permute-done.8.ko_ref.vo_ref, bf16[1024,256]{1,0:T(8,128)(2,1)} %collective-permute-done.8.ko_ref.vo_ref, ...), custom_call_target="tpu_custom_call" | custom-call | flops 2684354560 | bytes 2097152 | tf_op jit(solution)/shard_map/pallas_call | solution.py:498
  216.8 7.0 %shard_map.256 = (f32[1024,128]{1,0:T(8,128)}, bf16[1024,256]{1,0:T(8,128)(2,1)}) custom-call(s32[9]{0:T(128)} %pad_add_fusion.1.table, bf16[1024,1152]{1,0:T(8,128)(2,1)} %copy-done.2, bf16[1024,256]{1,0:T(8,128)(2,1)} %copy-done.14, bf16[1024,256]{1,0:T(8,128)(2,1)} %copy-done.14, s32[8,1024]{1,0:T(8,128)} %pad.21.span_ref, ...), custom_call_target="tpu_custom_call" | custom-call | flops 2684354560 | bytes 2097152 | tf_op jit(solution)/shard_map/pallas_call | solution.py:498
  223.8 9.0 %shard_map.259 = (bf16[1024,128]{1,0:T(8,128)(2,1)}, f32[1024,128]{1,0:T(8,128)}, f32[1024,128]{1,0:T(8,128)}) custom-call(s32[9]{0:T(128)} %pad_add_fusion.1.table, bf16[1024,1152]{1,0:T(8,128)(2,1)} %copy-done.2, bf16[1024,1152]{1,0:T(8,128)(2,1)} %copy-done.2, bf16[1024,1152]{1,0:T(8,128)(2,1)} %copy-done.2, s32[8,1024]{1,0:T(8,128)} %pad.21.span_ref, ...), custom_call_target="tpu_custom_call" | custom-call | flops 2684354560 | bytes 2097152 | tf_op jit(solution)/shard_map/pallas_call | solution.py:498
  234.8 9.0 %shard_map.260 = (bf16[1024,128]{1,0:T(8,128)(2,1)}, f32[1024,128]{1,0:T(8,128)}, f32[1024,128]{1,0:T(8,128)}) custom-call(s32[9]{0:T(128)} %pad_add_fusion.1.table, bf16[1024,1152]{1,0:T(8,128)(2,1)} %copy-done.2, bf16[1024,1152]{1,0:T(8,128)(2,1)} %copy-done.2, bf16[1024,1152]{1,0:T(8,128)(2,1)} %copy-done.2, s32[8,1024]{1,0:T(8,128)} %pad.21.span_ref, ...), custom_call_target="tpu_custom_call" | custom-call | flops 2684354560 | bytes 2097152 | tf_op jit(solution)/shard_map/pallas_call | solution.py:498
  244.9 9.0 %shard_map.261 = (bf16[1024,128]{1,0:T(8,128)(2,1)}, f32[1024,128]{1,0:T(8,128)}, f32[1024,128]{1,0:T(8,128)}) custom-call(s32[9]{0:T(128)} %pad_add_fusion.1.table, bf16[1024,1152]{1,0:T(8,128)(2,1)} %copy-done.2, bf16[1024,1152]{1,0:T(8,128)(2,1)} %copy-done.2, bf16[1024,1152]{1,0:T(8,128)(2,1)} %copy-done.2, s32[8,1024]{1,0:T(8,128)} %pad.21.span_ref, ...), custom_call_target="tpu_custom_call" | custom-call | flops 2684354560 | bytes 2097152 | tf_op jit(solution)/shard_map/pallas_call | solution.py:498
  255.3 4.9 %collective-permute-start.56 = (bf16[4,192,384]{2,1,0:T(8,128)(2,1)}, bf16[4,192,384]{2,1,0:T(8,128)(2,1)}, u32[]{:S(2)}, u32[]{:S(2)}) collective-permute-start(bf16[4,192,384]{2,1,0:T(8,128)(2,1)} %get-tuple-element.115), channel_id=1, source_target_pairs={{0,24},{8,16},{16,8},{24,0},{1,25},{9,17},{17,9},{25,1},{2,26},{10... | collective-permute-start | bytes 1769480 | tf_op jit(solution)/shard_map/ppermute | solution.py:70
  287.7 23.7 %collective-permute-done.35 = bf16[4,64,384]{2,1,0:T(8,128)(2,1)S(1)} collective-permute-done((bf16[4,64,384]{2,1,0:T(8,128)(2,1)S(1)}, bf16[4,64,384]{2,1,0:T(8,128)(2,1)S(1)}, u32[]{:S(2)}, u32[]{:S(2)}) %collective-permute-start.35) | collective-permute-done | bytes 196640 | tf_op jit(solution)/shard_map/ppermute | solution.py:70
  314.1 11.5 %collective-permute-done.36 = bf16[4,64,384]{2,1,0:T(8,128)(2,1)S(1)} collective-permute-done((bf16[4,64,384]{2,1,0:T(8,128)(2,1)S(1)}, bf16[4,64,384]{2,1,0:T(8,128)(2,1)S(1)}, u32[]{:S(2)}, u32[]{:S(2)}) %collective-permute-start.36) | collective-permute-done | bytes 196640 | tf_op jit(solution)/shard_map/ppermute | solution.py:70
  337.8 4.0 collective-permute-done.58
  350.2 10.1 %collective-permute-done.33 = bf16[4,96,384]{2,1,0:T(8,128)(2,1)S(1)} collective-permute-done((bf16[4,96,384]{2,1,0:T(8,128)(2,1)S(1)}, bf16[4,96,384]{2,1,0:T(8,128)(2,1)S(1)}, u32[]{:S(2)}, u32[]{:S(2)}) %collective-permute-start.33) | collective-permute-done | bytes 294944 | tf_op jit(solution)/shard_map/ppermute | solution.py:70
  376.7 4.8 %collective-permute-done.49 = bf16[256,384]{1,0:T(8,128)(2,1)S(1)} collective-permute-done((bf16[256,384]{1,0:T(8,128)(2,1)S(1)}, bf16[256,384]{1,0:T(8,128)(2,1)S(1)}, u32[]{:S(2)}, u32[]{:S(2)}) %collective-permute-start.49) | collective-permute-done | bytes 196640 | tf_op jit(solution)/shard_map/ppermute | solution.py:70
  382.8 7.0 %collective-permute-done.48 = bf16[256,384]{1,0:T(8,128)(2,1)S(1)} collective-permute-done((bf16[256,384]{1,0:T(8,128)(2,1)S(1)}, bf16[256,384]{1,0:T(8,128)(2,1)S(1)}, u32[]{:S(2)}, u32[]{:S(2)}) %collective-permute-start.48) | collective-permute-done | bytes 196640 | tf_op jit(solution)/shard_map/ppermute | solution.py:70
  (452 shorter events, 199.6 us)
Async XLA Ops:
  19.5 28.4 %collective-permute-start.11 = (bf16[448,384]{1,0:T(8,128)(2,1)S(1)}, bf16[448,384]{1,0:T(8,128)(2,1)S(1)}, u32[]{:S(2)}, u32[]{:S(2)}) collective-permute-start(bf16[448,384]{1,0:T(8,128)(2,1)S(1)} %pad_maximum_fusion.1), channel_id=1, source_target_pairs={{0,2},{1,3},{2,0},{3,1},{4,6},{5,7},{6,4},{7,5},{8,10},{9,11},{10,... | collective-permute-start | bytes 1032200 | tf_op jit(solution)/shard_map/ppermute | solution.py:70
  23.0 26.5 %collective-permute-start.10 = (bf16[448,384]{1,0:T(8,128)(2,1)S(1)}, bf16[448,384]{1,0:T(8,128)(2,1)S(1)}, u32[]{:S(2)}, u32[]{:S(2)}) collective-permute-start(bf16[448,384]{1,0:T(8,128)(2,1)S(1)} %pad_maximum_fusion.1), channel_id=1, source_target_pairs={{0,1},{1,0},{2,3},{3,2},{4,5},{5,4},{6,7},{7,6},{8,9},{9,8},{10,11... | collective-permute-start | bytes 1032200 | tf_op jit(solution)/shard_map/ppermute | solution.py:70
  23.6 38.0 %collective-permute-start = (bf16[1024,384]{1,0:T(8,128)(2,1)}, bf16[1024,384]{1,0:T(8,128)(2,1)}, u32[]{:S(2)}, u32[]{:S(2)}) collective-permute-start(bf16[1024,384]{1,0:T(8,128)(2,1)} %param.15), channel_id=1, source_target_pairs={{0,4},{4,0},{1,5},{5,1},{2,6},{6,2},{3,7},{7,3},{8,12},{12,8},{9,1... | collective-permute-start | bytes 2359304 | tf_op jit(solution)/shard_map/ppermute | solution.py:43
  24.1 28.5 %collective-permute-start.6 = (bf16[3,144,384]{2,1,0:T(8,128)(2,1)S(1)}, bf16[3,144,384]{2,1,0:T(8,128)(2,1)S(1)}, u32[]{:S(2)}, u32[]{:S(2)}) collective-permute-start(bf16[3,144,384]{2,1,0:T(8,128)(2,1)S(1)} %pad_maximum_fusion.2.refs_0_), channel_id=1, source_target_pairs={{0,24},{8,16},{16,8},{24,0},{1,25},{9,17},{17,9},{25,1},{2,26},{10... | collective-permute-start | bytes 995336 | tf_op jit(solution)/shard_map/ppermute | solution.py:70
  28.5 24.6 %collective-permute-start.5 = (bf16[3,144,384]{2,1,0:T(8,128)(2,1)S(1)}, bf16[3,144,384]{2,1,0:T(8,128)(2,1)}, u32[]{:S(2)}, u32[]{:S(2)}) collective-permute-start(bf16[3,144,384]{2,1,0:T(8,128)(2,1)S(1)} %pad_maximum_fusion.2.refs_0_), channel_id=1, source_target_pairs={{0,16},{8,24},{16,0},{24,8},{1,17},{9,25},{17,1},{25,9},{2,18},{10... | collective-permute-start | bytes 995336 | tf_op jit(solution)/shard_map/ppermute | solution.py:70
  51.1 70.5 %collective-permute-start.15 = (bf16[3,432,384]{2,1,0:T(8,128)(2,1)S(1)}, bf16[3,432,384]{2,1,0:T(8,128)(2,1)}, u32[]{:S(2)}, u32[]{:S(2)}) collective-permute-start(bf16[3,432,384]{2,1,0:T(8,128)(2,1)S(1)} %pad_maximum_fusion.refs_0_), channel_id=1, source_target_pairs={{0,24},{8,16},{16,8},{24,0},{1,25},{9,17},{17,9},{25,1},{2,26},{10... | collective-permute-start | bytes 2985992 | tf_op jit(solution)/shard_map/ppermute | solution.py:70
  52.7 68.9 %collective-permute-start.14 = (bf16[3,432,384]{2,1,0:T(8,128)(2,1)S(1)}, bf16[3,432,384]{2,1,0:T(8,128)(2,1)}, u32[]{:S(2)}, u32[]{:S(2)}) collective-permute-start(bf16[3,432,384]{2,1,0:T(8,128)(2,1)S(1)} %pad_maximum_fusion.refs_0_), channel_id=1, source_target_pairs={{0,16},{8,24},{16,0},{24,8},{1,17},{9,25},{17,1},{25,9},{2,18},{10... | collective-permute-start | bytes 2985992 | tf_op jit(solution)/shard_map/ppermute | solution.py:70
  53.2 68.4 %collective-permute-start.13 = (bf16[3,432,384]{2,1,0:T(8,128)(2,1)S(1)}, bf16[3,432,384]{2,1,0:T(8,128)(2,1)}, u32[]{:S(2)}, u32[]{:S(2)}) collective-permute-start(bf16[3,432,384]{2,1,0:T(8,128)(2,1)S(1)} %pad_maximum_fusion.refs_0_), channel_id=1, source_target_pairs={{0,8},{8,0},{16,24},{24,16},{1,9},{9,1},{17,25},{25,17},{2,10},{10... | collective-permute-start | bytes 2985992 | tf_op jit(solution)/shard_map/ppermute | solution.py:70
  68.6 28.9 %collective-permute-start.8 = (bf16[1024,256]{1,0:T(8,128)(2,1)}, bf16[1024,256]{1,0:T(8,128)(2,1)}, u32[]{:S(2)}, u32[]{:S(2)}) collective-permute-start(bf16[1024,256]{1,0:T(8,128)(2,1)} %get-tuple-element.119), channel_id=1, source_target_pairs={{1,0},{0,1},{3,2},{2,3},{5,4},{4,5},{7,6},{6,7},{9,8},{8,9},{11,10... | collective-permute-start | bytes 1572872 | tf_op jit(solution)/shard_map/ppermute | solution.py:728
  83.3 27.0 %collective-permute-start.9 = (bf16[1024,256]{1,0:T(8,128)(2,1)}, bf16[1024,256]{1,0:T(8,128)(2,1)}, u32[]{:S(2)}, u32[]{:S(2)}) collective-permute-start(bf16[1024,256]{1,0:T(8,128)(2,1)} %get-tuple-element.118), channel_id=1, source_target_pairs={{1,0},{0,1},{3,2},{2,3},{5,4},{4,5},{7,6},{6,7},{9,8},{8,9},{11,10... | collective-permute-start | bytes 1572872 | tf_op jit(solution)/shard_map/ppermute | solution.py:728
  97.5 45.6 %collective-permute-start.22 = (bf16[512,384]{1,0:T(8,128)(2,1)}, bf16[512,384]{1,0:T(8,128)(2,1)S(1)}, u32[]{:S(2)}, u32[]{:S(2)}) collective-permute-start(bf16[512,384]{1,0:T(8,128)(2,1)} %get-tuple-element.134), channel_id=1, source_target_pairs={{0,4},{4,0},{1,5},{5,1},{2,6},{6,2},{3,7},{7,3},{8,12},{12,8},{9,1... | collective-permute-start | bytes 1179656 | tf_op jit(solution)/shard_map/ppermute | solution.py:43
  171.9 26.8 %collective-permute-start.24 = (bf16[768,1536]{1,0:T(8,128)(2,1)}, bf16[768,1536]{1,0:T(8,128)(2,1)}, u32[]{:S(2)}, u32[]{:S(2)}) collective-permute-start(bf16[768,1536]{1,0:T(8,128)(2,1)} %convolution_convert_fusion.1), channel_id=1, source_target_pairs={{0,4},{4,0},{1,5},{5,1},{2,6},{6,2},{3,7},{7,3},{8,12},{12,8},{9,1... | collective-permute-start | bytes 7077896 | tf_op jit(solution)/shard_map/ppermute | solution.py:43
  189.8 91.7 %collective-permute-start.54 = (bf16[4,192,384]{2,1,0:T(8,128)(2,1)}, bf16[4,192,384]{2,1,0:T(8,128)(2,1)}, u32[]{:S(2)}, u32[]{:S(2)}) collective-permute-start(bf16[4,192,384]{2,1,0:T(8,128)(2,1)} %get-tuple-element.113), channel_id=1, source_target_pairs={{0,8},{8,0},{16,24},{24,16},{1,9},{9,1},{17,25},{25,17},{2,10},{10... | collective-permute-start | bytes 1769480 | tf_op jit(solution)/shard_map/ppermute | solution.py:70
  197.3 85.4 %collective-permute-start.55 = (bf16[4,192,384]{2,1,0:T(8,128)(2,1)}, bf16[4,192,384]{2,1,0:T(8,128)(2,1)}, u32[]{:S(2)}, u32[]{:S(2)}) collective-permute-start(bf16[4,192,384]{2,1,0:T(8,128)(2,1)} %get-tuple-element.114), channel_id=1, source_target_pairs={{0,16},{8,24},{16,0},{24,8},{1,17},{9,25},{17,1},{25,9},{2,18},{10... | collective-permute-start | bytes 1769480 | tf_op jit(solution)/shard_map/ppermute | solution.py:70
  232.8 30.7 %collective-permute-start.29 = (bf16[1024,256]{1,0:T(8,128)(2,1)}, bf16[1024,256]{1,0:T(8,128)(2,1)}, u32[]{:S(2)}, u32[]{:S(2)}) collective-permute-start(bf16[1024,256]{1,0:T(8,128)(2,1)} %get-tuple-element.77), channel_id=1, source_target_pairs={{0,1},{1,0},{2,3},{3,2},{4,5},{5,4},{6,7},{7,6},{8,9},{9,8},{10,11... | collective-permute-start | bytes 1572872 | tf_op jit(solution)/shard_map/ppermute | solution.py:921
  243.9 25.4 %collective-permute-start.30 = (bf16[1024,256]{1,0:T(8,128)(2,1)}, bf16[1024,256]{1,0:T(8,128)(2,1)}, u32[]{:S(2)}, u32[]{:S(2)}) collective-permute-start(bf16[1024,256]{1,0:T(8,128)(2,1)} %get-tuple-element.84), channel_id=1, source_target_pairs={{0,1},{1,0},{2,3},{3,2},{4,5},{5,4},{6,7},{7,6},{8,9},{9,8},{10,11... | collective-permute-start | bytes 1572872 | tf_op jit(solution)/shard_map/ppermute | solution.py:921
  255.3 29.1 %collective-permute-start.56 = (bf16[4,192,384]{2,1,0:T(8,128)(2,1)}, bf16[4,192,384]{2,1,0:T(8,128)(2,1)}, u32[]{:S(2)}, u32[]{:S(2)}) collective-permute-start(bf16[4,192,384]{2,1,0:T(8,128)(2,1)} %get-tuple-element.115), channel_id=1, source_target_pairs={{0,24},{8,16},{16,8},{24,0},{1,25},{9,17},{17,9},{25,1},{2,26},{10... | collective-permute-start | bytes 1769480 | tf_op jit(solution)/shard_map/ppermute | solution.py:70
  263.5 79.5 %collective-permute-start.44 = (bf16[4,256,384]{2,1,0:T(8,128)(2,1)}, bf16[4,256,384]{2,1,0:T(8,128)(2,1)}, u32[]{:S(2)}, u32[]{:S(2)}) collective-permute-start(bf16[4,256,384]{2,1,0:T(8,128)(2,1)} %get-tuple-element.110), channel_id=1, source_target_pairs={{0,8},{8,0},{16,24},{24,16},{1,9},{9,1},{17,25},{25,17},{2,10},{10... | collective-permute-start | bytes 2359304 | tf_op jit(solution)/shard_map/ppermute | solution.py:70
  269.3 75.5 %collective-permute-start.46 = (bf16[4,256,384]{2,1,0:T(8,128)(2,1)}, bf16[4,256,384]{2,1,0:T(8,128)(2,1)}, u32[]{:S(2)}, u32[]{:S(2)}) collective-permute-start(bf16[4,256,384]{2,1,0:T(8,128)(2,1)} %get-tuple-element.111), channel_id=1, source_target_pairs={{0,24},{8,16},{16,8},{24,0},{1,25},{9,17},{17,9},{25,1},{2,26},{10... | collective-permute-start | bytes 2359304 | tf_op jit(solution)/shard_map/ppermute | solution.py:70
  281.5 64.5 %collective-permute-start.45 = (bf16[4,256,384]{2,1,0:T(8,128)(2,1)S(1)}, bf16[4,256,384]{2,1,0:T(8,128)(2,1)S(1)}, u32[]{:S(2)}, u32[]{:S(2)}) collective-permute-start(bf16[4,256,384]{2,1,0:T(8,128)(2,1)S(1)} %copy-done.29), channel_id=1, source_target_pairs={{0,16},{8,24},{16,0},{24,8},{1,17},{9,25},{17,1},{25,9},{2,18},{10... | collective-permute-start | bytes 2359304 | tf_op jit(solution)/shard_map/ppermute | solution.py:70
  282.7 28.7 %collective-permute-start.35 = (bf16[4,64,384]{2,1,0:T(8,128)(2,1)S(1)}, bf16[4,64,384]{2,1,0:T(8,128)(2,1)S(1)}, u32[]{:S(2)}, u32[]{:S(2)}) collective-permute-start(bf16[4,64,384]{2,1,0:T(8,128)(2,1)S(1)} %get-tuple-element.130), channel_id=1, source_target_pairs={{0,8},{8,0},{16,24},{24,16},{1,9},{9,1},{17,25},{25,17},{2,10},{10... | collective-permute-start | bytes 589832 | tf_op jit(solution)/shard_map/ppermute | solution.py:70
  284.4 41.2 %collective-permute-start.36 = (bf16[4,64,384]{2,1,0:T(8,128)(2,1)S(1)}, bf16[4,64,384]{2,1,0:T(8,128)(2,1)S(1)}, u32[]{:S(2)}, u32[]{:S(2)}) collective-permute-start(bf16[4,64,384]{2,1,0:T(8,128)(2,1)S(1)} %get-tuple-element.131), channel_id=1, source_target_pairs={{0,16},{8,24},{16,0},{24,8},{1,17},{9,25},{17,1},{25,9},{2,18},{10... | collective-permute-start | bytes 589832 | tf_op jit(solution)/shard_map/ppermute | solution.py:70
  365.7 40.9 %collective-permute-start.23 = (f32[512,384]{1,0:T(8,128)S(1)}, f32[512,384]{1,0:T(8,128)S(1)}, u32[]{:S(2)}, u32[]{:S(2)}) collective-permute-start(f32[512,384]{1,0:T(8,128)S(1)} %copy-done.24), channel_id=1, source_target_pairs={{0,4},{4,0},{1,5},{5,1},{2,6},{6,2},{3,7},{7,3},{8,12},{12,8},{9,1... | collective-permute-start | bytes 2359304 | tf_op jit(solution)/shard_map/ppermute | solution.py:43
  366.3 40.3 %collective-permute-start.31 = (bf16[1024,384]{1,0:T(8,128)(2,1)}, bf16[1024,384]{1,0:T(8,128)(2,1)}, u32[]{:S(2)}, u32[]{:S(2)}) collective-permute-start(bf16[1024,384]{1,0:T(8,128)(2,1)} %dynamic-slice_convert_fusion), channel_id=1, source_target_pairs={{0,4},{4,0},{1,5},{5,1},{2,6},{6,2},{3,7},{7,3},{8,12},{12,8},{9,1... | collective-permute-start | bytes 2359304 | tf_op jit(solution)/shard_map/ppermute | solution.py:43
  (103 other events, 910.6 us)

commit v5 on v4

--- a/solution.py
+++ b/solution.py
@@ -227,16 +227,18 @@
         ].astype(F32)
 
 
-def qkv_out_kernel(places, *refs):
-    parts, out = refs[:-1], refs[-1]
+def qkv_out_kernel(first_row, places, *refs):
+    parts, last_parts, out = refs[:4], refs[4:8], refs[8]
     dp = places[1]
     count = out.shape[1] // 4
     for j in range(4):
         rows = at_rows((dp ^ j) * count, count)
         for pair in range(PAIRS):
+            source = last_parts[j] if pair == PAIRS - 1 else parts[j]
+            start = 0 if pair == PAIRS - 1 else first_row + pair * count
             for kind in range(3):
-                out[kind, rows, pair * LANES : (pair + 1) * LANES] = parts[j][
-                    pair * count : (pair + 1) * count, kind * LANES : (kind + 1) * LANES
+                out[kind, rows, pair * LANES : (pair + 1) * LANES] = source[
+                    start : start + count, kind * LANES : (kind + 1) * LANES
                 ].astype(F32)
 
 
@@ -661,7 +663,7 @@
     own_col = lax.axis_index("col")
     group = LEN // rows
     start_row = own_col * rows
-    block = min(256, rows)
+    block = min(512, rows)
     blocks = rows // block
 
     qkv_piece = jnp.swapaxes(dp_part(w_qkv, own_dp), 0, 1)
@@ -893,7 +895,7 @@
         axis=2,
     )
     early, grad_attended = lax.optimization_barrier((early, grad_attended))
-    early_parts = spread_dp(reduce_col(reduce_dp(early)))
+    early_dp = reduce_dp(early)
     down_parts = spread_dp(reduce_col(down_dp))
 
     first_pass = []
@@ -937,6 +939,8 @@
     pairs_dp = reduce_dp(
         jnp.concatenate([quartered_rows(one, col_grid) for one in grad_w_pairs[:-1]], axis=2),
     )
+    early_piece = reduce_col(jnp.concatenate([early_dp, pairs_dp], axis=1))
+    early_parts = spread_dp(early_piece)
     late = jnp.concatenate(
         [
             quartered_rows(grad_w_pairs[-1], col_grid),
@@ -944,8 +948,7 @@
         ],
         axis=2,
     )
-    late_dp = jnp.concatenate([pairs_dp, reduce_dp(late)], axis=1)
-    late_parts = spread_dp(reduce_col(late_dp))
+    late_parts = spread_dp(reduce_col(reduce_dp(late)))
 
     partial = right_inner(grad_qkv, w_qkv_half)
     arrived = swap(half_of(partial, 1 - row, 1).astype(BF)).astype(F32)
@@ -953,6 +956,7 @@
 
     cut_in = w_in.shape[0]
     cut_out = cut_in + w_out.shape[0] // 2
+    cut_vec = cut_out + vec_pad
     if col_grid > 4:
         down_all = jnp.stack(picked(down_parts, "dp")).astype(F32)
         early_all = jnp.stack(picked(early_parts, "dp")).astype(F32)
@@ -960,7 +964,8 @@
         grad_down_own = rows_to_lanes(down_all, 2).reshape(w_down.shape)
         grad_in_own = rows_to_lanes(early_all[:, :cut_in], 4).reshape(w_in.shape)
         grad_out_own = rows_to_lanes(early_all[:, cut_in:cut_out], 2).reshape(w_out.shape)
-        qkv_own = late_all[:, :-vec_pad].reshape(4, PAIRS, depth, 3, LANES)
+        qkv_own = jnp.concatenate([early_all[:, cut_vec:], late_all[:, :-vec_pad]], axis=1)
+        qkv_own = qkv_own.reshape(4, PAIRS, depth, 3, LANES)
         qkv_own = jnp.transpose(qkv_own, (0, 2, 3, 1, 4)).reshape(w_qkv.shape)
     else:
         grad_down_own = local_call(
@@ -973,13 +978,16 @@
             tuple(jax.ShapeDtypeStruct(one.shape, F32) for one in (w_in, w_out)),
         )
         qkv_own = local_call(
-            qkv_out_kernel, places, late_parts, jax.ShapeDtypeStruct((3, w_qkv.shape[0], WIDE), F32)
+            functools.partial(qkv_out_kernel, cut_vec),
+            places,
+            early_parts + late_parts,
+            jax.ShapeDtypeStruct((3, w_qkv.shape[0], WIDE), F32),
         )
         qkv_own = jnp.swapaxes(qkv_own, 0, 1)
     vec_own = first_quarter(early_parts, cut_out, vec_pad)
     vecs = [vec_own[i * share : (i + 1) * share] for i in range(6)]
     bias_in_own = vec_own[6 * share : 10 * share]
-    bias_own = first_quarter(late_parts, PAIRS * depth, vec_pad)[: 2 * share].reshape(2, share)
+    bias_own = first_quarter(late_parts, depth, vec_pad)[: 2 * share].reshape(2, share)
     return (
         result,
         grad_input,

time: 416 us -> 407 us (0.978)
  the two profiles are of different devices: /device:TPU:0 before, /device:TPU:18 now
where the time goes in v5:
time: 407 us; the launch traced here: 400 us
  waiting for transfers between devices  116 us (29%)
  Pallas kernels  107 us (26%)
  starting transfers between devices  61.2 us (15%)
  matrix products  50.3 us (12%)
  local copies, waits for them, and re-layouts  36.1 us (9%)
  other arithmetic  27.9 us (7%)
    ppermute x42, waiting for transfers between devices, xor_swap(): return lax.ppermute(value, axis, [(i, i ^ mask) for i in range(count)])  98.9 us
    pallas_call x6, Pallas kernels, backward_call(): pl.pallas_call(kernel, out_shape=outs, grid_spec=pltpu.PrefetchScalarGrid...  51.9 us
    ppermute x42, starting transfers between devices, xor_swap(): return lax.ppermute(value, axis, [(i, i ^ mask) for i in range(count)])  50.7 us
    pallas_call x3, Pallas kernels, attend_forward(): pl.pallas_call(functools.partial(forward_kernel, blocks), out_shape=(jax....  32 us
    dot_general x9, matrix products, left_inner(): lax.dot_general(left_mat, right_mat, (((0,), (0,)), ((), ())), preferred_...  19.8 us
    dot_general x7, matrix products, right_inner(): lax.dot_general(left_mat, right_mat, (((1,), (1,)), ((), ())), preferred_...  19.4 us
    pallas_call x5, Pallas kernels, local_call(): pl.pallas_call(kernel, out_shape=outs, in_specs=[pl.BlockSpec(memory_spac...  15.2 us
    unnamed x137, local copies, waits for them, and re-layouts  12.1 us
  transfers between devices with their start and end apart: 63, of which 24 were waited for; matrix products, arithmetic and copies ran while one was open for 21% of the time, Pallas kernels for 26%

profile of v5, /device:TPU:18, one launch (start us, length us, event | category | flops | bytes accessed | tf_op | source)
XLA Modules:
  0.0 400.4 jit_solution(14666444294014477988)
XLA Ops:
  6.3 4.8 %concatenate.179 = bf16[960]{0:T(1024)(128)(2,1)S(1)} concatenate(bf16[96]{0:T(256)(128)(2,1)} %param.20, bf16[96]{0:T(256)(128)(2,1)} %param.21, bf16[96]{0:T(256)(128)(2,1)} %param.22, bf16[96]{0:T(256)(128)(2,1)} %param.26, bf16[96]{0:T(256)(128)(2,1)} %param.27, bf16[96]{0:T(256)(128)(2,1)} %param.28, bf16[384]{0:T(512)(128)(2,1)} %param.24), dimensions={0} | concatenate | bytes 3840 | tf_op jit(solution)/shard_map/concatenate | solution.py:671
  14.5 3.8 collective-permute-start.11
  24.0 15.7 %collective-permute-done.12 = bf16[448,384]{1,0:T(8,128)(2,1)S(1)} collective-permute-done((bf16[448,384]{1,0:T(8,128)(2,1)S(1)}, bf16[448,384]{1,0:T(8,128)(2,1)S(1)}, u32[]{:S(2)}, u32[]{:S(2)}) %collective-permute-start.12) | collective-permute-done | bytes 344096 | tf_op jit(solution)/shard_map/ppermute | solution.py:70
  49.2 5.0 %collective-permute-done.4.refs_1_ = bf16[3,144,384]{2,1,0:T(8,128)(2,1)} collective-permute-done((bf16[3,144,384]{2,1,0:T(8,128)(2,1)S(1)}, bf16[3,144,384]{2,1,0:T(8,128)(2,1)}, u32[]{:S(2)}, u32[]{:S(2)}) %collective-permute-start.4) | collective-permute-done | bytes 331808 | tf_op jit(solution)/shard_map/ppermute | solution.py:70
  69.1 11.1 %collective-permute-done.7.ko_ref.vo_ref = bf16[1024,256]{1,0:T(8,128)(2,1)S(1)} collective-permute-done((bf16[1024,256]{1,0:T(8,128)(2,1)}, bf16[1024,256]{1,0:T(8,128)(2,1)S(1)}, u32[]{:S(2)}, u32[]{:S(2)}) %collective-permute-start.7) | collective-permute-done | bytes 524320 | tf_op jit(solution)/shard_map/ppermute | solution.py:730
  82.2 10.8 %attend_forward.3 = (bf16[1024,128]{1,0:T(8,128)(2,1)}, f32[8,2048]{1,0:T(8,128)}) custom-call(s32[5]{0:T(128)} %pad_add_fusion.1.table, bf16[1024,1152]{1,0:T(8,128)(2,1)} %copy-done.2, bf16[1024,1152]{1,0:T(8,128)(2,1)} %copy-done.2, bf16[1024,1152]{1,0:T(8,128)(2,1)} %copy-done.2, bf16[1024,256]{1,0:T(8,128)(2,1)} %copy-done.16, ...), custom_call_target="tpu_custom_call" | custom-call | flops 2147483648 | bytes 1048576 | tf_op jit(solution)/shard_map/attend_forward/pallas_call | solution.py:476
  94.6 10.6 %attend_forward.4 = (bf16[1024,128]{1,0:T(8,128)(2,1)}, f32[8,2048]{1,0:T(8,128)}) custom-call(s32[5]{0:T(128)} %pad_add_fusion.1.table, bf16[1024,1152]{1,0:T(8,128)(2,1)} %copy-done.2, bf16[1024,1152]{1,0:T(8,128)(2,1)} %copy-done.2, bf16[1024,1152]{1,0:T(8,128)(2,1)} %copy-done.2, bf16[1024,256]{1,0:T(8,128)(2,1)} %collective-permute-done.8.ko_ref.vo_ref, ...), custom_call_target="tpu_custom_call" | custom-call | flops 2147483648 | bytes 1048576 | tf_op jit(solution)/shard_map/attend_forward/pallas_call | solution.py:476
  106.9 10.6 %attend_forward.5 = (bf16[1024,128]{1,0:T(8,128)(2,1)}, f32[8,2048]{1,0:T(8,128)}) custom-call(s32[5]{0:T(128)} %pad_add_fusion.1.table, bf16[1024,1152]{1,0:T(8,128)(2,1)} %copy-done.2, bf16[1024,1152]{1,0:T(8,128)(2,1)} %copy-done.2, bf16[1024,1152]{1,0:T(8,128)(2,1)} %copy-done.2, bf16[1024,256]{1,0:T(8,128)(2,1)} %collective-permute-done.9.ko_ref.vo_ref, ...), custom_call_target="tpu_custom_call" | custom-call | flops 2147483648 | bytes 1048576 | tf_op jit(solution)/shard_map/attend_forward/pallas_call | solution.py:476
  117.6 5.4 %shard_map.255 = (bf16[1536,768]{1,0:T(8,128)(2,1)}, bf16[768,1536]{1,0:T(8,128)(2,1)}, bf16[384,768]{1,0:T(8,128)(2,1)}) custom-call(s32[2]{0:T(128)} %pad_add_fusion.2.places, bf16[384,768]{1,0:T(8,128)(2,1)} %own_down.1, bf16[192,1536]{1,0:T(8,128)(2,1)} %own_in.1, bf16[96,768]{1,0:T(8,128)(2,1)} %own_out.1, bf16[3,432,384]{2,1,0:T(8,128)(2,1)} %copy-done.9, ...), custom_call_target="tpu_custom_call" | custom-call | bytes 4194304 | tf_op jit(solution)/shard_map/pallas_call | solution.py:147
  154.5 4.6 %multiply_reduce_fusion = (f32[768]{0:T(1024)S(1)}, f32[512]{0:T(512)S(1)}, f32[512]{0:T(512)S(1)}, f32[768]{0:T(1024)S(1)}, f32[512,768]{1,0:T(8,128)S(1)}) fusion(f32[512,768]{1,0:T(8,128)S(1)} %get-tuple-element.189, f32[512]{0:T(512)S(1)} %add_rsqrt_fusion.1, f32[512]{0:T(512)S(1)} %broadcast_multiply_fusion.5, f32[768]{0:T(1024)S(1)} %maximum_select_fusion.6, ...), kind=kOutput, calls=%fused_computation.72 | convolution fusion | flops 1212282368 | bytes 10241024 | tf_op jit(solution)/shard_map/dot_general | solution.py:37
  190.6 7.6 %shard_map.258 = (f32[1024,128]{1,0:T(8,128)}, bf16[1024,256]{1,0:T(8,128)(2,1)}) custom-call(s32[5]{0:T(128)} %pad_add_fusion.1.table, bf16[1024,1152]{1,0:T(8,128)(2,1)} %copy-done.2, bf16[1024,256]{1,0:T(8,128)(2,1)} %collective-permute-done.9.ko_ref.vo_ref, bf16[1024,256]{1,0:T(8,128)(2,1)} %collective-permute-done.9.ko_ref.vo_ref, ...), custom_call_target="tpu_custom_call" | custom-call | flops 2684354560 | bytes 2097152 | tf_op jit(solution)/shard_map/pallas_call | solution.py:500
  198.2 7.2 %shard_map.257 = (f32[1024,128]{1,0:T(8,128)}, bf16[1024,256]{1,0:T(8,128)(2,1)}) custom-call(s32[5]{0:T(128)} %pad_add_fusion.1.table, bf16[1024,1152]{1,0:T(8,128)(2,1)} %copy-done.2, bf16[1024,256]{1,0:T(8,128)(2,1)} %collective-permute-done.8.ko_ref.vo_ref, bf16[1024,256]{1,0:T(8,128)(2,1)} %collective-permute-done.8.ko_ref.vo_ref, ...), custom_call_target="tpu_custom_call" | custom-call | flops 2684354560 | bytes 2097152 | tf_op jit(solution)/shard_map/pallas_call | solution.py:500
  205.4 7.3 %shard_map.256 = (f32[1024,128]{1,0:T(8,128)}, bf16[1024,256]{1,0:T(8,128)(2,1)}) custom-call(s32[5]{0:T(128)} %pad_add_fusion.1.table, bf16[1024,1152]{1,0:T(8,128)(2,1)} %copy-done.2, bf16[1024,256]{1,0:T(8,128)(2,1)} %copy-done.16, bf16[1024,256]{1,0:T(8,128)(2,1)} %copy-done.16, s32[8,1024]{1,0:T(8,128)} %pad.21.span_ref, ...), custom_call_target="tpu_custom_call" | custom-call | flops 2684354560 | bytes 2097152 | tf_op jit(solution)/shard_map/pallas_call | solution.py:500
  212.7 9.9 %shard_map.259 = (bf16[1024,128]{1,0:T(8,128)(2,1)}, f32[1024,128]{1,0:T(8,128)}, f32[1024,128]{1,0:T(8,128)}) custom-call(s32[5]{0:T(128)} %pad_add_fusion.1.table, bf16[1024,1152]{1,0:T(8,128)(2,1)} %copy-done.2, bf16[1024,1152]{1,0:T(8,128)(2,1)} %copy-done.2, bf16[1024,1152]{1,0:T(8,128)(2,1)} %copy-done.2, s32[8,1024]{1,0:T(8,128)} %pad.21.span_ref, ...), custom_call_target="tpu_custom_call" | custom-call | flops 2684354560 | bytes 2097152 | tf_op jit(solution)/shard_map/pallas_call | solution.py:500
  224.7 10.0 %shard_map.260 = (bf16[1024,128]{1,0:T(8,128)(2,1)}, f32[1024,128]{1,0:T(8,128)}, f32[1024,128]{1,0:T(8,128)}) custom-call(s32[5]{0:T(128)} %pad_add_fusion.1.table, bf16[1024,1152]{1,0:T(8,128)(2,1)} %copy-done.2, bf16[1024,1152]{1,0:T(8,128)(2,1)} %copy-done.2, bf16[1024,1152]{1,0:T(8,128)(2,1)} %copy-done.2, s32[8,1024]{1,0:T(8,128)} %pad.21.span_ref, ...), custom_call_target="tpu_custom_call" | custom-call | flops 2684354560 | bytes 2097152 | tf_op jit(solution)/shard_map/pallas_call | solution.py:500
  234.7 9.9 %shard_map.261 = (bf16[1024,128]{1,0:T(8,128)(2,1)}, f32[1024,128]{1,0:T(8,128)}, f32[1024,128]{1,0:T(8,128)}) custom-call(s32[5]{0:T(128)} %pad_add_fusion.1.table, bf16[1024,1152]{1,0:T(8,128)(2,1)} %copy-done.2, bf16[1024,1152]{1,0:T(8,128)(2,1)} %copy-done.2, bf16[1024,1152]{1,0:T(8,128)(2,1)} %copy-done.2, s32[8,1024]{1,0:T(8,128)} %pad.21.span_ref, ...), custom_call_target="tpu_custom_call" | custom-call | flops 2684354560 | bytes 2097152 | tf_op jit(solution)/shard_map/pallas_call | solution.py:500
  255.4 4.4 %collective-permute-done.30.refs_0_ = bf16[1024,256]{1,0:T(8,128)(2,1)} collective-permute-done((bf16[1024,256]{1,0:T(8,128)(2,1)}, bf16[1024,256]{1,0:T(8,128)(2,1)}, u32[]{:S(2)}, u32[]{:S(2)}) %collective-permute-start.30) | collective-permute-done | bytes 524320 | tf_op jit(solution)/shard_map/ppermute | solution.py:923
  278.2 22.9 %collective-permute-done.44 = bf16[4,64,384]{2,1,0:T(8,128)(2,1)S(1)} collective-permute-done((bf16[4,64,384]{2,1,0:T(8,128)(2,1)S(1)}, bf16[4,64,384]{2,1,0:T(8,128)(2,1)S(1)}, u32[]{:S(2)}, u32[]{:S(2)}) %collective-permute-start.44) | collective-permute-done | bytes 196640 | tf_op jit(solution)/shard_map/ppermute | solution.py:70
  327.8 3.9 collective-permute-done.35
  333.7 7.2 %collective-permute-done.36 = bf16[4,96,384]{2,1,0:T(8,128)(2,1)S(1)} collective-permute-done((bf16[4,96,384]{2,1,0:T(8,128)(2,1)S(1)}, bf16[4,96,384]{2,1,0:T(8,128)(2,1)S(1)}, u32[]{:S(2)}, u32[]{:S(2)}) %collective-permute-start.36) | collective-permute-done | bytes 294944 | tf_op jit(solution)/shard_map/ppermute | solution.py:70
  348.7 3.8 collective-permute-done.51.refs_6_
  369.5 6.2 %collective-permute-done.39 = bf16[352,384]{1,0:T(8,128)(2,1)S(1)} collective-permute-done((bf16[352,384]{1,0:T(8,128)(2,1)}, bf16[352,384]{1,0:T(8,128)(2,1)S(1)}, u32[]{:S(2)}, u32[]{:S(2)}) %collective-permute-start.39) | collective-permute-done | bytes 270368 | tf_op jit(solution)/shard_map/ppermute | solution.py:70
  375.8 5.5 %collective-permute-done.40 = bf16[352,384]{1,0:T(8,128)(2,1)S(1)} collective-permute-done((bf16[352,384]{1,0:T(8,128)(2,1)S(1)}, bf16[352,384]{1,0:T(8,128)(2,1)S(1)}, u32[]{:S(2)}, u32[]{:S(2)}) %collective-permute-start.40) | collective-permute-done | bytes 270368 | tf_op jit(solution)/shard_map/ppermute | solution.py:70
  385.0 3.7 fusion.24
  (452 shorter events, 206.5 us)
Async XLA Ops:
  13.9 25.7 %collective-permute-start.12 = (bf16[448,384]{1,0:T(8,128)(2,1)S(1)}, bf16[448,384]{1,0:T(8,128)(2,1)S(1)}, u32[]{:S(2)}, u32[]{:S(2)}) collective-permute-start(bf16[448,384]{1,0:T(8,128)(2,1)S(1)} %pad_maximum_fusion.1), channel_id=1, source_target_pairs={{0,3},{1,2},{2,1},{3,0},{4,7},{5,6},{6,5},{7,4},{8,11},{9,10},{10,... | collective-permute-start | bytes 1032200 | tf_op jit(solution)/shard_map/ppermute | solution.py:70
  14.5 28.9 %collective-permute-start.11 = (bf16[448,384]{1,0:T(8,128)(2,1)S(1)}, bf16[448,384]{1,0:T(8,128)(2,1)S(1)}, u32[]{:S(2)}, u32[]{:S(2)}) collective-permute-start(bf16[448,384]{1,0:T(8,128)(2,1)S(1)} %pad_maximum_fusion.1), channel_id=1, source_target_pairs={{0,2},{1,3},{2,0},{3,1},{4,6},{5,7},{6,4},{7,5},{8,10},{9,11},{10,... | collective-permute-start | bytes 1032200 | tf_op jit(solution)/shard_map/ppermute | solution.py:70
  21.9 35.3 %collective-permute-start = (bf16[1024,384]{1,0:T(8,128)(2,1)}, bf16[1024,384]{1,0:T(8,128)(2,1)}, u32[]{:S(2)}, u32[]{:S(2)}) collective-permute-start(bf16[1024,384]{1,0:T(8,128)(2,1)} %param.15), channel_id=1, source_target_pairs={{0,4},{4,0},{1,5},{5,1},{2,6},{6,2},{3,7},{7,3},{8,12},{12,8},{9,1... | collective-permute-start | bytes 2359304 | tf_op jit(solution)/shard_map/ppermute | solution.py:43
  22.4 25.7 %collective-permute-start.6 = (bf16[3,144,384]{2,1,0:T(8,128)(2,1)S(1)}, bf16[3,144,384]{2,1,0:T(8,128)(2,1)S(1)}, u32[]{:S(2)}, u32[]{:S(2)}) collective-permute-start(bf16[3,144,384]{2,1,0:T(8,128)(2,1)S(1)} %pad_maximum_fusion.2.refs_0_), channel_id=1, source_target_pairs={{0,24},{8,16},{16,8},{24,0},{1,25},{9,17},{17,9},{25,1},{2,26},{10... | collective-permute-start | bytes 995336 | tf_op jit(solution)/shard_map/ppermute | solution.py:70
  45.6 71.9 %collective-permute-start.15 = (bf16[3,432,384]{2,1,0:T(8,128)(2,1)S(1)}, bf16[3,432,384]{2,1,0:T(8,128)(2,1)}, u32[]{:S(2)}, u32[]{:S(2)}) collective-permute-start(bf16[3,432,384]{2,1,0:T(8,128)(2,1)S(1)} %pad_maximum_fusion.refs_0_), channel_id=1, source_target_pairs={{0,24},{8,16},{16,8},{24,0},{1,25},{9,17},{17,9},{25,1},{2,26},{10... | collective-permute-start | bytes 2985992 | tf_op jit(solution)/shard_map/ppermute | solution.py:70
  48.1 69.4 %collective-permute-start.14 = (bf16[3,432,384]{2,1,0:T(8,128)(2,1)S(1)}, bf16[3,432,384]{2,1,0:T(8,128)(2,1)}, u32[]{:S(2)}, u32[]{:S(2)}) collective-permute-start(bf16[3,432,384]{2,1,0:T(8,128)(2,1)S(1)} %pad_maximum_fusion.refs_0_), channel_id=1, source_target_pairs={{0,16},{8,24},{16,0},{24,8},{1,17},{9,25},{17,1},{25,9},{2,18},{10... | collective-permute-start | bytes 2985992 | tf_op jit(solution)/shard_map/ppermute | solution.py:70
  48.7 68.9 %collective-permute-start.13 = (bf16[3,432,384]{2,1,0:T(8,128)(2,1)S(1)}, bf16[3,432,384]{2,1,0:T(8,128)(2,1)}, u32[]{:S(2)}, u32[]{:S(2)}) collective-permute-start(bf16[3,432,384]{2,1,0:T(8,128)(2,1)S(1)} %pad_maximum_fusion.refs_0_), channel_id=1, source_target_pairs={{0,8},{8,0},{16,24},{24,16},{1,9},{9,1},{17,25},{25,17},{2,10},{10... | collective-permute-start | bytes 2985992 | tf_op jit(solution)/shard_map/ppermute | solution.py:70
  67.4 27.2 %collective-permute-start.8 = (bf16[1024,256]{1,0:T(8,128)(2,1)}, bf16[1024,256]{1,0:T(8,128)(2,1)}, u32[]{:S(2)}, u32[]{:S(2)}) collective-permute-start(bf16[1024,256]{1,0:T(8,128)(2,1)} %get-tuple-element.119), channel_id=1, source_target_pairs={{1,0},{0,1},{3,2},{2,3},{5,4},{4,5},{7,6},{6,7},{9,8},{8,9},{11,10... | collective-permute-start | bytes 1572872 | tf_op jit(solution)/shard_map/ppermute | solution.py:730
  80.2 26.7 %collective-permute-start.9 = (bf16[1024,256]{1,0:T(8,128)(2,1)}, bf16[1024,256]{1,0:T(8,128)(2,1)}, u32[]{:S(2)}, u32[]{:S(2)}) collective-permute-start(bf16[1024,256]{1,0:T(8,128)(2,1)} %get-tuple-element.118), channel_id=1, source_target_pairs={{1,0},{0,1},{3,2},{2,3},{5,4},{4,5},{7,6},{6,7},{9,8},{8,9},{11,10... | collective-permute-start | bytes 1572872 | tf_op jit(solution)/shard_map/ppermute | solution.py:730
  94.6 44.4 %collective-permute-start.22 = (bf16[512,384]{1,0:T(8,128)(2,1)}, bf16[512,384]{1,0:T(8,128)(2,1)S(1)}, u32[]{:S(2)}, u32[]{:S(2)}) collective-permute-start(bf16[512,384]{1,0:T(8,128)(2,1)} %get-tuple-element.134), channel_id=1, source_target_pairs={{0,4},{4,0},{1,5},{5,1},{2,6},{6,2},{3,7},{7,3},{8,12},{12,8},{9,1... | collective-permute-start | bytes 1179656 | tf_op jit(solution)/shard_map/ppermute | solution.py:43
  186.0 86.9 %collective-permute-start.54 = (bf16[4,192,384]{2,1,0:T(8,128)(2,1)}, bf16[4,192,384]{2,1,0:T(8,128)(2,1)}, u32[]{:S(2)}, u32[]{:S(2)}) collective-permute-start(bf16[4,192,384]{2,1,0:T(8,128)(2,1)} %get-tuple-element.113), channel_id=1, source_target_pairs={{0,8},{8,0},{16,24},{24,16},{1,9},{9,1},{17,25},{25,17},{2,10},{10... | collective-permute-start | bytes 1769480 | tf_op jit(solution)/shard_map/ppermute | solution.py:70
  186.0 87.1 %collective-permute-start.55 = (bf16[4,192,384]{2,1,0:T(8,128)(2,1)}, bf16[4,192,384]{2,1,0:T(8,128)(2,1)}, u32[]{:S(2)}, u32[]{:S(2)}) collective-permute-start(bf16[4,192,384]{2,1,0:T(8,128)(2,1)} %get-tuple-element.114), channel_id=1, source_target_pairs={{0,16},{8,24},{16,0},{24,8},{1,17},{9,25},{17,1},{25,9},{2,18},{10... | collective-permute-start | bytes 1769480 | tf_op jit(solution)/shard_map/ppermute | solution.py:70
  222.6 23.4 %collective-permute-start.28 = (bf16[1024,256]{1,0:T(8,128)(2,1)}, bf16[1024,256]{1,0:T(8,128)(2,1)}, u32[]{:S(2)}, u32[]{:S(2)}) collective-permute-start(bf16[1024,256]{1,0:T(8,128)(2,1)} %get-tuple-element.70), channel_id=1, source_target_pairs={{0,1},{1,0},{2,3},{3,2},{4,5},{5,4},{6,7},{7,6},{8,9},{9,8},{10,11... | collective-permute-start | bytes 1572872 | tf_op jit(solution)/shard_map/ppermute | solution.py:923
  222.6 28.1 %collective-permute-start.29 = (bf16[1024,256]{1,0:T(8,128)(2,1)}, bf16[1024,256]{1,0:T(8,128)(2,1)}, u32[]{:S(2)}, u32[]{:S(2)}) collective-permute-start(bf16[1024,256]{1,0:T(8,128)(2,1)} %get-tuple-element.77), channel_id=1, source_target_pairs={{0,1},{1,0},{2,3},{3,2},{4,5},{5,4},{6,7},{7,6},{8,9},{9,8},{10,11... | collective-permute-start | bytes 1572872 | tf_op jit(solution)/shard_map/ppermute | solution.py:923
  234.7 25.1 %collective-permute-start.30 = (bf16[1024,256]{1,0:T(8,128)(2,1)}, bf16[1024,256]{1,0:T(8,128)(2,1)}, u32[]{:S(2)}, u32[]{:S(2)}) collective-permute-start(bf16[1024,256]{1,0:T(8,128)(2,1)} %get-tuple-element.84), channel_id=1, source_target_pairs={{0,1},{1,0},{2,3},{3,2},{4,5},{5,4},{6,7},{7,6},{8,9},{9,8},{10,11... | collective-permute-start | bytes 1572872 | tf_op jit(solution)/shard_map/ppermute | solution.py:923
  246.0 29.8 %collective-permute-start.56 = (bf16[4,192,384]{2,1,0:T(8,128)(2,1)}, bf16[4,192,384]{2,1,0:T(8,128)(2,1)}, u32[]{:S(2)}, u32[]{:S(2)}) collective-permute-start(bf16[4,192,384]{2,1,0:T(8,128)(2,1)} %get-tuple-element.115), channel_id=1, source_target_pairs={{0,24},{8,16},{16,8},{24,0},{1,25},{9,17},{17,9},{25,1},{2,26},{10... | collective-permute-start | bytes 1769480 | tf_op jit(solution)/shard_map/ppermute | solution.py:70
  250.7 70.4 %collective-permute-start.32 = (bf16[4,256,384]{2,1,0:T(8,128)(2,1)}, bf16[4,256,384]{2,1,0:T(8,128)(2,1)}, u32[]{:S(2)}, u32[]{:S(2)}) collective-permute-start(bf16[4,256,384]{2,1,0:T(8,128)(2,1)} %get-tuple-element.110), channel_id=1, source_target_pairs={{0,8},{8,0},{16,24},{24,16},{1,9},{9,1},{17,25},{25,17},{2,10},{10... | collective-permute-start | bytes 2359304 | tf_op jit(solution)/shard_map/ppermute | solution.py:70
  259.7 64.1 %collective-permute-start.34 = (bf16[4,256,384]{2,1,0:T(8,128)(2,1)}, bf16[4,256,384]{2,1,0:T(8,128)(2,1)}, u32[]{:S(2)}, u32[]{:S(2)}) collective-permute-start(bf16[4,256,384]{2,1,0:T(8,128)(2,1)} %get-tuple-element.111), channel_id=1, source_target_pairs={{0,24},{8,16},{16,8},{24,0},{1,25},{9,17},{17,9},{25,1},{2,26},{10... | collective-permute-start | bytes 2359304 | tf_op jit(solution)/shard_map/ppermute | solution.py:70
  272.8 28.3 %collective-permute-start.44 = (bf16[4,64,384]{2,1,0:T(8,128)(2,1)S(1)}, bf16[4,64,384]{2,1,0:T(8,128)(2,1)S(1)}, u32[]{:S(2)}, u32[]{:S(2)}) collective-permute-start(bf16[4,64,384]{2,1,0:T(8,128)(2,1)S(1)} %get-tuple-element.130), channel_id=1, source_target_pairs={{0,8},{8,0},{16,24},{24,16},{1,9},{9,1},{17,25},{25,17},{2,10},{10... | collective-permute-start | bytes 589832 | tf_op jit(solution)/shard_map/ppermute | solution.py:70
  273.1 28.1 %collective-permute-start.45 = (bf16[4,64,384]{2,1,0:T(8,128)(2,1)S(1)}, bf16[4,64,384]{2,1,0:T(8,128)(2,1)S(1)}, u32[]{:S(2)}, u32[]{:S(2)}) collective-permute-start(bf16[4,64,384]{2,1,0:T(8,128)(2,1)S(1)} %get-tuple-element.131), channel_id=1, source_target_pairs={{0,16},{8,24},{16,0},{24,8},{1,17},{9,25},{17,1},{25,9},{2,18},{10... | collective-permute-start | bytes 589832 | tf_op jit(solution)/shard_map/ppermute | solution.py:70
  275.9 28.6 %collective-permute-start.46 = (bf16[4,64,384]{2,1,0:T(8,128)(2,1)S(1)}, bf16[4,64,384]{2,1,0:T(8,128)(2,1)S(1)}, u32[]{:S(2)}, u32[]{:S(2)}) collective-permute-start(bf16[4,64,384]{2,1,0:T(8,128)(2,1)S(1)} %get-tuple-element.132), channel_id=1, source_target_pairs={{0,24},{8,16},{16,8},{24,0},{1,25},{9,17},{17,9},{25,1},{2,26},{10... | collective-permute-start | bytes 589832 | tf_op jit(solution)/shard_map/ppermute | solution.py:70
  318.6 66.4 %collective-permute-start.23 = (f32[512,384]{1,0:T(8,128)}, f32[512,384]{1,0:T(8,128)}, u32[]{:S(2)}, u32[]{:S(2)}) collective-permute-start(f32[512,384]{1,0:T(8,128)} %get-tuple-element.123), channel_id=1, source_target_pairs={{0,4},{4,0},{1,5},{5,1},{2,6},{6,2},{3,7},{7,3},{8,12},{12,8},{9,1... | collective-permute-start | bytes 2359304 | tf_op jit(solution)/shard_map/ppermute | solution.py:43
  321.1 64.0 %collective-permute-start.31 = (bf16[1024,384]{1,0:T(8,128)(2,1)}, bf16[1024,384]{1,0:T(8,128)(2,1)}, u32[]{:S(2)}, u32[]{:S(2)}) collective-permute-start(bf16[1024,384]{1,0:T(8,128)(2,1)} %dynamic-slice_convert_fusion), channel_id=1, source_target_pairs={{0,4},{4,0},{1,5},{5,1},{2,6},{6,2},{3,7},{7,3},{8,12},{12,8},{9,1... | collective-permute-start | bytes 2359304 | tf_op jit(solution)/shard_map/ppermute | solution.py:43
  331.7 27.1 %collective-permute-start.62 = (bf16[192,384]{1,0:T(8,128)(2,1)S(1)}, bf16[192,384]{1,0:T(8,128)(2,1)S(1)}, u32[]{:S(2)}, u32[]{:S(2)}) collective-permute-start(bf16[192,384]{1,0:T(8,128)(2,1)S(1)} %fusion.62.refs_0_), channel_id=1, source_target_pairs={{0,24},{8,16},{16,8},{24,0},{1,25},{9,17},{17,9},{25,1},{2,26},{10... | collective-permute-start | bytes 442376 | tf_op jit(solution)/shard_map/ppermute | solution.py:70
  (103 other events, 1022.1 us)
